TPU v7x, 128 devices: a whole 4x4x4 slice. The times are simulated.
128 devices in a mesh: col: 8 (over y, core), row: 16 (over z, x).
Axes of the slice: x: 4, y: 4, z: 4, core: 2. Of those that a mesh axis runs over, the one named last changes fastest.
Arguments:
- tokens: bfloat16 [4096, 2880], P('row'), may hold values from -6 to 6
- moe_gain: bfloat16 [2880], replicated, may hold values from 0.5 to 1.5
- route_ids: int32 [4096, 4], P('row'), may hold values from 0 to 63, all different within a row; in each aligned block of 256 rows (0 to 255, 256 to 511, ...) at most 24 rows name the same one
- route_weight: float32 [4096, 4], P('row'), may hold values from 0.1 to 1
- w_gate: bfloat16 [64, 2880, 2880], P('row', None, 'col'), may hold values from -0.109375 to 0.109375
- w_up: bfloat16 [64, 2880, 2880], P('row', None, 'col'), may hold values from -0.109375 to 0.109375
- w_down: bfloat16 [64, 2880, 2880], P('row', 'col'), may hold values from -0.109375 to 0.109375
- next_gain: bfloat16 [2880], replicated, may hold values from 0.5 to 1.5
- next_gate: bfloat16 [2880, 128], P(None, 'col'), may hold values from -2 to 2
- next_ids: int32 [4096, 4], P('row'), may hold values from 0 to 127, all different within a row
Outputs:
- mixed: bfloat16 [4096, 2880], P('row', 'col')
- next_logprob: float32 [4096, 4], P('row')
Inputs may be any that keep to these rules, and one draw needn't show every extreme that they name: `route_ids`: among the 256 tokens of one index of row, no expert is picked more than 24 times, a bound that some block reaches; a token's picks differ. `next_ids`: A token's picks differ.
All inputs are finite; a program needn't handle non-finite values.
Results may differ from a plain program's by a relative error of at most 0.0095.
Values may be sent and summed in bfloat16 or wider, within the bound.
No kernel may reach another device: no remote copies, remote signals or barrier semaphores. Data moves between devices by JAX's collectives and lax.ppermute only.
A program may use at most 128 MiB of HBM per device.

v0:
```python
import jax
import jax.numpy as jnp
from jax import lax
from jax.sharding import Mesh
from jax.sharding import PartitionSpec as P

TOP = 4
CAP = 24
COL = ("col_0", "col_1")


def copy_for_each(array, axis):
    size = lax.axis_size(axis)
    return lax.all_to_all(
        jnp.broadcast_to(array[None], (size, *array.shape)), axis, 0, 0, tiled=True
    )


def gathered_once(array, axis):
    leaves = jax.tree.leaves(array)
    sequence = sorted(range(len(leaves)), key=lambda k: -leaves[k].size)
    width = (1, *leaves[sequence[0]].shape)[-1]
    lines = [
        jnp.pad(leaves[k].reshape(-1), (0, -leaves[k].size % width)).reshape(-1, width)
        for k in sequence
    ]
    both, at, found = (copy_for_each(jnp.concatenate(lines), axis), 0, {})
    for k, line in zip(sequence, lines):
        piece = both[:, at : at + len(line)].reshape(len(both), -1)
        found[k] = piece[:, : leaves[k].size].reshape(-1, *leaves[k].shape)
        at += len(line)
    numbers = iter(range(len(leaves)))
    return jax.tree.map(lambda _: found[next(numbers)], array)


def combined_pairwise(pieces, combine):
    while len(jax.tree.leaves(pieces)[0]) > 1:
        pieces = jax.vmap(combine)(
            *(jax.tree.map(lambda part: part[side::2], pieces) for side in (0, 1))
        )
    return jax.tree.map(lambda part: part[0], pieces)


def combined_all(array, axis, combine):
    pieces = gathered_once(array, axis)
    return combined_pairwise(pieces, combine)


def reduced_to_own(pieces, axes, sequence):
    inside = pieces.shape[1:]
    pieces = pieces.reshape(*(lax.axis_size(a) for a in axes), *inside)
    pieces = jnp.moveaxis(pieces, sequence, range(len(axes))).reshape(-1, *inside)
    for k in sequence:
        pieces = lax.psum_scatter(pieces, axes[k], scatter_dimension=0, tiled=True)
    return pieces[0]


def in_blocks(array, dim, size):
    before, after = (array.shape[:dim], array.shape[dim + 1 :])
    return jnp.moveaxis(array.reshape(*before, size, -1, *after), dim, 0)


def sum_by_axis(array, axes, sequence, dim):
    size = lax.axis_size(axes)
    return reduced_to_own(in_blocks(array, dim, size), axes, sequence)


def merge_softmax(first, second):
    highest = jnp.maximum(first[0], second[0])
    total = first[1] * jnp.exp(first[0] - highest) + second[1] * jnp.exp(second[0] - highest)
    return (highest, total, first[2] + second[2])


def local(
    tokens, moe_gain, route_ids, route_weight, w_gate, w_up, w_down, next_gain, next_gate, next_ids
):
    row_count = lax.axis_size("row")
    col_count = lax.axis_size(COL)
    tok_rows = tokens.shape[0]
    feature_count = tokens.shape[1]
    local_experts = w_gate.shape[0]
    expert_count = local_experts * row_count
    part_width = feature_count // col_count
    col_start = lax.axis_index(COL) * part_width
    floats = tokens.astype(jnp.float32)
    inverse = lax.rsqrt(jnp.mean(floats * floats, axis=-1, keepdims=True) + 1e-05)
    normed = (floats * inverse * moe_gain.astype(jnp.float32)).astype(jnp.bfloat16)
    gated_in = (floats * inverse * next_gain.astype(jnp.float32)).astype(jnp.bfloat16)
    flat_ids = route_ids.reshape(-1)
    onehot = (flat_ids[:, None] == jnp.arange(expert_count, dtype=jnp.int32)[None, :]).astype(
        jnp.int32
    )
    slots = jnp.sum(jnp.cumsum(onehot, axis=0) * onehot, axis=1) - 1
    target = flat_ids * CAP + slots
    token_of = jnp.arange(tok_rows * TOP, dtype=jnp.int32) // TOP
    buffer = jnp.zeros((expert_count * CAP, normed.shape[1]), jnp.bfloat16)
    buffer = buffer.at[target].set(normed[token_of])
    arrived = lax.all_to_all(
        buffer.reshape(row_count, local_experts, CAP, normed.shape[1]),
        "row",
        split_axis=0,
        concat_axis=0,
        tiled=True,
    )
    logits = jnp.dot(gated_in, next_gate, preferred_element_type=jnp.float32)
    cols_local = next_gate.shape[1]
    local_index = next_ids - lax.axis_index(COL) * cols_local
    owned = (
        local_index[:, :, None] == jnp.arange(cols_local, dtype=jnp.int32)[None, None, :]
    ).astype(jnp.float32)
    picked_logit = jnp.sum(owned * logits[:, None, :], axis=-1)
    local_max = jnp.max(logits, axis=-1)
    gate = jnp.einsum("sjcd,jdf->sjcf", arrived, w_gate, preferred_element_type=jnp.float32)
    upward = jnp.einsum("sjcd,jdf->sjcf", arrived, w_up, preferred_element_type=jnp.float32)
    hidden = (jax.nn.silu(gate) * upward).astype(jnp.bfloat16)
    partial_value = jnp.einsum(
        "sjcf,jfd->sjcd", hidden, w_down, preferred_element_type=jnp.float32
    ).astype(jnp.bfloat16)
    local_sum = jnp.sum(jnp.exp(logits - local_max[:, None]), axis=-1)
    highest, total, chosen = combined_all((local_max, local_sum, picked_logit), COL, merge_softmax)
    next_logprob = chosen - highest[:, None] - jnp.log(total)[:, None]
    summed = sum_by_axis(partial_value, COL, (1, 0), 3).astype(jnp.float32).astype(jnp.bfloat16)
    returned = lax.all_to_all(summed, "row", split_axis=0, concat_axis=0, tiled=True)
    flat_back = returned.reshape(expert_count * CAP, part_width)
    gathered = flat_back[target].astype(jnp.float32).reshape(tok_rows, TOP, part_width)
    combined = jnp.sum(gathered * route_weight[:, :, None], axis=1)
    residual = lax.dynamic_slice_in_dim(floats, col_start, part_width, 1)
    mixed = (residual + combined).astype(jnp.bfloat16)
    return (mixed, next_logprob)


def solution(mesh):
    torus = Mesh(mesh.devices.reshape(4, 2, mesh.shape["row"]), ("col_0", "col_1", "row"))
    return jax.shard_map(
        local,
        mesh=torus,
        in_specs=(
            P("row", None),
            P(),
            P("row", None),
            P("row", None),
            P("row", None, COL),
            P("row", None, COL),
            P("row", COL, None),
            P(),
            P(None, COL),
            P("row", None),
        ),
        out_specs=(P("row", COL), P("row", None)),
        check_vma=False,
    )
```

profile of v0, /device:TPU:0, one launch (start us, length us, event | category | flops | bytes accessed | tf_op | source)
XLA Modules:
  0.0 363.0 jit_solution(17383374542606089668)
XLA Ops:
  7.2 0.8 broadcast_multiply_fusion
  8.0 0.8 copy.69
  8.9 0.1 eq.42
  9.0 0.1 eq.38
  9.1 0.1 copy.68
  9.3 0.1 mul.105
  9.4 18.0 %reduce-window.6 = s32[64,8,128]{2,1,0:T(8,128)S(1)} reduce-window(s32[64,8,128]{2,1,0:T(8,128)S(1)} %fusion.31, s32[]{:T(128)} %constant.22.clone.1), window={size=1x1x128 pad=0_0x0_0x127_0}, to_apply=%region_0.0 | reduce-window | flops 8323072 | bytes 524292 | tf_op jit(solution)/shard_map/reduce-window
  27.4 0.1 slice.102
  27.6 0.1 copy.71
  27.8 0.1 broadcast_add_fusion
  28.1 1.0 copy.67
  29.1 0.4 multiply_reduce_fusion
  29.5 0.4 multiply_convert_fusion.1
  30.0 32.6 %scatter_custom_fusion = bf16[1536,2880]{1,0:T(8,128)(2,1)} fusion(s32[1024]{0:T(1024)S(1)} %bitcast.96, bf16[256,2880]{1,0:T(8,128)(2,1)S(1)} %multiply_convert_fusion.1, s32[1024]{0:T(1024)S(1)} %broadcast_clamp_fusion.1, bf16[]{:T(256)} %constant.53.clone.1), kind=kCustom, calls=%fused_computation.12 | custom fusion | bytes 8847362 | tf_op jit(solution)/shard_map/scatter | solution.py:97
  62.5 110.9 %all_to_all.15 = bf16[16,4,24,2880]{3,2,1,0:T(8,128)(2,1)} all-to-all(bf16[16,4,24,2880]{3,2,1,0:T(8,128)(2,1)} %bitcast.88), channel_id=1, replica_groups=mesh['col_0'=4,'col_1'=2,'row'=16] {'row'}, dimensions={0} | all-to-all | bytes 17694720 | tf_op jit(solution)/shard_map/all_to_all | solution.py:98
  173.4 11.9 %fusion.2 = f32[4,16,24,360]{3,2,1,0:T(8,128)} fusion(bf16[4,2880,360]{1,2,0:T(8,128)(2,1)} %param.15, bf16[16,4,24,2880]{3,2,1,0:T(8,128)(2,1)} %all_to_all.15), kind=kOutput, calls=%fused_computation.6 | convolution fusion | flops 3185049600 | bytes 19353600 | tf_op jit(solution)/shard_map/sjcd,jdf->sjcf/dot_general | solution.py:114
  185.3 17.0 %convert_bitcast_fusion = bf16[16,4,24,2880]{3,2,0,1:T(8,128)(2,1)} fusion(bf16[4,360,2880]{2,1,0:T(8,128)(2,1)} %param.16, f32[4,16,24,360]{3,2,1,0:T(8,128)} %fusion.2, bf16[4,2880,360]{1,2,0:T(8,128)(2,1)} %param.14, bf16[16,4,24,2880]{3,2,1,0:T(8,128)(2,1)} %all_to_all.15), kind=kOutput, calls=%fused_computation.3 | convolution fusion | flops 6377840640 | bytes 36495360 | tf_op jit(solution)/shard_map/sjcf,jfd->sjcd/dot_general | solution.py:116
  202.3 19.5 %reshape.155 = bf16[16,4,24,8,360]{4,3,2,0,1:T(8,128)(2,1)} reshape(bf16[16,4,24,2880]{3,2,0,1:T(8,128)(2,1)} %convert_bitcast_fusion) | data formatting | bytes 17694720 | tf_op jit(solution)/shard_map/reshape | solution.py:60
  221.7 19.2 %reshape.156 = bf16[4,2,16,4,24,360]{5,1,0,4,2,3:T(2,128)(2,1)} reshape(bf16[8,16,4,24,360]{4,0,3,1,2:T(8,128)(2,1)} %bitcast.86) | data formatting | bytes 17694720 | tf_op jit(solution)/shard_map/reshape | solution.py:51
  240.9 8.7 %copy.75 = bf16[2,4,16,4,24,360]{5,4,3,2,1,0:T(8,128)(2,1)} copy(bf16[2,4,16,4,24,360]{5,0,1,4,2,3:T(2,128)(2,1)} %bitcast.87) | data formatting | bytes 17694720 | tf_op jit(solution)/shard_map/transpose | solution.py:52
  249.7 17.9 %reduce-scatter.3.cloned.1.call-done = bf16[4,16,4,24,360]{4,3,2,1,0:T(8,128)(2,1)} async-done(((bf16[8,16,4,24,360]{4,3,2,1,0:T(8,128)(2,1)}), bf16[4,16,4,24,360]{4,3,2,1,0:T(8,128)(2,1)}) %reduce-scatter.3.cloned.1.call-update) | async-done | bytes 4423696 | tf_op jit(solution)/shard_map/reduce_scatter | solution.py:54
  267.7 0.6 fusion.40
  268.4 0.1 reshape.160
  268.8 0.6 broadcast_in_dim.5
  269.4 4.4 %all-to-all-start.2 = ((f32[8,384,4]{1,2,0:T(4,128)}), f32[8,384,4]{1,2,0:T(4,128)S(1)}, u32[]{:S(2)}, u32[]{:S(2)}) async-start(f32[8,384,4]{1,2,0:T(4,128)} %broadcast_in_dim.5), calls=%async_computation.4 | async-start | bytes 98304 | tf_op jit(solution)/shard_map/all_to_all | solution.py:14
  273.8 1.8 convert_element_type.42
  275.7 0.1 copy.76
  275.8 3.6 all-to-all-done.2
  279.4 0.1 copy.80
  279.6 0.3 slice.93
  279.9 0.3 slice.92
  280.2 0.1 copy.79
  280.3 0.3 slice.86
  280.7 0.3 slice.85
  281.1 0.3 slice.95
  281.3 0.2 slice.94
  281.6 0.3 slice.88
  281.9 0.2 slice.87
  282.1 40.4 %reduce-scatter.5.cloned.1.call-done = bf16[1,16,4,24,360]{4,3,2,1,0:T(8,128)(2,1)} async-done(((bf16[4,16,4,24,360]{4,3,2,1,0:T(8,128)(2,1)}), bf16[1,16,4,24,360]{4,3,2,1,0:T(8,128)(2,1)}) %reduce-scatter.5.cloned.1.call-update) | async-done | bytes 1105936 | tf_op jit(solution)/shard_map/reduce_scatter | solution.py:54
  322.5 7.0 %all-to-all-start.1 = ((bf16[16,4,24,360]{3,2,1,0:T(8,128)(2,1)}), bf16[16,4,24,360]{3,2,1,0:T(8,128)(2,1)S(1)}, u32[]{:S(2)}, u32[]{:S(2)}) async-start(bf16[16,4,24,360]{3,2,1,0:T(8,128)(2,1)} %bitcast.89), calls=%async_computation.3 | async-start | bytes 2359296 | tf_op jit(solution)/shard_map/all_to_all | solution.py:123
  329.6 0.2 maximum_reduce_fusion
  329.8 0.6 fusion.37
  330.4 18.3 %all-to-all-done.1 = bf16[16,4,24,360]{3,2,1,0:T(8,128)(2,1)S(1)} async-done(((bf16[16,4,24,360]{3,2,1,0:T(8,128)(2,1)}), bf16[16,4,24,360]{3,2,1,0:T(8,128)(2,1)S(1)}, u32[]{:S(2)}, u32[]{:S(2)}) %all-to-all-start.1) | async-done | bytes 1105952 | tf_op jit(solution)/shard_map/all_to_all | solution.py:123
  348.7 3.9 %gather_fusion = bf16[1024,360]{1,0:T(8,128)(2,1)S(1)} fusion(bf16[1536,360]{1,0:T(8,128)(2,1)S(1)} %bitcast.84, s32[1024]{0:T(1024)S(1)} %broadcast_clamp_fusion), kind=kCustom, calls=%fused_computation.1 | custom fusion | bytes 1478656 | tf_op jit(solution)/shard_map/gather | solution.py:125
  352.6 0.4 reshape.163
  353.0 1.0 multiply_reduce_fusion.1
  354.1 1.2 add_convert_fusion
  355.3 0.8 copy.81
  (42 shorter events, 1.0 us)
Async XLA Ops:
  7.2 260.5 %copy-start = (bf16[2880,16]{0,1:T(8,128)(2,1)S(1)}, bf16[2880,16]{0,1:T(8,128)(2,1)}, u32[]{:S(2)}) copy-start(bf16[2880,16]{0,1:T(8,128)(2,1)} %param.18) | copy-start | bytes 276484
  7.2 20.9 %copy-start.1 = (bf16[256,2880]{0,1:T(8,128)(2,1)S(1)}, bf16[256,2880]{0,1:T(8,128)(2,1)}, u32[]{:S(2)}) copy-start(bf16[256,2880]{0,1:T(8,128)(2,1)} %param.10) | copy-start | bytes 4423684
  7.2 260.4 %reduce-scatter.3.cloned.1.call-start = ((), (), s32[]{:S(2)}) async-start(), calls=%async_computation.5 | async-start | bytes 14155776 | tf_op jit(solution)/shard_map/reduce_scatter | solution.py:54
  8.9 20.2 %copy-start.2 = (bf16[2880]{0:T(1024)(128)(2,1)S(1)}, bf16[2880]{0:T(1024)(128)(2,1)}, u32[]{:S(2)}) copy-start(bf16[2880]{0:T(1024)(128)(2,1)} %param.11) | copy-start | bytes 17284
  249.7 18.0 %copy-start.3 = (bf16[2880]{0:T(1024)(128)(2,1)S(1)}, bf16[2880]{0:T(1024)(128)(2,1)}, u32[]{:S(2)}) copy-start(bf16[2880]{0:T(1024)(128)(2,1)} %param.17) | copy-start | bytes 17284
  249.7 72.9 %reduce-scatter.5.cloned.1.call-start = ((), (), s32[]{:S(2)}) async-start(), calls=%async_computation.6 | async-start | bytes 5898240 | tf_op jit(solution)/shard_map/reduce_scatter | solution.py:54
  267.6 1.1 copy-start.5
  268.3 7.4 %copy-start.4 = (f32[256,4]{0,1:T(4,128)S(1)}, f32[256,4]{0,1:T(4,128)}, u32[]{:S(2)}) copy-start(f32[256,4]{0,1:T(4,128)} %param.13) | copy-start | bytes 12292
  269.4 9.9 %all-to-all-start.2 = ((f32[8,384,4]{1,2,0:T(4,128)}), f32[8,384,4]{1,2,0:T(4,128)S(1)}, u32[]{:S(2)}, u32[]{:S(2)}) async-start(f32[8,384,4]{1,2,0:T(4,128)} %broadcast_in_dim.5), calls=%async_computation.4 | async-start | bytes 98304 | tf_op jit(solution)/shard_map/all_to_all | solution.py:14
  322.5 26.2 %all-to-all-start.1 = ((bf16[16,4,24,360]{3,2,1,0:T(8,128)(2,1)}), bf16[16,4,24,360]{3,2,1,0:T(8,128)(2,1)S(1)}, u32[]{:S(2)}, u32[]{:S(2)}) async-start(bf16[16,4,24,360]{3,2,1,0:T(8,128)(2,1)} %bitcast.89), calls=%async_computation.3 | async-start | bytes 2359296 | tf_op jit(solution)/shard_map/all_to_all | solution.py:123
Sparse Core Ops, SparseCore 0:
  249.8 17.7 reduce-scatter.2
  270.0 52.4 reduce-scatter.4
where the time goes:
time: 364 us; the launch traced here: 363 us
  blocking collectives  111 us (30%)
  local copies, waits for them, and re-layouts  91.5 us (25%)
  waiting for transfers between devices  80.2 us (22%)
  matrix products  29.4 us (8%)
  other arithmetic  25.1 us (7%)
  between operations  14.4 us (4%)
  starting transfers between devices  11.4 us (3%)
    all_to_all x1, blocking collectives, local(): lax.all_to_all(buffer.reshape(row_count, local_experts, CAP, normed.shape...  111 us
    reduce_scatter x2, waiting for transfers between devices, reduced_to_own(): pieces = lax.psum_scatter(pieces, axes[k], scatter_dimension=0, tiled=True)  58.3 us
    scatter x1, local copies, waits for them, and re-layouts, local(): buffer = buffer.at[target].set(normed[token_of])  32.6 us
    reshape x1, local copies, waits for them, and re-layouts, in_blocks(): return jnp.moveaxis(array.reshape(*before, size, -1, *after), dim, 0)  19.5 us
    reshape x1, local copies, waits for them, and re-layouts, reduced_to_own(): pieces = pieces.reshape(*(lax.axis_size(a) for a in axes), *inside)  19.2 us
    all_to_all x1, waiting for transfers between devices, local(): lax.all_to_all(summed, 'row', split_axis=0, concat_axis=0, tiled=True)  18.3 us
    another operation x3, other arithmetic  18.2 us
    dot_general x1, matrix products, local(): jnp.einsum('sjcf,jfd->sjcd', hidden, w_down, preferred_element_type=jnp.f...  17 us
  transfers between devices with their start and end apart: 4, of which 4 were waited for; matrix products, arithmetic and copies ran while one was open for 2% of the time, Pallas kernels for 0%

commit v1 on v0

v1 whole, which is shorter than its diff:
```python
import functools

import jax
import jax.numpy as jnp
from jax import lax
from jax.experimental import pallas as pl
from jax.experimental.pallas import tpu as pltpu
from jax.sharding import Mesh
from jax.sharding import PartitionSpec as P

TOP = 4
CAP = 24
COL = ("y", "core")
LANES = 128
VMEM_MB = 56


def params():
    return pltpu.CompilerParams(vmem_limit_bytes=VMEM_MB * 1024 * 1024)


def vmem():
    return pl.BlockSpec(memory_space=pltpu.VMEM)


def smem():
    return pl.BlockSpec(memory_space=pltpu.SMEM)


def round_up(value, step):
    return -(-value // step) * step


def named_by(ids, expert, weight=None):
    total = None
    for k in range(TOP):
        same = ids[k : k + 1, :] == expert
        term = jnp.where(same, 1.0 if weight is None else weight[k : k + 1, :], 0.0)
        total = term if total is None else total + term
    return total


def slot_mask(hot, slot):
    count = hot.shape[1]
    earlier = lax.broadcasted_iota(jnp.int32, (count, count), 0)
    later = lax.broadcasted_iota(jnp.int32, (count, count), 1)
    before = jnp.where(earlier < later, 1.0, 0.0).astype(jnp.bfloat16)
    rank = jnp.dot(hot.astype(jnp.bfloat16), before, preferred_element_type=jnp.float32)
    return jnp.where(rank == slot.astype(jnp.float32), hot, 0.0)


def normalized(tokens, gain):
    floats = tokens.astype(jnp.float32)
    inverse = lax.rsqrt(jnp.mean(floats * floats, axis=0, keepdims=True) + 1e-05)
    return (floats * inverse * gain.astype(jnp.float32)).astype(jnp.bfloat16)


def dot_nt(first, second):
    return lax.dot_general(
        first, second, (((1,), (1,)), ((), ())), preferred_element_type=jnp.float32
    )


def pick_rows(ids, normed, local_expert, local_experts, rows):
    row = lax.broadcasted_iota(jnp.int32, (rows, 1), 0)
    hot = named_by(ids, (row // CAP) * local_experts + local_expert)
    return dot_nt(slot_mask(hot, row % CAP).astype(jnp.bfloat16), normed).astype(jnp.bfloat16)


def dispatch_kernel(local_experts, own_ref, tokens_ref, gain_ref, ids_ref, out_ref):
    normed = normalized(tokens_ref[...], gain_ref[...])
    out_ref[...] = pick_rows(ids_ref[...], normed, own_ref[0], local_experts, out_ref.shape[0])


def route_kernel(
    local_experts, chunks, own_ref, ids_ref, weight_ref, tokens_ref, gain_ref, gate_ref, next_ids_ref,
    high_ref, low_ref, stats_ref,
):
    ids = ids_ref[...]
    weight = weight_ref[...]
    core = own_ref[0]
    rows = high_ref.shape[2]
    row = lax.broadcasted_iota(jnp.int32, (rows, 1), 0)
    other = (row // CAP) % 2
    half = local_experts // 2
    for k in range(chunks):
        expert = (row // (2 * CAP)) * local_experts + (core + other - 2 * core * other) * half + k
        mask = slot_mask(named_by(ids, expert), row % CAP)
        scaled = (named_by(ids, expert, weight) * mask).T
        high = scaled.astype(jnp.bfloat16)
        high_ref[k] = high
        low_ref[k] = (scaled - high.astype(jnp.float32)).astype(jnp.bfloat16)
    gated = normalized(tokens_ref[...], gain_ref[...])
    logits = jnp.dot(gate_ref[...], gated, preferred_element_type=jnp.float32)
    peak = jnp.max(logits, axis=0, keepdims=True)
    total = jnp.sum(jnp.exp(logits - peak), axis=0, keepdims=True)
    column = lax.broadcasted_iota(jnp.int32, logits.shape, 0) + own_ref[1] * logits.shape[0]
    stats_ref[0:1] = peak
    stats_ref[1:2] = total
    for k in range(TOP):
        same = column == next_ids_ref[k : k + 1, :]
        stats_ref[2 + k : 3 + k] = jnp.sum(jnp.where(same, logits, 0.0), axis=0, keepdims=True)
    stats_ref[2 + TOP :] = jnp.zeros((stats_ref.shape[0] - 2 - TOP, logits.shape[1]), jnp.float32)


def expert_kernel(blocks, own_ref, x_ref, gate_ref, up_ref, down_ref, keep_ref, send_ref):
    x = x_ref[...]
    gate = dot_nt(x, gate_ref[0])
    up = dot_nt(x, up_ref[0])
    hidden = (gate / (1.0 + jnp.exp(-gate)) * up).astype(jnp.bfloat16)
    out = jnp.dot(hidden, down_ref[0], preferred_element_type=jnp.float32)
    width = out.shape[1] // blocks
    padded = keep_ref.shape[2]
    rest = jnp.zeros((out.shape[0], padded - width), keep_ref.dtype)

    def store(even_ref, odd_ref):
        for b in range(blocks):
            target = (even_ref, odd_ref)[b % 2]
            target[b // 2, :, :width] = out[:, b * width : (b + 1) * width].astype(target.dtype)
            target[b // 2, :, width:] = rest

    @pl.when(own_ref[1] == 0)
    def _():
        store(keep_ref, send_ref)

    @pl.when(own_ref[1] != 0)
    def _():
        store(send_ref, keep_ref)


def combine_kernel(high_ref, low_ref, rest_ref, *refs):
    parts, out_ref = refs[:-1], refs[-1]
    total = rest_ref[...].astype(jnp.float32)
    width = out_ref.shape[0]
    summed = None
    for k, part_ref in enumerate(parts):
        part = part_ref[...]
        for weight_ref in (high_ref, low_ref):
            term = jnp.dot(weight_ref[k], part, preferred_element_type=jnp.float32)
            summed = term if summed is None else summed + term
    out_ref[...] = (total + summed.T[:width]).astype(out_ref.dtype)


def run_expert(x, w_gate, w_up, w_down, expert, core, blocks, padded):
    rows, features = x.shape
    hidden = w_gate.shape[1]
    out = jax.ShapeDtypeStruct((blocks // 2, rows, padded), jnp.bfloat16)
    whole = lambda *shape: pl.BlockSpec(shape, lambda i, own: (0,) * len(shape))
    return pl.pallas_call(
        functools.partial(expert_kernel, blocks),
        grid_spec=pltpu.PrefetchScalarGridSpec(
            num_scalar_prefetch=1,
            grid=(1,),
            in_specs=[
                whole(rows, features),
                pl.BlockSpec((1, hidden, features), lambda i, own: (own[0], 0, 0)),
                pl.BlockSpec((1, hidden, features), lambda i, own: (own[0], 0, 0)),
                pl.BlockSpec((1, hidden, features), lambda i, own: (own[0], 0, 0)),
            ],
            out_specs=[whole(*out.shape), whole(*out.shape)],
        ),
        out_shape=[out, out],
        compiler_params=params(),
        name="expert",
    )(jnp.stack([expert, core]).astype(jnp.int32), x, w_gate, w_up, w_down)


def swap_cores(x):
    return lax.ppermute(x, "core", [(0, 1), (1, 0)])


def merge_stats(first, second):
    peak = jnp.maximum(first[0:1], second[0:1])
    total = first[1:2] * jnp.exp(first[0:1] - peak) + second[1:2] * jnp.exp(second[0:1] - peak)
    return jnp.concatenate([peak, total, first[2:] + second[2:]], axis=0)


def local(
    tokens, moe_gain, route_ids, route_weight, w_gate, w_up, w_down, next_gain, next_gate, next_ids
):
    row_count = lax.axis_size("row")
    y_count = lax.axis_size("y")
    blocks = 2 * y_count
    tok_rows, features = tokens.shape
    tokens, route_ids, route_weight, next_ids = tokens.T, route_ids.T, route_weight.T, next_ids.T
    next_gate = next_gate.T
    w_gate, w_up = jnp.swapaxes(w_gate, 1, 2), jnp.swapaxes(w_up, 1, 2)
    local_experts = w_gate.shape[0]
    chunks = local_experts // 2
    width = features // blocks
    padded = round_up(width, LANES)
    rows = row_count * CAP
    core = lax.axis_index("core")
    position = lax.axis_index(COL)
    moe_gain = moe_gain.reshape(-1, 1)
    next_gain = next_gain.reshape(-1, 1)

    own = [core * chunks + k for k in range(chunks)]
    others = [(1 - core) * chunks + k for k in range(chunks)]

    def dispatched(k):
        return pl.pallas_call(
            functools.partial(dispatch_kernel, local_experts),
            in_specs=[smem(), vmem(), vmem(), vmem()],
            out_specs=vmem(),
            out_shape=jax.ShapeDtypeStruct((rows, features), jnp.bfloat16),
            compiler_params=params(),
            name="dispatch",
        )(own[k].reshape(1).astype(jnp.int32), tokens, moe_gain, route_ids)

    arrived = []
    for k in range(chunks):
        sent = dispatched(k).reshape(row_count, CAP, features)
        arrived.append(lax.all_to_all(sent, "row", split_axis=0, concat_axis=0, tiled=True))

    table = jax.ShapeDtypeStruct((chunks, tok_rows, 2 * rows), jnp.bfloat16)
    high, low, stats = pl.pallas_call(
        functools.partial(route_kernel, local_experts, chunks),
        in_specs=[smem()] + [vmem()] * 6,
        out_specs=[vmem()] * 3,
        out_shape=[table, table, jax.ShapeDtypeStruct((8, tok_rows), jnp.float32)],
        compiler_params=params(),
        name="route",
    )(jnp.stack([core, position]).astype(jnp.int32), route_ids, route_weight, tokens, next_gain, next_gate, next_ids)

    returned = []
    for k in range(chunks):
        mine = arrived[k]
        theirs = swap_cores(mine)
        keep0, send0 = run_expert(mine.reshape(rows, features), w_gate, w_up, w_down, own[k], core, blocks, padded)
        got0 = swap_cores(send0)
        keep1, send1 = run_expert(theirs.reshape(rows, features), w_gate, w_up, w_down, others[k], core, blocks, padded)
        got1 = swap_cores(send1)
        shape = (y_count, row_count, 1, CAP, padded)
        both = jnp.concatenate(
            [(keep0 + got1).reshape(shape), (keep1 + got0).reshape(shape)], axis=2
        )
        summed = lax.psum_scatter(both, "y", scatter_dimension=0, tiled=True)[0]
        back = lax.all_to_all(summed, "row", split_axis=0, concat_axis=0, tiled=True)
        returned.append(back.reshape(2 * rows, padded))

    merged = merge_stats(stats, swap_cores(stats))
    for step in (1, 2):
        moved = lax.ppermute(merged, "y", [(i, i ^ step) for i in range(y_count)])
        merged = merge_stats(merged, moved)
    next_logprob = (merged[2 : 2 + TOP] - merged[0:1] - jnp.log(merged[1:2])).T

    rest = lax.dynamic_slice_in_dim(tokens, position * width, width, 0)
    mixed = pl.pallas_call(
        combine_kernel,
        in_specs=[vmem()] * (3 + chunks),
        out_specs=vmem(),
        out_shape=jax.ShapeDtypeStruct((width, tok_rows), jnp.bfloat16),
        compiler_params=params(),
        name="combine",
    )(high, low, rest, *returned)
    return (mixed.T, next_logprob)


def solution(mesh):
    torus = Mesh(mesh.devices.reshape(4, 2, mesh.shape["row"]), ("y", "core", "row"))
    return jax.shard_map(
        local,
        mesh=torus,
        in_specs=(
            P("row", None),
            P(),
            P("row", None),
            P("row", None),
            P("row", None, COL),
            P("row", None, COL),
            P("row", COL, None),
            P(),
            P(None, COL),
            P("row", None),
        ),
        out_specs=(P("row", COL), P("row", None)),
        check_vma=False,
    )
```

time: 364 us -> 210 us (0.58)
  local copies, waits for them, and re-layouts: 91.5 us -> 8.06 us
  blocking collectives: 111 us -> 38.1 us
  Pallas kernels: 0 us -> 59.5 us
  matrix products: 29.4 us -> 0 us
  waiting for transfers between devices: 80.2 us -> 55 us
  other arithmetic: 25.1 us -> 14 us
  starting transfers between devices: 11.4 us -> 20.5 us
    all_to_all x1, blocking collectives: 111 us -> 38.1 us  [local(): lax.all_to_all(sent, 'row', split_axis=0, concat_axis=0, tiled=True)]
    pallas_call x0 -> x8, Pallas kernels: none -> 59.5 us  [the longest x4 41.1 us: run_expert(): pl.pallas_call(functools.partial(expert_kernel, blocks), grid_spec=pltpu....]
    reduce_scatter x2, waiting for transfers between devices: 58.3 us -> 10.9 us  [local(): summed = lax.psum_scatter(both, 'y', scatter_dimension=0, tiled=True)[0]]
    reshape x6 -> x2, local copies, waits for them, and re-layouts: 39 us -> 3.42 us  [the longest x1 2.02 us: local(): moe_gain = moe_gain.reshape(-1, 1)]
    scatter x1 -> x0, local copies, waits for them, and re-layouts: 32.6 us -> none  [local(): buffer = buffer.at[target].set(normed[token_of])]
    dot_general x3 -> x0, matrix products: 29.4 us -> none  [the longest x1 17 us: local(): jnp.einsum('sjcf,jfd->sjcd', hidden, w_down, preferred_element_type=jnp.f...]
    all_to_all x1, waiting for transfers between devices: 3.58 us -> 31.6 us  [local(): lax.all_to_all(sent, 'row', split_axis=0, concat_axis=0, tiled=True)]
    another operation x3 -> x5, other arithmetic: 18.2 us -> 3.35 us  [the longest x4 2.7 us: run_expert(): jnp.stack([expert, core]).astype(jnp.int32)]
  transfers between devices with their start and end apart: 4 -> 14, of which waited for: 4 -> 5; matrix products, arithmetic and copies ran while one was open for 2% -> 8% of each run, Pallas kernels for 0% -> 24%
where the time goes in v1:
time: 210 us; the launch traced here: 209 us
  Pallas kernels  59.5 us (28%)
  waiting for transfers between devices  55 us (26%)
  blocking collectives  38.1 us (18%)
  starting transfers between devices  20.5 us (10%)
  between operations  14.2 us (7%)
  other arithmetic  14 us (7%)
  local copies, waits for them, and re-layouts  8.06 us (4%)
    pallas_call x4, Pallas kernels, run_expert(): pl.pallas_call(functools.partial(expert_kernel, blocks), grid_spec=pltpu....  41.1 us
    all_to_all x1, blocking collectives, local(): lax.all_to_all(sent, 'row', split_axis=0, concat_axis=0, tiled=True)  38.1 us
    all_to_all x1, waiting for transfers between devices, local(): lax.all_to_all(sent, 'row', split_axis=0, concat_axis=0, tiled=True)  31.6 us
    reduce_scatter x2, waiting for transfers between devices, local(): summed = lax.psum_scatter(both, 'y', scatter_dimension=0, tiled=True)[0]  10.9 us
    all_to_all x2, starting transfers between devices, local(): lax.all_to_all(summed, 'row', split_axis=0, concat_axis=0, tiled=True)  10.9 us
    all_to_all x2, waiting for transfers between devices, local(): lax.all_to_all(summed, 'row', split_axis=0, concat_axis=0, tiled=True)  9.92 us
    pallas_call x2, Pallas kernels, dispatched(): pl.pallas_call(functools.partial(dispatch_kernel, local_experts), in_spec...  9.35 us
    pallas_call x1, Pallas kernels, local(): pl.pallas_call(functools.partial(route_kernel, local_experts, chunks), in...  5.49 us
  transfers between devices with their start and end apart: 14, of which 5 were waited for; matrix products, arithmetic and copies ran while one was open for 8% of the time, Pallas kernels for 24%

profile of v1, /device:TPU:0, one launch (start us, length us, event | category | flops | bytes accessed | tf_op | source)
XLA Modules:
  0.0 209.3 jit_solution(11115421890775979704)
XLA Ops:
  7.2 2.0 reshape.63.gain_ref
  9.2 4.7 %dispatch.3 = bf16[384,2880]{1,0:T(8,128)(2,1)} custom-call(s32[1]{0:T(128)} %bitcast.21.own_ref, bf16[2880,256]{1,0:T(8,128)(2,1)} %bitcast.50, bf16[2880,1]{1,0:T(8,128)(2,1)} %reshape.63.gain_ref, s32[4,256]{1,0:T(4,128)} %bitcast.68), custom_call_target="tpu_custom_call" | custom-call | tf_op jit(solution)/shard_map/dispatch/pallas_call | solution.py:202
  13.9 38.1 %all_to_all.20 = bf16[16,24,2880]{2,1,0:T(8,128)(2,1)S(1)} all-to-all(bf16[16,24,2880]{2,1,0:T(8,128)(2,1)} %bitcast.56), channel_id=1, replica_groups=mesh['y'=4,'core'=2,'row'=16] {'row'}, dimensions={0} | all-to-all | bytes 4423680 | tf_op jit(solution)/shard_map/all_to_all | solution.py:214
  52.0 0.7 pad_add_fusion.3.own_ref
  52.7 0.7 pad_add_fusion.4.own_ref
  53.3 0.0 copy-done.1
  53.3 10.2 %expert.6 = (bf16[4,384,384]{2,1,0:T(8,128)(2,1)}, bf16[4,384,384]{2,1,0:T(8,128)(2,1)}) custom-call(s32[2]{0:T(128)} %pad_add_fusion.3.own_ref, bf16[384,2880]{1,0:T(8,128)(2,1)} %bitcast.54, bf16[4,360,2880]{2,1,0:T(8,128)(2,1)} %bitcast.42, bf16[4,360,2880]{2,1,0:T(8,128)(2,1)} %bitcast.46, bf16[4,360,2880]{2,1,0:T(8,128)(2,1)} %down_ref.7), custom_call_target="tpu_custom_call" | custom-call | tf_op jit(solution)/shard_map/expert/pallas_call | solution.py:149
  63.6 0.4 collective-permute-start.5
  64.0 10.3 %expert.7 = (bf16[4,384,384]{2,1,0:T(8,128)(2,1)}, bf16[4,384,384]{2,1,0:T(8,128)(2,1)}) custom-call(s32[2]{0:T(128)} %pad_add_fusion.4.own_ref, bf16[384,2880]{1,0:T(8,128)(2,1)} %bitcast.25.x_ref, bf16[4,360,2880]{2,1,0:T(8,128)(2,1)} %bitcast.43, bf16[4,360,2880]{2,1,0:T(8,128)(2,1)} %bitcast.47, bf16[4,360,2880]{2,1,0:T(8,128)(2,1)} %down_ref.7), custom_call_target="tpu_custom_call" | custom-call | tf_op jit(solution)/shard_map/expert/pallas_call | solution.py:149
  74.2 0.1 collective-permute-start.4
  74.3 4.7 %dispatch.2 = bf16[384,2880]{1,0:T(8,128)(2,1)} custom-call(s32[1]{0:T(128)} %bitcast.8.own_ref, bf16[2880,256]{1,0:T(8,128)(2,1)} %bitcast.51, bf16[2880,1]{1,0:T(8,128)(2,1)} %reshape.63.gain_ref, s32[4,256]{1,0:T(4,128)} %bitcast.69), custom_call_target="tpu_custom_call" | custom-call | tf_op jit(solution)/shard_map/dispatch/pallas_call | solution.py:202
  79.0 3.7 %all-to-all-start = ((bf16[16,24,2880]{2,1,0:T(8,128)(2,1)}), bf16[16,24,2880]{2,1,0:T(8,128)(2,1)S(1)}, u32[]{:S(2)}, u32[]{:S(2)}) async-start(bf16[16,24,2880]{2,1,0:T(8,128)(2,1)} %bitcast.55), calls=%async_computation | async-start | bytes 4521984 | tf_op jit(solution)/shard_map/all_to_all | solution.py:214
  82.7 0.0 reduce-scatter.5.cloned.1.call-start
  82.8 1.7 add.53
  84.5 1.6 add.52
  86.1 1.7 pad_maximum_fusion.1
  87.8 0.0 reduce-scatter.3.cloned.1.call-start
  87.8 31.6 %all-to-all-done = bf16[16,24,2880]{2,1,0:T(8,128)(2,1)S(1)} async-done(((bf16[16,24,2880]{2,1,0:T(8,128)(2,1)}), bf16[16,24,2880]{2,1,0:T(8,128)(2,1)S(1)}, u32[]{:S(2)}, u32[]{:S(2)}) %all-to-all-start) | async-done | bytes 2211872 | tf_op jit(solution)/shard_map/all_to_all | solution.py:214
  119.4 0.7 pad_add_fusion.1.own_ref
  120.1 0.7 pad_add_fusion.2.own_ref
  120.8 10.2 %expert.4 = (bf16[4,384,384]{2,1,0:T(8,128)(2,1)}, bf16[4,384,384]{2,1,0:T(8,128)(2,1)}) custom-call(s32[2]{0:T(128)} %pad_add_fusion.1.own_ref, bf16[384,2880]{1,0:T(8,128)(2,1)} %bitcast.53, bf16[4,360,2880]{2,1,0:T(8,128)(2,1)} %bitcast.44, bf16[4,360,2880]{2,1,0:T(8,128)(2,1)} %bitcast.48, bf16[4,360,2880]{2,1,0:T(8,128)(2,1)} %down_ref.7), custom_call_target="tpu_custom_call" | custom-call | tf_op jit(solution)/shard_map/expert/pallas_call | solution.py:149
  131.0 0.4 collective-permute-start.2
  131.4 1.5 copy-done.4
  132.9 10.4 %expert.5 = (bf16[4,384,384]{2,1,0:T(8,128)(2,1)}, bf16[4,384,384]{2,1,0:T(8,128)(2,1)}) custom-call(s32[2]{0:T(128)} %pad_add_fusion.2.own_ref, bf16[384,2880]{1,0:T(8,128)(2,1)} %bitcast.63, bf16[4,360,2880]{2,1,0:T(8,128)(2,1)} %bitcast.45, bf16[4,360,2880]{2,1,0:T(8,128)(2,1)} %bitcast.49, bf16[4,360,2880]{2,1,0:T(8,128)(2,1)} %down_ref.7), custom_call_target="tpu_custom_call" | custom-call | tf_op jit(solution)/shard_map/expert/pallas_call | solution.py:149
  143.3 0.1 collective-permute-start.1
  143.4 1.7 add.49
  145.0 1.3 collective-permute-done.1
  146.3 0.3 add.48
  146.7 1.6 pad_maximum_fusion
  148.3 0.0 reduce-scatter.3.cloned.1.call-update
  148.3 0.7 copy-done.7
  149.0 1.4 reshape.62.gain_ref
  150.4 0.7 pad_add_fusion.own_ref
  151.0 5.5 %route.1 = (bf16[2,256,768]{2,1,0:T(8,128)(2,1)}, bf16[2,256,768]{2,1,0:T(8,128)(2,1)}, f32[8,256]{1,0:T(8,128)}) custom-call(s32[2]{0:T(128)} %pad_add_fusion.own_ref, s32[4,256]{1,0:T(4,128)} %bitcast.70, f32[4,256]{1,0:T(4,128)} %bitcast.71, bf16[2880,256]{1,0:T(8,128)(2,1)} %bitcast.52, bf16[2880,1]{1,0:T(8,128)(2,1)} %reshape.62.gain_ref, ...), custom_call_target="tpu_custom_call" | custom-call | tf_op jit(solution)/shard_map/route/pallas_call | solution.py:217
  156.5 0.1 collective-permute-start.6
  156.7 1.2 collective-permute-done.6
  157.9 0.8 fusion.5
  158.7 0.7 slice_add_fusion.1
  159.4 1.7 collective-permute-start.7
  161.1 4.0 %all-to-all-start.3 = ((bf16[16,2,24,384]{3,2,1,0:T(8,128)(2,1)}), bf16[16,2,24,384]{3,2,1,0:T(8,128)(2,1)S(1)}, u32[]{:S(2)}, u32[]{:S(2)}) async-start(bf16[16,2,24,384]{3,2,1,0:T(8,128)(2,1)} %bitcast.64), calls=%async_computation.5 | async-start | bytes 1179648 | tf_op jit(solution)/shard_map/all_to_all | solution.py:239
  165.1 2.9 %collective-permute-start.8 = (f32[8,256]{1,0:T(8,128)S(1)}, f32[8,256]{1,0:T(8,128)S(1)}, u32[]{:S(2)}, u32[]{:S(2)}) collective-permute-start(f32[8,256]{1,0:T(8,128)S(1)} %pad_maximum_fusion.3), channel_id=1, source_target_pairs={{0,64},{32,96},{64,0},{96,32},{1,65},{33,97},{65,1},{97,33},{2,66}... | collective-permute-start | bytes 24584 | tf_op jit(solution)/shard_map/ppermute | solution.py:244
  168.0 10.9 %reduce-scatter.3.cloned.1.call-done = bf16[1,16,2,24,384]{4,3,2,1,0:T(8,128)(2,1)} async-done(((bf16[4,16,2,24,384]{4,3,2,1,0:T(8,128)(2,1)}), bf16[1,16,2,24,384]{4,3,2,1,0:T(8,128)(2,1)}) %reduce-scatter.3.cloned.1.call-update) | async-done | bytes 589840 | tf_op jit(solution)/shard_map/reduce_scatter | solution.py:238
  179.0 6.9 %all-to-all-start.1 = ((bf16[16,2,24,384]{3,2,1,0:T(8,128)(2,1)}), bf16[16,2,24,384]{3,2,1,0:T(8,128)(2,1)S(1)}, u32[]{:S(2)}, u32[]{:S(2)}) async-start(bf16[16,2,24,384]{3,2,1,0:T(8,128)(2,1)} %bitcast.65), calls=%async_computation.2 | async-start | bytes 1179648 | tf_op jit(solution)/shard_map/all_to_all | solution.py:239
  185.9 1.6 dynamic-slice_bitcast_fusion.rest_ref
  187.6 0.6 fusion.2
  188.2 9.9 %all-to-all-done.1 = bf16[16,2,24,384]{3,2,1,0:T(8,128)(2,1)S(1)} async-done(((bf16[16,2,24,384]{3,2,1,0:T(8,128)(2,1)}), bf16[16,2,24,384]{3,2,1,0:T(8,128)(2,1)S(1)}, u32[]{:S(2)}, u32[]{:S(2)}) %all-to-all-start.1) | async-done | bytes 589856 | tf_op jit(solution)/shard_map/all_to_all | solution.py:239
  198.1 0.8 copy-done.3
  198.9 3.5 %combine.1 = bf16[360,256]{1,0:T(8,128)(2,1)} custom-call(bf16[2,256,768]{2,1,0:T(8,128)(2,1)} %get-tuple-element.13.high_ref, bf16[2,256,768]{2,1,0:T(8,128)(2,1)} %get-tuple-element.14.low_ref, bf16[360,256]{1,0:T(8,128)(2,1)} %dynamic-slice_bitcast_fusion.rest_ref, bf16[768,384]{1,0:T(8,128)(2,1)} %bitcast.62, bf16[768,384]{1,0:T(8,128)(2,1)} %bitcast.61), custom_call_target="tpu_custom_call" | custom-call | tf_op jit(solution)/shard_map/combine/pallas_call | solution.py:249
  (30 shorter events, 0.1 us)
Async XLA Ops:
  52.0 1.4 copy-start.1
  52.0 12.0 %collective-permute-start.3 = (bf16[16,24,2880]{2,1,0:T(8,128)(2,1)S(1)}, bf16[16,24,2880]{2,1,0:T(8,128)(2,1)}, u32[]{:S(2)}, u32[]{:S(2)}) collective-permute-start(bf16[16,24,2880]{2,1,0:T(8,128)(2,1)S(1)} %all_to_all.20), channel_id=1, source_target_pairs={{0,16},{16,0},{1,17},{17,1},{2,18},{18,2},{3,19},{19,3},{4,20},{20... | collective-permute-start | bytes 6635528 | tf_op jit(solution)/shard_map/ppermute | solution.py:169
  63.6 19.2 %collective-permute-start.5 = (bf16[4,384,384]{2,1,0:T(8,128)(2,1)}, bf16[4,384,384]{2,1,0:T(8,128)(2,1)S(1)}, u32[]{:S(2)}, u32[]{:S(2)}) collective-permute-start(bf16[4,384,384]{2,1,0:T(8,128)(2,1)} %get-tuple-element.22), channel_id=1, source_target_pairs={{0,16},{16,0},{1,17},{17,1},{2,18},{18,2},{3,19},{19,3},{4,20},{20... | collective-permute-start | bytes 3538952 | tf_op jit(solution)/shard_map/ppermute | solution.py:169
  74.2 10.2 %collective-permute-start.4 = (bf16[4,384,384]{2,1,0:T(8,128)(2,1)}, bf16[4,384,384]{2,1,0:T(8,128)(2,1)}, u32[]{:S(2)}, u32[]{:S(2)}) collective-permute-start(bf16[4,384,384]{2,1,0:T(8,128)(2,1)} %get-tuple-element.20), channel_id=1, source_target_pairs={{0,16},{16,0},{1,17},{17,1},{2,18},{18,2},{3,19},{19,3},{4,20},{20... | collective-permute-start | bytes 3538952 | tf_op jit(solution)/shard_map/ppermute | solution.py:169
  79.0 40.4 %all-to-all-start = ((bf16[16,24,2880]{2,1,0:T(8,128)(2,1)}), bf16[16,24,2880]{2,1,0:T(8,128)(2,1)S(1)}, u32[]{:S(2)}, u32[]{:S(2)}) async-start(bf16[16,24,2880]{2,1,0:T(8,128)(2,1)} %bitcast.55), calls=%async_computation | async-start | bytes 4521984 | tf_op jit(solution)/shard_map/all_to_all | solution.py:214
  82.7 78.3 %reduce-scatter.5.cloned.1.call-start = ((), (), s32[]{:S(2)}) async-start(), calls=%async_computation.7 | async-start | bytes 2949120 | tf_op jit(solution)/shard_map/reduce_scatter | solution.py:238
  82.8 1.7 copy-start.5
  87.8 91.2 %reduce-scatter.3.cloned.1.call-start = ((), (), s32[]{:S(2)}) async-start(), calls=%async_computation.6 | async-start | bytes 2949120 | tf_op jit(solution)/shard_map/reduce_scatter | solution.py:238
  119.4 1.4 copy-start
  119.4 12.0 %collective-permute-start = (bf16[16,24,2880]{2,1,0:T(8,128)(2,1)S(1)}, bf16[16,24,2880]{2,1,0:T(8,128)(2,1)S(1)}, u32[]{:S(2)}, u32[]{:S(2)}) collective-permute-start(bf16[16,24,2880]{2,1,0:T(8,128)(2,1)S(1)} %all-to-all-done), channel_id=1, source_target_pairs={{0,16},{16,0},{1,17},{17,1},{2,18},{18,2},{3,19},{19,3},{4,20},{20... | collective-permute-start | bytes 6635528 | tf_op jit(solution)/shard_map/ppermute | solution.py:169
  131.0 12.4 %collective-permute-start.2 = (bf16[4,384,384]{2,1,0:T(8,128)(2,1)}, bf16[4,384,384]{2,1,0:T(8,128)(2,1)S(1)}, u32[]{:S(2)}, u32[]{:S(2)}) collective-permute-start(bf16[4,384,384]{2,1,0:T(8,128)(2,1)} %get-tuple-element.18), channel_id=1, source_target_pairs={{0,16},{16,0},{1,17},{17,1},{2,18},{18,2},{3,19},{19,3},{4,20},{20... | collective-permute-start | bytes 3538952 | tf_op jit(solution)/shard_map/ppermute | solution.py:169
  131.4 1.5 copy-start.4
  143.3 3.1 %collective-permute-start.1 = (bf16[4,384,384]{2,1,0:T(8,128)(2,1)}, bf16[4,384,384]{2,1,0:T(8,128)(2,1)S(1)}, u32[]{:S(2)}, u32[]{:S(2)}) collective-permute-start(bf16[4,384,384]{2,1,0:T(8,128)(2,1)} %get-tuple-element.16), channel_id=1, source_target_pairs={{0,16},{16,0},{1,17},{17,1},{2,18},{18,2},{3,19},{19,3},{4,20},{20... | collective-permute-start | bytes 3538952 | tf_op jit(solution)/shard_map/ppermute | solution.py:169
  143.4 3.0 %copy-start.6 = (bf16[4,384,384]{2,1,0:T(8,128)(2,1)S(1)}, bf16[4,384,384]{2,1,0:T(8,128)(2,1)}, u32[]{:S(2)}) copy-start(bf16[4,384,384]{2,1,0:T(8,128)(2,1)} %get-tuple-element.15) | copy-start | bytes 3538948
  148.3 0.7 copy-start.7
  156.5 1.4 collective-permute-start.6
  159.4 5.6 %collective-permute-start.7 = (f32[8,256]{1,0:T(8,128)S(1)}, f32[8,256]{1,0:T(8,128)S(1)}, u32[]{:S(2)}, u32[]{:S(2)}) collective-permute-start(f32[8,256]{1,0:T(8,128)S(1)} %pad_maximum_fusion.2), channel_id=1, source_target_pairs={{0,32},{32,0},{64,96},{96,64},{1,33},{33,1},{65,97},{97,65},{2,34}... | collective-permute-start | bytes 24584 | tf_op jit(solution)/shard_map/ppermute | solution.py:244
  161.1 17.9 %all-to-all-start.3 = ((bf16[16,2,24,384]{3,2,1,0:T(8,128)(2,1)}), bf16[16,2,24,384]{3,2,1,0:T(8,128)(2,1)S(1)}, u32[]{:S(2)}, u32[]{:S(2)}) async-start(bf16[16,2,24,384]{3,2,1,0:T(8,128)(2,1)} %bitcast.64), calls=%async_computation.5 | async-start | bytes 1179648 | tf_op jit(solution)/shard_map/all_to_all | solution.py:239
  165.1 22.5 %collective-permute-start.8 = (f32[8,256]{1,0:T(8,128)S(1)}, f32[8,256]{1,0:T(8,128)S(1)}, u32[]{:S(2)}, u32[]{:S(2)}) collective-permute-start(f32[8,256]{1,0:T(8,128)S(1)} %pad_maximum_fusion.3), channel_id=1, source_target_pairs={{0,64},{32,96},{64,0},{96,32},{1,65},{33,97},{65,1},{97,33},{2,66}... | collective-permute-start | bytes 24584 | tf_op jit(solution)/shard_map/ppermute | solution.py:244
  179.0 19.1 %copy-start.2 = (bf16[16,2,24,384]{3,2,1,0:T(8,128)(2,1)}, bf16[16,2,24,384]{3,2,1,0:T(8,128)(2,1)S(1)}, u32[]{:S(2)}) copy-start(bf16[16,2,24,384]{3,2,1,0:T(8,128)(2,1)S(1)} %all-to-all-done.3) | copy-start | bytes 1769476
  179.0 19.1 %all-to-all-start.1 = ((bf16[16,2,24,384]{3,2,1,0:T(8,128)(2,1)}), bf16[16,2,24,384]{3,2,1,0:T(8,128)(2,1)S(1)}, u32[]{:S(2)}, u32[]{:S(2)}) async-start(bf16[16,2,24,384]{3,2,1,0:T(8,128)(2,1)} %bitcast.65), calls=%async_computation.2 | async-start | bytes 1179648 | tf_op jit(solution)/shard_map/all_to_all | solution.py:239
  198.1 0.8 copy-start.3
Sparse Core Ops, SparseCore 0:
  87.9 33.4 reduce-scatter.4
  148.4 30.4 reduce-scatter.2

commit v2 on v1

v2 whole, which is shorter than its diff:
```python
import functools

import jax
import jax.numpy as jnp
from jax import lax
from jax.experimental import pallas as pl
from jax.experimental.pallas import tpu as pltpu
from jax.sharding import Mesh
from jax.sharding import PartitionSpec as P


TOP = 4
CAP = 24
COL = ("y", "core")
LANES = 128


def params(megabytes=24):
    return pltpu.CompilerParams(vmem_limit_bytes=megabytes * 1024 * 1024)


def vmem():
    return pl.BlockSpec(memory_space=pltpu.VMEM)


def hbm():
    return pl.BlockSpec(memory_space=pltpu.MemorySpace.HBM)


def smem():
    return pl.BlockSpec(memory_space=pltpu.SMEM)


def round_up(value, step):
    return -(-value // step) * step


def named_by(ids, expert, weight=None):
    total = None
    for k in range(TOP):
        same = ids[k : k + 1, :] == expert
        term = jnp.where(same, 1.0 if weight is None else weight[k : k + 1, :], 0.0)
        total = term if total is None else total + term
    return total


def slot_mask(hot, slot):
    count = hot.shape[1]
    earlier = lax.broadcasted_iota(jnp.int32, (count, count), 0)
    later = lax.broadcasted_iota(jnp.int32, (count, count), 1)
    before = jnp.where(earlier < later, 1.0, 0.0).astype(jnp.bfloat16)
    rank = jnp.dot(hot.astype(jnp.bfloat16), before, preferred_element_type=jnp.float32)
    return jnp.where(rank == slot.astype(jnp.float32), hot, 0.0)


def inverse_norm(tokens):
    floats = tokens.astype(jnp.float32)
    return lax.rsqrt(jnp.mean(floats * floats, axis=0, keepdims=True) + 1e-05)


def normalized(tokens, gain):
    scaled = tokens.astype(jnp.float32) * inverse_norm(tokens)
    return (scaled * gain.astype(jnp.float32)).astype(jnp.bfloat16)


def dot_nt(first, second):
    return lax.dot_general(
        first, second, (((1,), (1,)), ((), ())), preferred_element_type=jnp.float32
    )


def dispatch_kernel(local_experts, own_ref, tokens_ref, gain_ref, ids_ref, out_ref):
    tokens = tokens_ref[...]
    rows = out_ref.shape[0]
    row = lax.broadcasted_iota(jnp.int32, (rows, 1), 0)
    hot = named_by(ids_ref[...], (row // CAP) * local_experts + own_ref[0])
    chosen = slot_mask(hot, row % CAP)
    inverse = jnp.sum(chosen * inverse_norm(tokens), axis=1, keepdims=True)
    picked = dot_nt(chosen.astype(jnp.bfloat16), tokens)
    out_ref[...] = (picked * inverse * gain_ref[...].astype(jnp.float32)).astype(jnp.bfloat16)


def route_kernel(
    local_experts, chunks, own_ref, ids_ref, weight_ref, tokens_ref, gain_ref, gate_ref, next_ids_ref,
    high_ref, low_ref, stats_ref,
):
    ids = ids_ref[...]
    weight = weight_ref[...]
    core = own_ref[0]
    rows = high_ref.shape[2]
    row = lax.broadcasted_iota(jnp.int32, (rows, 1), 0)
    other = (row // CAP) % 2
    half = local_experts // 2
    for k in range(chunks):
        expert = (row // (2 * CAP)) * local_experts + (core + other - 2 * core * other) * half + k
        mask = slot_mask(named_by(ids, expert), row % CAP)
        scaled = (named_by(ids, expert, weight) * mask).T
        high = scaled.astype(jnp.bfloat16)
        high_ref[k] = high
        low_ref[k] = (scaled - high.astype(jnp.float32)).astype(jnp.bfloat16)
    gated = normalized(tokens_ref[...], gain_ref[...])
    logits = jnp.dot(gate_ref[...], gated, preferred_element_type=jnp.float32)
    peak = jnp.max(logits, axis=0, keepdims=True)
    total = jnp.sum(jnp.exp(logits - peak), axis=0, keepdims=True)
    column = lax.broadcasted_iota(jnp.int32, logits.shape, 0) + own_ref[1] * logits.shape[0]
    stats_ref[0:1] = peak
    stats_ref[1:2] = total
    for k in range(TOP):
        same = column == next_ids_ref[k : k + 1, :]
        stats_ref[2 + k : 3 + k] = jnp.sum(jnp.where(same, logits, 0.0), axis=0, keepdims=True)
    stats_ref[2 + TOP :] = jnp.zeros((stats_ref.shape[0] - 2 - TOP, logits.shape[1]), jnp.float32)


def expert_kernel(
    blocks, parts, own_ref, x_hbm, gate_hbm, up_hbm, down_hbm, keep_hbm, send_hbm,
    x_ref, gate_ref, up_ref, down_ref, even_ref, odd_ref, in_sems, out_sems,
):
    expert = own_ref[2]
    loads = [
        pltpu.make_async_copy(source, target, in_sems.at[i])
        for i, (source, target) in enumerate(
            (
                (x_hbm, x_ref),
                (gate_hbm.at[expert], gate_ref),
                (up_hbm.at[expert], up_ref),
                (down_hbm.at[expert], down_ref),
            )
        )
    ]
    for load in loads:
        load.start()
    loads[0].wait()
    loads[1].wait()
    x = x_ref[...]
    gate = dot_nt(x, gate_ref[...])
    loads[2].wait()
    up = dot_nt(x, up_ref[...])
    hidden = (gate / (1.0 + jnp.exp(-gate)) * up).astype(jnp.bfloat16)
    loads[3].wait()
    rows, features = x.shape
    around = blocks // 2
    width = features // blocks
    rest = jnp.zeros((rows // parts, even_ref.shape[2] - width), even_ref.dtype)

    def stores(part, even_hbm, odd_hbm):
        here = pl.ds(part * (rows // parts), rows // parts)
        return [
            pltpu.make_async_copy(buf.at[:, here], target.at[:, here], out_sems.at[part, i])
            for i, (buf, target) in enumerate(((even_ref, even_hbm), (odd_ref, odd_hbm)))
        ]

    def each(part, act):
        @pl.when(own_ref[0] == 0)
        def _():
            for copy in stores(part, keep_hbm, send_hbm):
                act(copy)

        @pl.when(own_ref[0] != 0)
        def _():
            for copy in stores(part, send_hbm, keep_hbm):
                act(copy)

    for part in range(parts):
        here = slice(part * (rows // parts), (part + 1) * (rows // parts))
        out = jnp.dot(hidden[here], down_ref[...], preferred_element_type=jnp.float32)
        for b in range(blocks):
            target = (even_ref, odd_ref)[b % 2]
            j = lax.rem(b // 2 - own_ref[1] + around, around)
            target[j, here, :width] = out[:, b * width : (b + 1) * width].astype(target.dtype)
            target[j, here, width:] = rest
        each(part, lambda copy: copy.start())
    for part in range(parts):
        each(part, lambda copy: copy.wait())


def combine_kernel(high_ref, low_ref, part_ref, rest_ref, out_ref):
    part = part_ref[...]
    summed = jnp.dot(high_ref[...], part, preferred_element_type=jnp.float32)
    summed = summed + jnp.dot(low_ref[...], part, preferred_element_type=jnp.float32)
    width = out_ref.shape[0]
    out_ref[...] = (rest_ref[...].astype(jnp.float32) + summed.T[:width]).astype(out_ref.dtype)


def run_expert(x, stacks, place, blocks, padded):
    rows, features = x.shape
    hidden = stacks[0].shape[1]
    parts = 2
    half = (blocks // 2, rows, padded)
    out = jax.ShapeDtypeStruct(half, jnp.bfloat16)
    weight = pltpu.VMEM((hidden, features), jnp.bfloat16)
    return pl.pallas_call(
        functools.partial(expert_kernel, blocks, parts),
        in_specs=[smem()] + [hbm()] * 4,
        out_specs=[hbm(), hbm()],
        out_shape=[out, out],
        scratch_shapes=[
            pltpu.VMEM(x.shape, jnp.bfloat16), weight, weight, weight,
            pltpu.VMEM(half, jnp.bfloat16), pltpu.VMEM(half, jnp.bfloat16),
            pltpu.SemaphoreType.DMA((4,)), pltpu.SemaphoreType.DMA((parts, 2)),
        ],
        compiler_params=params(32),
        name="expert",
    )(place, x, *stacks)


def run_combine(high, low, part, rest, dtype):
    return pl.pallas_call(
        combine_kernel,
        in_specs=[vmem()] * 4,
        out_specs=vmem(),
        out_shape=jax.ShapeDtypeStruct(rest.shape, dtype),
        compiler_params=params(),
        name="combine",
    )(high, low, part, rest)


def swap_cores(x):
    return lax.ppermute(x, "core", [(0, 1), (1, 0)])


def shift_y(x, step):
    count = lax.axis_size("y")
    return lax.ppermute(x, "y", [(i, (i + step) % count) for i in range(count)])


def wide(x):
    return x.astype(jnp.float32)


def reduced_over_y(keep, got):
    half = keep.shape[1] // 2
    pair = lambda j: wide(keep[j]) + wide(got[j])
    far = pair(2).astype(keep.dtype)
    from_low = shift_y(far[:half], 1)
    from_high = shift_y(far[half:], -1)
    up = pair(1)
    down = pair(3)
    up = jnp.concatenate([up[:half] + wide(from_low), up[half:]]).astype(keep.dtype)
    down = jnp.concatenate([down[:half], down[half:] + wide(from_high)]).astype(keep.dtype)
    from_low = shift_y(up, 1)
    from_high = shift_y(down, -1)
    return (pair(0) + wide(from_low) + wide(from_high)).astype(keep.dtype)


def merge_stats(first, second):
    peak = jnp.maximum(first[0:1], second[0:1])
    total = first[1:2] * jnp.exp(first[0:1] - peak) + second[1:2] * jnp.exp(second[0:1] - peak)
    return jnp.concatenate([peak, total, first[2:] + second[2:]], axis=0)


def local(
    tokens, moe_gain, route_ids, route_weight, w_gate, w_up, w_down, next_gain, next_gate, next_ids
):
    row_count = lax.axis_size("row")
    y_count = lax.axis_size("y")
    blocks = 2 * y_count
    tok_rows, features = tokens.shape
    tokens, route_ids, route_weight, next_ids = tokens.T, route_ids.T, route_weight.T, next_ids.T
    next_gate = next_gate.T
    w_gate, w_up = jnp.swapaxes(w_gate, 1, 2), jnp.swapaxes(w_up, 1, 2)
    local_experts = w_gate.shape[0]
    chunks = local_experts // 2
    width = features // blocks
    padded = round_up(width, LANES)
    rows = row_count * CAP
    core = lax.axis_index("core")
    position = lax.axis_index(COL)
    moe_gain = moe_gain.reshape(1, -1)
    next_gain = next_gain.reshape(-1, 1)

    own = [core * chunks + k for k in range(chunks)]
    others = [(1 - core) * chunks + k for k in range(chunks)]
    stacks = tuple(
        pltpu.with_memory_space_constraint(stack, pltpu.MemorySpace.HBM) for stack in (w_gate, w_up, w_down)
    )

    def dispatched(k):
        return pl.pallas_call(
            functools.partial(dispatch_kernel, local_experts),
            in_specs=[smem(), vmem(), vmem(), vmem()],
            out_specs=vmem(),
            out_shape=jax.ShapeDtypeStruct((rows, features), jnp.bfloat16),
            compiler_params=params(),
            name="dispatch",
        )(own[k].reshape(1).astype(jnp.int32), tokens, moe_gain, route_ids)

    arrived = []
    for k in range(chunks):
        sent = dispatched(k).reshape(row_count, CAP, features)
        arrived.append(lax.all_to_all(sent, "row", split_axis=0, concat_axis=0, tiled=True))

    table = jax.ShapeDtypeStruct((chunks, tok_rows, 2 * rows), jnp.bfloat16)
    high, low, stats = pl.pallas_call(
        functools.partial(route_kernel, local_experts, chunks),
        in_specs=[smem()] + [vmem()] * 6,
        out_specs=[vmem()] * 3,
        out_shape=[table, table, jax.ShapeDtypeStruct((8, tok_rows), jnp.float32)],
        compiler_params=params(),
        name="route",
    )(
        jnp.stack([core, position]).astype(jnp.int32),
        route_ids, route_weight, tokens, next_gain, next_gate, next_ids,
    )

    def place(expert):
        return jnp.stack([core, lax.axis_index("y"), expert]).astype(jnp.int32)

    mixed = lax.dynamic_slice_in_dim(tokens, position * width, width, 0)
    for k in range(chunks):
        mine = arrived[k]
        theirs = swap_cores(mine)
        keep0, send0 = run_expert(mine.reshape(rows, features), stacks, place(own[k]), blocks, padded)
        got0 = swap_cores(send0)
        keep1, send1 = run_expert(theirs.reshape(rows, features), stacks, place(others[k]), blocks, padded)
        got1 = swap_cores(send1)
        shape = (y_count, row_count, 1, CAP, padded)
        keep = jnp.concatenate([keep0.reshape(shape), keep1.reshape(shape)], axis=2)
        got = jnp.concatenate([got1.reshape(shape), got0.reshape(shape)], axis=2)
        summed = reduced_over_y(keep, got)
        back = lax.all_to_all(summed, "row", split_axis=0, concat_axis=0, tiled=True)
        dtype = jnp.bfloat16 if k == chunks - 1 else jnp.float32
        mixed = run_combine(high[k], low[k], back.reshape(2 * rows, padded), mixed, dtype)

    merged = merge_stats(stats, swap_cores(stats))
    for step in (1, 2):
        moved = lax.ppermute(merged, "y", [(i, i ^ step) for i in range(y_count)])
        merged = merge_stats(merged, moved)
    next_logprob = (merged[2 : 2 + TOP] - merged[0:1] - jnp.log(merged[1:2])).T
    return (mixed.T, next_logprob)


def solution(mesh):
    torus = Mesh(mesh.devices.reshape(4, 2, mesh.shape["row"]), ("y", "core", "row"))

    return jax.shard_map(
        local,
        mesh=torus,
        in_specs=(
            P("row", None),
            P(),
            P("row", None),
            P("row", None),
            P("row", None, COL),
            P("row", None, COL),
            P("row", COL, None),
            P(),
            P(None, COL),
            P("row", None),
        ),
        out_specs=(P("row", COL), P("row", None)),
        check_vma=False,
    )
```

time: 210 us -> 197 us (0.938)
  blocking collectives: 38.1 us -> 0 us
  waiting for transfers between devices: 55 us -> 89.1 us
  starting transfers between devices: 20.5 us -> 39.6 us
  Pallas kernels: 59.5 us -> 41.2 us
  between operations: 14.2 us -> 1.1 us
  local copies, waits for them, and re-layouts: 8.06 us -> 13.4 us
    all_to_all x1 -> x0, blocking collectives: 38.1 us -> none  [local(): lax.all_to_all(sent, 'row', split_axis=0, concat_axis=0, tiled=True)]
    all_to_all x1 -> x2, waiting for transfers between devices: 31.6 us -> 63.7 us  [local(): lax.all_to_all(sent, 'row', split_axis=0, concat_axis=0, tiled=True)]
    ppermute x0 -> x8, waiting for transfers between devices: none -> 15.9 us  [shift_y(): return lax.ppermute(x, 'y', [(i, (i + step) % count) for i in range(count)])]
    ppermute x0 -> x8, starting transfers between devices: none -> 13.5 us  [shift_y(): return lax.ppermute(x, 'y', [(i, (i + step) % count) for i in range(count)])]
    reduce_scatter x2 -> x0, waiting for transfers between devices: 10.9 us -> none  [local(): summed = lax.psum_scatter(both, 'y', scatter_dimension=0, tiled=True)[0]]
    pallas_call x5 -> x6, Pallas kernels: 44.6 us -> 35.4 us  [the longest x4 33.4 us: run_expert(): pl.pallas_call(functools.partial(expert_kernel, blocks, parts), in_specs=...]
    all_to_all x1 -> x2, starting transfers between devices: 3.72 us -> 12.7 us  [local(): lax.all_to_all(sent, 'row', split_axis=0, concat_axis=0, tiled=True)]
    unnamed x16 -> x46, local copies, waits for them, and re-layouts: 3.02 us -> 10.8 us
  transfers between devices with their start and end apart: 14 -> 21, of which waited for: 5 -> 9; matrix products, arithmetic and copies ran while one was open for 8% -> 7% of each run, Pallas kernels for 24% -> 20%
where the time goes in v2:
time: 197 us; the launch traced here: 196 us
  waiting for transfers between devices  89.1 us (45%)
  Pallas kernels  41.2 us (21%)
  starting transfers between devices  39.6 us (20%)
  local copies, waits for them, and re-layouts  13.4 us (7%)
  other arithmetic  12 us (6%)
    all_to_all x2, waiting for transfers between devices, local(): lax.all_to_all(sent, 'row', split_axis=0, concat_axis=0, tiled=True)  63.7 us
    pallas_call x4, Pallas kernels, run_expert(): pl.pallas_call(functools.partial(expert_kernel, blocks, parts), in_specs=...  33.4 us
    ppermute x8, waiting for transfers between devices, shift_y(): return lax.ppermute(x, 'y', [(i, (i + step) % count) for i in range(count)])  15.9 us
    ppermute x8, starting transfers between devices, shift_y(): return lax.ppermute(x, 'y', [(i, (i + step) % count) for i in range(count)])  13.5 us
    all_to_all x2, starting transfers between devices, local(): lax.all_to_all(sent, 'row', split_axis=0, concat_axis=0, tiled=True)  12.7 us
    unnamed x46, local copies, waits for them, and re-layouts  10.8 us
    all_to_all x2, waiting for transfers between devices, local(): lax.all_to_all(summed, 'row', split_axis=0, concat_axis=0, tiled=True)  8.66 us
    all_to_all x2, starting transfers between devices, local(): lax.all_to_all(summed, 'row', split_axis=0, concat_axis=0, tiled=True)  7.3 us
  transfers between devices with their start and end apart: 21, of which 9 were waited for; matrix products, arithmetic and copies ran while one was open for 7% of the time, Pallas kernels for 20%

profile of v2, /device:TPU:0, one launch (start us, length us, event | category | flops | bytes accessed | tf_op | source)
XLA Modules:
  0.0 196.3 jit_solution(7637469412497482073)
XLA Ops:
  0.6 0.7 reshape.103.gain_ref
  1.3 1.4 copy-done
  2.7 0.7 copy-done.18
  3.4 1.1 dispatch.3
  4.5 1.4 copy-done.3
  6.0 8.2 %all-to-all-start.2 = ((bf16[16,24,2880]{2,1,0:T(8,128)(2,1)}), bf16[16,24,2880]{2,1,0:T(8,128)(2,1)}, u32[]{:S(2)}, u32[]{:S(2)}) async-start(bf16[16,24,2880]{2,1,0:T(8,128)(2,1)} %bitcast.117), calls=%async_computation.2 | async-start | bytes 4521984 | tf_op jit(solution)/shard_map/all_to_all | solution.py:290
  14.2 1.1 dispatch.2
  15.3 1.4 copy-done.2
  16.7 31.7 %all-to-all-done.2 = bf16[16,24,2880]{2,1,0:T(8,128)(2,1)} async-done(((bf16[16,24,2880]{2,1,0:T(8,128)(2,1)}), bf16[16,24,2880]{2,1,0:T(8,128)(2,1)}, u32[]{:S(2)}, u32[]{:S(2)}) %all-to-all-start.2) | async-done | bytes 2211872 | tf_op jit(solution)/shard_map/all_to_all | solution.py:290
  48.4 4.6 %all-to-all-start = ((bf16[16,24,2880]{2,1,0:T(8,128)(2,1)}), bf16[16,24,2880]{2,1,0:T(8,128)(2,1)}, u32[]{:S(2)}, u32[]{:S(2)}) async-start(bf16[16,24,2880]{2,1,0:T(8,128)(2,1)} %bitcast.116), calls=%async_computation | async-start | bytes 4521984 | tf_op jit(solution)/shard_map/all_to_all | solution.py:290
  53.1 32.0 %all-to-all-done = bf16[16,24,2880]{2,1,0:T(8,128)(2,1)} async-done(((bf16[16,24,2880]{2,1,0:T(8,128)(2,1)}), bf16[16,24,2880]{2,1,0:T(8,128)(2,1)}, u32[]{:S(2)}, u32[]{:S(2)}) %all-to-all-start) | async-done | bytes 2211872 | tf_op jit(solution)/shard_map/all_to_all | solution.py:290
  85.7 8.3 %expert.6 = (bf16[4,384,384]{2,1,0:T(8,128)(2,1)S(1)}, bf16[4,384,384]{2,1,0:T(8,128)(2,1)}) custom-call(s32[3]{0:T(128)S(1)} %get-tuple-element.46.own_ref, bf16[384,2880]{1,0:T(8,128)(2,1)} %bitcast.37.x_hbm, bf16[4,360,2880]{2,1,0:T(8,128)(2,1)} %bitcast.134, bf16[4,360,2880]{2,1,0:T(8,128)(2,1)} %bitcast.138, bf16[4,360,2880]{2,1,0:T(8,128)(2,1)} %down_hbm.7), custom_call_target="tpu_custom_call" | custom-call | tf_op jit(solution)/shard_map/expert/pallas_call | solution.py:191
  94.6 8.3 %expert.7 = (bf16[4,384,384]{2,1,0:T(8,128)(2,1)S(1)}, bf16[4,384,384]{2,1,0:T(8,128)(2,1)}) custom-call(s32[3]{0:T(128)S(1)} %get-tuple-element.28.own_ref, bf16[384,2880]{1,0:T(8,128)(2,1)} %bitcast.41.x_hbm, bf16[4,360,2880]{2,1,0:T(8,128)(2,1)} %bitcast.135, bf16[4,360,2880]{2,1,0:T(8,128)(2,1)} %bitcast.139, bf16[4,360,2880]{2,1,0:T(8,128)(2,1)} %down_hbm.7), custom_call_target="tpu_custom_call" | custom-call | tf_op jit(solution)/shard_map/expert/pallas_call | solution.py:191
  103.3 3.6 %route.1 = (bf16[2,256,768]{2,1,0:T(8,128)(2,1)S(1)}, bf16[2,256,768]{2,1,0:T(8,128)(2,1)S(1)}, f32[8,256]{1,0:T(8,128)S(1)}) custom-call(s32[2]{0:T(128)S(1)} %pad_add_fusion.own_ref, s32[4,256]{1,0:T(4,128)S(1)} %bitcast.131, f32[4,256]{1,0:T(4,128)S(1)} %bitcast.132, bf16[2880,256]{1,0:T(8,128)(2,1)S(1)} %bitcast.115, ...), custom_call_target="tpu_custom_call" | custom-call | tf_op jit(solution)/shard_map/route/pallas_call | solution.py:293
  107.5 0.8 collective-permute-done.14
  108.4 1.6 collective-permute-start.15
  110.0 8.3 %expert.4 = (bf16[4,384,384]{2,1,0:T(8,128)(2,1)S(1)}, bf16[4,384,384]{2,1,0:T(8,128)(2,1)}) custom-call(s32[3]{0:T(128)S(1)} %get-tuple-element.48.own_ref, bf16[384,2880]{1,0:T(8,128)(2,1)} %bitcast.12.x_hbm, bf16[4,360,2880]{2,1,0:T(8,128)(2,1)} %bitcast.136, bf16[4,360,2880]{2,1,0:T(8,128)(2,1)} %bitcast.140, bf16[4,360,2880]{2,1,0:T(8,128)(2,1)} %down_hbm.7), custom_call_target="tpu_custom_call" | custom-call | tf_op jit(solution)/shard_map/expert/pallas_call | solution.py:191
  118.4 1.0 copy-done.6
  119.4 8.3 %expert.5 = (bf16[4,384,384]{2,1,0:T(8,128)(2,1)S(1)}, bf16[4,384,384]{2,1,0:T(8,128)(2,1)}) custom-call(s32[3]{0:T(128)S(1)} %get-tuple-element.47.own_ref, bf16[384,2880]{1,0:T(8,128)(2,1)} %bitcast.18.x_hbm, bf16[4,360,2880]{2,1,0:T(8,128)(2,1)} %bitcast.137, bf16[4,360,2880]{2,1,0:T(8,128)(2,1)} %bitcast.141, bf16[4,360,2880]{2,1,0:T(8,128)(2,1)} %down_hbm.7), custom_call_target="tpu_custom_call" | custom-call | tf_op jit(solution)/shard_map/expert/pallas_call | solution.py:191
  127.8 1.1 copy-done.9
  129.3 1.2 slice_bitcast_fusion.4
  130.5 2.1 %convert_add_fusion.1 = (f32[1,16,2,24,384]{4,3,2,1,0:T(8,128)S(1)}, f32[1,16,2,24,384]{4,3,2,1,0:T(8,128)S(1)}, bf16[1,16,2,24,384]{4,3,2,1,0:T(8,128)(2,1)S(1)}) fusion(bf16[4,16,1,24,384]{4,3,2,1,0:T(8,128)(2,1)} %bitcast.45, bf16[4,16,1,24,384]{4,3,2,1,0:T(8,128)(2,1)} %bitcast.47, bf16[4,16,1,24,384]{4,3,2,1,0:T(8,128)(2,1)S(1)} %bitcast.118, ...), kind=kLoop, calls=%fused_computation.32 | loop fusion | flops 4718592 | bytes 7667712 | tf_op jit(solution)/shard_map/add | solution.py:232
  132.7 0.8 collective-permute-start.10
  133.5 2.8 %collective-permute-start.12 = (bf16[8,2,24,384]{3,2,1,0:T(8,128)(2,1)S(1)}, bf16[8,2,24,384]{3,2,1,0:T(8,128)(2,1)S(1)}, u32[]{:S(2)}, u32[]{:S(2)}) collective-permute-start(bf16[8,2,24,384]{3,2,1,0:T(8,128)(2,1)S(1)} %get-tuple-element.41), channel_id=1, source_target_pairs={{0,96},{32,0},{64,32},{96,64},{1,97},{33,1},{65,33},{97,65},{2,98}... | collective-permute-start | bytes 884744 | tf_op jit(solution)/shard_map/ppermute | solution.py:223
  136.4 1.9 convert_add_fusion.3
  138.4 3.3 %collective-permute-start.5 = (bf16[8,2,24,384]{3,2,1,0:T(8,128)(2,1)S(1)}, bf16[8,2,24,384]{3,2,1,0:T(8,128)(2,1)S(1)}, u32[]{:S(2)}, u32[]{:S(2)}) collective-permute-start(bf16[8,2,24,384]{3,2,1,0:T(8,128)(2,1)S(1)} %get-tuple-element.43), channel_id=1, source_target_pairs={{0,96},{32,0},{64,32},{96,64},{1,97},{33,1},{65,33},{97,65},{2,98}... | collective-permute-start | bytes 884744 | tf_op jit(solution)/shard_map/ppermute | solution.py:223
  141.8 2.4 %collective-permute-done.10 = bf16[8,2,24,384]{3,2,1,0:T(8,128)(2,1)S(1)} collective-permute-done((bf16[8,2,24,384]{3,2,1,0:T(8,128)(2,1)S(1)}, bf16[8,2,24,384]{3,2,1,0:T(8,128)(2,1)S(1)}, u32[]{:S(2)}, u32[]{:S(2)}) %collective-permute-start.10) | collective-permute-done | bytes 294944 | tf_op jit(solution)/shard_map/ppermute | solution.py:223
  144.5 3.3 %collective-permute-start.13 = (bf16[16,2,24,384]{3,2,1,0:T(8,128)(2,1)S(1)}, bf16[16,2,24,384]{3,2,1,0:T(8,128)(2,1)S(1)}, u32[]{:S(2)}, u32[]{:S(2)}) collective-permute-start(bf16[16,2,24,384]{3,2,1,0:T(8,128)(2,1)S(1)} %pad_maximum_fusion.7), channel_id=1, source_target_pairs={{0,96},{32,0},{64,32},{96,64},{1,97},{33,1},{65,33},{97,65},{2,98}... | collective-permute-start | bytes 1769480 | tf_op jit(solution)/shard_map/ppermute | solution.py:223
  147.8 2.6 %collective-permute-done.3 = bf16[8,2,24,384]{3,2,1,0:T(8,128)(2,1)S(1)} collective-permute-done((bf16[8,2,24,384]{3,2,1,0:T(8,128)(2,1)S(1)}, bf16[8,2,24,384]{3,2,1,0:T(8,128)(2,1)S(1)}, u32[]{:S(2)}, u32[]{:S(2)}) %collective-permute-start.3) | collective-permute-done | bytes 294944 | tf_op jit(solution)/shard_map/ppermute | solution.py:223
  150.5 0.9 pad_maximum_fusion.4
  151.5 0.9 pad_maximum_fusion.5
  152.4 3.2 %collective-permute-start.6 = (bf16[16,2,24,384]{3,2,1,0:T(8,128)(2,1)}, bf16[16,2,24,384]{3,2,1,0:T(8,128)(2,1)}, u32[]{:S(2)}, u32[]{:S(2)}) collective-permute-start(bf16[16,2,24,384]{3,2,1,0:T(8,128)(2,1)} %pad_maximum_fusion.5), channel_id=1, source_target_pairs={{0,96},{32,0},{64,32},{96,64},{1,97},{33,1},{65,33},{97,65},{2,98}... | collective-permute-start | bytes 1769480 | tf_op jit(solution)/shard_map/ppermute | solution.py:223
  155.6 7.4 %collective-permute-done.11 = bf16[16,2,24,384]{3,2,1,0:T(8,128)(2,1)S(1)} collective-permute-done((bf16[16,2,24,384]{3,2,1,0:T(8,128)(2,1)S(1)}, bf16[16,2,24,384]{3,2,1,0:T(8,128)(2,1)S(1)}, u32[]{:S(2)}, u32[]{:S(2)}) %collective-permute-start.11) | collective-permute-done | bytes 589856 | tf_op jit(solution)/shard_map/ppermute | solution.py:223
  163.1 2.2 %fusion.1 = bf16[16,2,24,384]{3,2,1,0:T(8,128)(2,1)} fusion(bf16[16,2,24,384]{3,2,1,0:T(8,128)(2,1)S(1)} %collective-permute-done.13, bf16[16,2,24,384]{3,2,1,0:T(8,128)(2,1)S(1)} %collective-permute-done.11, bf16[4,16,1,24,384]{4,3,2,1,0:T(8,128)(2,1)} %bitcast.45, bf16[4,16,1,24,384]{4,3,2,1,0:T(8,128)(2,1)} %bitcast.47, ...), kind=kLoop, calls=%fused_computation.26 | loop fusion | flops 2949120 | bytes 6488064 | tf_op jit(solution)/shard_map/convert_element_type | solution.py:242
  165.3 3.7 %all-to-all-start.3 = ((bf16[16,2,24,384]{3,2,1,0:T(8,128)(2,1)}), bf16[16,2,24,384]{3,2,1,0:T(8,128)(2,1)S(1)}, u32[]{:S(2)}, u32[]{:S(2)}) async-start(bf16[16,2,24,384]{3,2,1,0:T(8,128)(2,1)} %fusion.1), calls=%async_computation.3 | async-start | bytes 1179648 | tf_op jit(solution)/shard_map/all_to_all | solution.py:320
  169.0 2.5 %collective-permute-start.16 = (f32[8,256]{1,0:T(8,128)S(1)}, f32[8,256]{1,0:T(8,128)S(1)}, u32[]{:S(2)}, u32[]{:S(2)}) collective-permute-start(f32[8,256]{1,0:T(8,128)S(1)} %pad_maximum_fusion.9), channel_id=1, source_target_pairs={{0,64},{32,96},{64,0},{96,32},{1,65},{33,97},{65,1},{97,33},{2,66}... | collective-permute-start | bytes 24584 | tf_op jit(solution)/shard_map/ppermute | solution.py:326
  171.6 3.4 %collective-permute-done.4 = bf16[16,2,24,384]{3,2,1,0:T(8,128)(2,1)} collective-permute-done((bf16[16,2,24,384]{3,2,1,0:T(8,128)(2,1)}, bf16[16,2,24,384]{3,2,1,0:T(8,128)(2,1)}, u32[]{:S(2)}, u32[]{:S(2)}) %collective-permute-start.4) | collective-permute-done | bytes 589856 | tf_op jit(solution)/shard_map/ppermute | solution.py:223
  175.0 2.6 %fusion.3 = bf16[16,2,24,384]{3,2,1,0:T(8,128)(2,1)} fusion(bf16[16,2,24,384]{3,2,1,0:T(8,128)(2,1)} %collective-permute-done.6, bf16[16,2,24,384]{3,2,1,0:T(8,128)(2,1)} %collective-permute-done.4, bf16[4,16,1,24,384]{4,3,2,1,0:T(8,128)(2,1)} %bitcast.22, bf16[4,16,1,24,384]{4,3,2,1,0:T(8,128)(2,1)} %bitcast.24, ...), kind=kLoop, calls=%fused_computation.29 | loop fusion | flops 2949120 | bytes 6488064 | tf_op jit(solution)/shard_map/convert_element_type | solution.py:242
  177.7 2.3 %all-to-all-done.3 = bf16[16,2,24,384]{3,2,1,0:T(8,128)(2,1)S(1)} async-done(((bf16[16,2,24,384]{3,2,1,0:T(8,128)(2,1)}), bf16[16,2,24,384]{3,2,1,0:T(8,128)(2,1)S(1)}, u32[]{:S(2)}, u32[]{:S(2)}) %all-to-all-start.3) | async-done | bytes 589856 | tf_op jit(solution)/shard_map/all_to_all | solution.py:320
  180.0 3.6 %all-to-all-start.1 = ((bf16[16,2,24,384]{3,2,1,0:T(8,128)(2,1)}), bf16[16,2,24,384]{3,2,1,0:T(8,128)(2,1)S(1)}, u32[]{:S(2)}, u32[]{:S(2)}) async-start(bf16[16,2,24,384]{3,2,1,0:T(8,128)(2,1)} %fusion.3), calls=%async_computation.1 | async-start | bytes 1179648 | tf_op jit(solution)/shard_map/all_to_all | solution.py:320
  183.7 0.6 fusion.30
  184.3 1.0 copy-done.13
  185.3 1.0 copy-done.14
  186.3 0.7 combine.2.rest_ref
  187.0 0.7 copy-done.15
  187.7 6.3 %all-to-all-done.1 = bf16[16,2,24,384]{3,2,1,0:T(8,128)(2,1)S(1)} async-done(((bf16[16,2,24,384]{3,2,1,0:T(8,128)(2,1)}), bf16[16,2,24,384]{3,2,1,0:T(8,128)(2,1)S(1)}, u32[]{:S(2)}, u32[]{:S(2)}) %all-to-all-start.1) | async-done | bytes 589856 | tf_op jit(solution)/shard_map/all_to_all | solution.py:320
  194.0 1.0 copy-done.16
  195.0 1.3 combine.3
  (83 shorter events, 3.6 us)
Async XLA Ops:
  1.3 1.4 copy-start
  2.7 0.7 copy-start.18
  4.5 1.5 copy-start.3
  6.0 8.2 %copy-start.1 = (bf16[256,2880]{0,1:T(8,128)(2,1)S(1)}, bf16[256,2880]{0,1:T(8,128)(2,1)}, u32[]{:S(2)}) copy-start(bf16[256,2880]{0,1:T(8,128)(2,1)} %param.10) | copy-start | bytes 4423684
  6.0 8.2 %copy-start.19 = (s32[256,4]{0,1:T(4,128)S(1)}, s32[256,4]{0,1:T(4,128)}, u32[]{:S(2)}) copy-start(s32[256,4]{0,1:T(4,128)} %param.12) | copy-start | bytes 12292
  6.0 42.4 %all-to-all-start.2 = ((bf16[16,24,2880]{2,1,0:T(8,128)(2,1)}), bf16[16,24,2880]{2,1,0:T(8,128)(2,1)}, u32[]{:S(2)}, u32[]{:S(2)}) async-start(bf16[16,24,2880]{2,1,0:T(8,128)(2,1)} %bitcast.117), calls=%async_computation.2 | async-start | bytes 4521984 | tf_op jit(solution)/shard_map/all_to_all | solution.py:290
  15.3 1.4 copy-start.2
  48.4 36.7 %copy-start.22 = (bf16[2880]{0:T(1024)(128)(2,1)S(1)}, bf16[2880]{0:T(1024)(128)(2,1)}, u32[]{:S(2)}) copy-start(bf16[2880]{0:T(1024)(128)(2,1)} %param.17) | copy-start | bytes 17284
  48.4 36.6 %all-to-all-start = ((bf16[16,24,2880]{2,1,0:T(8,128)(2,1)}), bf16[16,24,2880]{2,1,0:T(8,128)(2,1)}, u32[]{:S(2)}, u32[]{:S(2)}) async-start(bf16[16,24,2880]{2,1,0:T(8,128)(2,1)} %bitcast.116), calls=%async_computation | async-start | bytes 4521984 | tf_op jit(solution)/shard_map/all_to_all | solution.py:290
  53.0 41.6 %collective-permute-start.7 = (bf16[16,24,2880]{2,1,0:T(8,128)(2,1)}, bf16[16,24,2880]{2,1,0:T(8,128)(2,1)}, u32[]{:S(2)}, u32[]{:S(2)}) collective-permute-start(bf16[16,24,2880]{2,1,0:T(8,128)(2,1)} %all-to-all-done.2), channel_id=1, source_target_pairs={{0,16},{16,0},{1,17},{17,1},{2,18},{18,2},{3,19},{19,3},{4,20},{20... | collective-permute-start | bytes 6635528 | tf_op jit(solution)/shard_map/ppermute | solution.py:218
  85.0 34.4 %collective-permute-start = (bf16[16,24,2880]{2,1,0:T(8,128)(2,1)}, bf16[16,24,2880]{2,1,0:T(8,128)(2,1)}, u32[]{:S(2)}, u32[]{:S(2)}) collective-permute-start(bf16[16,24,2880]{2,1,0:T(8,128)(2,1)} %all-to-all-done), channel_id=1, source_target_pairs={{0,16},{16,0},{1,17},{17,1},{2,18},{18,2},{3,19},{19,3},{4,20},{20... | collective-permute-start | bytes 6635528 | tf_op jit(solution)/shard_map/ppermute | solution.py:218
  94.0 36.5 %collective-permute-start.9 = (bf16[4,384,384]{2,1,0:T(8,128)(2,1)}, bf16[4,384,384]{2,1,0:T(8,128)(2,1)}, u32[]{:S(2)}, u32[]{:S(2)}) collective-permute-start(bf16[4,384,384]{2,1,0:T(8,128)(2,1)} %get-tuple-element.22), channel_id=1, source_target_pairs={{0,16},{16,0},{1,17},{17,1},{2,18},{18,2},{3,19},{19,3},{4,20},{20... | collective-permute-start | bytes 3538952 | tf_op jit(solution)/shard_map/ppermute | solution.py:218
  94.6 8.7 %copy-start.17 = (bf16[2880,16]{0,1:T(8,128)(2,1)S(1)}, bf16[2880,16]{0,1:T(8,128)(2,1)}, u32[]{:S(2)}) copy-start(bf16[2880,16]{0,1:T(8,128)(2,1)} %param.18) | copy-start | bytes 276484
  94.6 8.7 %copy-start.20 = (f32[256,4]{0,1:T(4,128)S(1)}, f32[256,4]{0,1:T(4,128)}, u32[]{:S(2)}) copy-start(f32[256,4]{0,1:T(4,128)} %param.13) | copy-start | bytes 12292
  94.6 8.7 %copy-start.21 = (s32[256,4]{0,1:T(4,128)S(1)}, s32[256,4]{0,1:T(4,128)}, u32[]{:S(2)}) copy-start(s32[256,4]{0,1:T(4,128)} %param.19) | copy-start | bytes 12292
  102.9 5.4 %copy-start.4 = (bf16[4,384,384]{2,1,0:T(8,128)(2,1)}, bf16[4,384,384]{2,1,0:T(8,128)(2,1)S(1)}, u32[]{:S(2)}) copy-start(bf16[4,384,384]{2,1,0:T(8,128)(2,1)S(1)} %get-tuple-element.20) | copy-start | bytes 3538948
  102.9 27.6 %collective-permute-start.8 = (bf16[4,384,384]{2,1,0:T(8,128)(2,1)}, bf16[4,384,384]{2,1,0:T(8,128)(2,1)}, u32[]{:S(2)}, u32[]{:S(2)}) collective-permute-start(bf16[4,384,384]{2,1,0:T(8,128)(2,1)} %get-tuple-element.21), channel_id=1, source_target_pairs={{0,16},{16,0},{1,17},{17,1},{2,18},{18,2},{3,19},{19,3},{4,20},{20... | collective-permute-start | bytes 3538952 | tf_op jit(solution)/shard_map/ppermute | solution.py:218
  106.9 1.4 collective-permute-start.14
  108.4 22.1 %collective-permute-start.15 = (f32[8,256]{1,0:T(8,128)S(1)}, f32[8,256]{1,0:T(8,128)S(1)}, u32[]{:S(2)}, u32[]{:S(2)}) collective-permute-start(f32[8,256]{1,0:T(8,128)S(1)} %pad_maximum_fusion.8), channel_id=1, source_target_pairs={{0,32},{32,0},{64,96},{96,64},{1,33},{33,1},{65,97},{97,65},{2,34}... | collective-permute-start | bytes 24584 | tf_op jit(solution)/shard_map/ppermute | solution.py:326
  118.3 1.0 copy-start.6
  119.4 16.9 %collective-permute-start.2 = (bf16[4,384,384]{2,1,0:T(8,128)(2,1)}, bf16[4,384,384]{2,1,0:T(8,128)(2,1)}, u32[]{:S(2)}, u32[]{:S(2)}) collective-permute-start(bf16[4,384,384]{2,1,0:T(8,128)(2,1)} %get-tuple-element.18), channel_id=1, source_target_pairs={{0,16},{16,0},{1,17},{17,1},{2,18},{18,2},{3,19},{19,3},{4,20},{20... | collective-permute-start | bytes 3538952 | tf_op jit(solution)/shard_map/ppermute | solution.py:218
  127.8 1.1 copy-start.9
  128.9 7.5 %collective-permute-start.1 = (bf16[4,384,384]{2,1,0:T(8,128)(2,1)}, bf16[4,384,384]{2,1,0:T(8,128)(2,1)}, u32[]{:S(2)}, u32[]{:S(2)}) collective-permute-start(bf16[4,384,384]{2,1,0:T(8,128)(2,1)} %get-tuple-element.17), channel_id=1, source_target_pairs={{0,16},{16,0},{1,17},{17,1},{2,18},{18,2},{3,19},{19,3},{4,20},{20... | collective-permute-start | bytes 3538952 | tf_op jit(solution)/shard_map/ppermute | solution.py:218
  132.6 3.7 %copy-start.7 = (bf16[4,384,384]{2,1,0:T(8,128)(2,1)S(1)}, bf16[4,384,384]{2,1,0:T(8,128)(2,1)}, u32[]{:S(2)}) copy-start(bf16[4,384,384]{2,1,0:T(8,128)(2,1)} %copy-done.6) | copy-start | bytes 3538948
  132.7 3.7 %copy-start.10 = (bf16[4,384,384]{2,1,0:T(8,128)(2,1)S(1)}, bf16[4,384,384]{2,1,0:T(8,128)(2,1)}, u32[]{:S(2)}) copy-start(bf16[4,384,384]{2,1,0:T(8,128)(2,1)} %copy-done.9) | copy-start | bytes 3538948
  132.7 11.4 %collective-permute-start.10 = (bf16[8,2,24,384]{3,2,1,0:T(8,128)(2,1)S(1)}, bf16[8,2,24,384]{3,2,1,0:T(8,128)(2,1)S(1)}, u32[]{:S(2)}, u32[]{:S(2)}) collective-permute-start(bf16[8,2,24,384]{3,2,1,0:T(8,128)(2,1)S(1)} %get-tuple-element.40), channel_id=1, source_target_pairs={{0,32},{32,64},{64,96},{96,0},{1,33},{33,65},{65,97},{97,1},{2,34}... | collective-permute-start | bytes 884744 | tf_op jit(solution)/shard_map/ppermute | solution.py:223
  133.5 10.9 %collective-permute-start.12 = (bf16[8,2,24,384]{3,2,1,0:T(8,128)(2,1)S(1)}, bf16[8,2,24,384]{3,2,1,0:T(8,128)(2,1)S(1)}, u32[]{:S(2)}, u32[]{:S(2)}) collective-permute-start(bf16[8,2,24,384]{3,2,1,0:T(8,128)(2,1)S(1)} %get-tuple-element.41), channel_id=1, source_target_pairs={{0,96},{32,0},{64,32},{96,64},{1,97},{33,1},{65,33},{97,65},{2,98}... | collective-permute-start | bytes 884744 | tf_op jit(solution)/shard_map/ppermute | solution.py:223
  138.3 12.1 %collective-permute-start.3 = (bf16[8,2,24,384]{3,2,1,0:T(8,128)(2,1)S(1)}, bf16[8,2,24,384]{3,2,1,0:T(8,128)(2,1)S(1)}, u32[]{:S(2)}, u32[]{:S(2)}) collective-permute-start(bf16[8,2,24,384]{3,2,1,0:T(8,128)(2,1)S(1)} %get-tuple-element.42), channel_id=1, source_target_pairs={{0,32},{32,64},{64,96},{96,0},{1,33},{33,65},{65,97},{97,1},{2,34}... | collective-permute-start | bytes 884744 | tf_op jit(solution)/shard_map/ppermute | solution.py:223
  138.4 13.0 %collective-permute-start.5 = (bf16[8,2,24,384]{3,2,1,0:T(8,128)(2,1)S(1)}, bf16[8,2,24,384]{3,2,1,0:T(8,128)(2,1)S(1)}, u32[]{:S(2)}, u32[]{:S(2)}) collective-permute-start(bf16[8,2,24,384]{3,2,1,0:T(8,128)(2,1)S(1)} %get-tuple-element.43), channel_id=1, source_target_pairs={{0,96},{32,0},{64,32},{96,64},{1,97},{33,1},{65,33},{97,65},{2,98}... | collective-permute-start | bytes 884744 | tf_op jit(solution)/shard_map/ppermute | solution.py:223
  144.3 18.8 %collective-permute-start.11 = (bf16[16,2,24,384]{3,2,1,0:T(8,128)(2,1)S(1)}, bf16[16,2,24,384]{3,2,1,0:T(8,128)(2,1)S(1)}, u32[]{:S(2)}, u32[]{:S(2)}) collective-permute-start(bf16[16,2,24,384]{3,2,1,0:T(8,128)(2,1)S(1)} %pad_maximum_fusion.6), channel_id=1, source_target_pairs={{0,32},{32,64},{64,96},{96,0},{1,33},{33,65},{65,97},{97,1},{2,34}... | collective-permute-start | bytes 1769480 | tf_op jit(solution)/shard_map/ppermute | solution.py:223
  144.5 18.6 %collective-permute-start.13 = (bf16[16,2,24,384]{3,2,1,0:T(8,128)(2,1)S(1)}, bf16[16,2,24,384]{3,2,1,0:T(8,128)(2,1)S(1)}, u32[]{:S(2)}, u32[]{:S(2)}) collective-permute-start(bf16[16,2,24,384]{3,2,1,0:T(8,128)(2,1)S(1)} %pad_maximum_fusion.7), channel_id=1, source_target_pairs={{0,96},{32,0},{64,32},{96,64},{1,97},{33,1},{65,33},{97,65},{2,98}... | collective-permute-start | bytes 1769480 | tf_op jit(solution)/shard_map/ppermute | solution.py:223
  151.4 11.7 %copy-start.5 = (bf16[4,384,384]{2,1,0:T(8,128)(2,1)S(1)}, bf16[4,384,384]{2,1,0:T(8,128)(2,1)}, u32[]{:S(2)}) copy-start(bf16[4,384,384]{2,1,0:T(8,128)(2,1)} %copy-done.4) | copy-start | bytes 3538948
  151.4 23.6 %collective-permute-start.4 = (bf16[16,2,24,384]{3,2,1,0:T(8,128)(2,1)}, bf16[16,2,24,384]{3,2,1,0:T(8,128)(2,1)}, u32[]{:S(2)}, u32[]{:S(2)}) collective-permute-start(bf16[16,2,24,384]{3,2,1,0:T(8,128)(2,1)} %pad_maximum_fusion.4), channel_id=1, source_target_pairs={{0,32},{32,64},{64,96},{96,0},{1,33},{33,65},{65,97},{97,1},{2,34}... | collective-permute-start | bytes 1769480 | tf_op jit(solution)/shard_map/ppermute | solution.py:223
  152.4 22.6 %collective-permute-start.6 = (bf16[16,2,24,384]{3,2,1,0:T(8,128)(2,1)}, bf16[16,2,24,384]{3,2,1,0:T(8,128)(2,1)}, u32[]{:S(2)}, u32[]{:S(2)}) collective-permute-start(bf16[16,2,24,384]{3,2,1,0:T(8,128)(2,1)} %pad_maximum_fusion.5), channel_id=1, source_target_pairs={{0,96},{32,0},{64,32},{96,64},{1,97},{33,1},{65,33},{97,65},{2,98}... | collective-permute-start | bytes 1769480 | tf_op jit(solution)/shard_map/ppermute | solution.py:223
  165.3 9.7 %copy-start.8 = (bf16[4,384,384]{2,1,0:T(8,128)(2,1)S(1)}, bf16[4,384,384]{2,1,0:T(8,128)(2,1)}, u32[]{:S(2)}) copy-start(bf16[4,384,384]{2,1,0:T(8,128)(2,1)} %copy-done.6) | copy-start | bytes 3538948
  165.3 14.7 %all-to-all-start.3 = ((bf16[16,2,24,384]{3,2,1,0:T(8,128)(2,1)}), bf16[16,2,24,384]{3,2,1,0:T(8,128)(2,1)S(1)}, u32[]{:S(2)}, u32[]{:S(2)}) async-start(bf16[16,2,24,384]{3,2,1,0:T(8,128)(2,1)} %fusion.1), calls=%async_computation.3 | async-start | bytes 1179648 | tf_op jit(solution)/shard_map/all_to_all | solution.py:320
  169.0 14.6 %collective-permute-start.16 = (f32[8,256]{1,0:T(8,128)S(1)}, f32[8,256]{1,0:T(8,128)S(1)}, u32[]{:S(2)}, u32[]{:S(2)}) collective-permute-start(f32[8,256]{1,0:T(8,128)S(1)} %pad_maximum_fusion.9), channel_id=1, source_target_pairs={{0,64},{32,96},{64,0},{96,32},{1,65},{33,97},{65,1},{97,33},{2,66}... | collective-permute-start | bytes 24584 | tf_op jit(solution)/shard_map/ppermute | solution.py:326
  180.0 14.0 %all-to-all-start.1 = ((bf16[16,2,24,384]{3,2,1,0:T(8,128)(2,1)}), bf16[16,2,24,384]{3,2,1,0:T(8,128)(2,1)S(1)}, u32[]{:S(2)}, u32[]{:S(2)}) async-start(bf16[16,2,24,384]{3,2,1,0:T(8,128)(2,1)} %fusion.3), calls=%async_computation.1 | async-start | bytes 1179648 | tf_op jit(solution)/shard_map/all_to_all | solution.py:320
  183.6 10.4 %copy-start.11 = (bf16[256,768]{1,0:T(8,128)(2,1)S(1)}, bf16[256,768]{1,0:T(8,128)(2,1)}, u32[]{:S(2)}) copy-start(bf16[256,768]{1,0:T(8,128)(2,1)} %get-tuple-element.37.low_ref) | copy-start | bytes 1179652
  183.6 10.4 %copy-start.12 = (bf16[256,768]{1,0:T(8,128)(2,1)S(1)}, bf16[256,768]{1,0:T(8,128)(2,1)}, u32[]{:S(2)}) copy-start(bf16[256,768]{1,0:T(8,128)(2,1)} %get-tuple-element.49.high_ref) | copy-start | bytes 1179652
  184.3 1.0 copy-start.13
  185.3 1.0 copy-start.14
  187.0 0.7 copy-start.15
  194.0 1.0 copy-start.16

commit v3 on v2

--- a/solution.py
+++ b/solution.py
@@ -112,57 +112,65 @@
 
 
 def expert_kernel(
-    blocks, parts, own_ref, x_hbm, gate_hbm, up_hbm, down_hbm, keep_hbm, send_hbm,
-    x_ref, gate_ref, up_ref, down_ref, even_ref, odd_ref, in_sems, out_sems,
+    blocks, parts, ready, own_ref, x_hbm, gate_in, up_in, down_in, keep_hbm, send_hbm, *refs
 ):
-    expert = own_ref[2]
-    loads = [
-        pltpu.make_async_copy(source, target, in_sems.at[i])
-        for i, (source, target) in enumerate(
-            (
-                (x_hbm, x_ref),
-                (gate_hbm.at[expert], gate_ref),
-                (up_hbm.at[expert], up_ref),
-                (down_hbm.at[expert], down_ref),
-            )
-        )
-    ]
-    for load in loads:
-        load.start()
-    loads[0].wait()
-    loads[1].wait()
-    x = x_ref[...]
-    gate = dot_nt(x, gate_ref[...])
-    loads[2].wait()
-    up = dot_nt(x, up_ref[...])
-    hidden = (gate / (1.0 + jnp.exp(-gate)) * up).astype(jnp.bfloat16)
-    loads[3].wait()
-    rows, features = x.shape
+    expert, following = own_ref[2], own_ref[3]
+    weights_in = (gate_in, up_in, down_in)
+    if ready:
+        x_ref, even_ref, odd_ref, in_sems, out_sems = refs
+        weights = weights_in
+        loads = []
+        fetches = []
+    else:
+        ahead, refs = refs[:3], refs[3:]
+        x_ref, even_ref, odd_ref, in_sems, out_sems = refs[:5]
+        weights = refs[5:8]
+        loads = [
+            pltpu.make_async_copy(source.at[expert], target, in_sems.at[1 + i])
+            for i, (source, target) in enumerate(zip(weights_in, weights))
+        ]
+        fetches = [
+            pltpu.make_async_copy(source.at[following], target, in_sems.at[4 + i])
+            for i, (source, target) in enumerate(zip(weights_in, ahead))
+        ]
+    first = pltpu.make_async_copy(x_hbm, x_ref, in_sems.at[0])
+    for copy in [first, *loads, *fetches]:
+        copy.start()
+    rows, features = x_ref.shape
     around = blocks // 2
     width = features // blocks
-    rest = jnp.zeros((rows // parts, even_ref.shape[2] - width), even_ref.dtype)
-
-    def stores(part, even_hbm, odd_hbm):
-        here = pl.ds(part * (rows // parts), rows // parts)
-        return [
-            pltpu.make_async_copy(buf.at[:, here], target.at[:, here], out_sems.at[part, i])
-            for i, (buf, target) in enumerate(((even_ref, even_hbm), (odd_ref, odd_hbm)))
-        ]
+    size = rows // parts
+    rest = jnp.zeros((size, even_ref.shape[2] - width), even_ref.dtype)
 
     def each(part, act):
+        here = pl.ds(part * size, size)
+
+        def both(even_hbm, odd_hbm):
+            for i, (buf, target) in enumerate(((even_ref, even_hbm), (odd_ref, odd_hbm))):
+                act(pltpu.make_async_copy(buf.at[:, here], target.at[:, here], out_sems.at[part, i]))
+
         @pl.when(own_ref[0] == 0)
         def _():
-            for copy in stores(part, keep_hbm, send_hbm):
-                act(copy)
+            both(keep_hbm, send_hbm)
 
         @pl.when(own_ref[0] != 0)
         def _():
-            for copy in stores(part, send_hbm, keep_hbm):
-                act(copy)
-
+            both(send_hbm, keep_hbm)
+
+    def weight(i):
+        if loads:
+            loads[i].wait()
+        return weights[i][...]
+
+    first.wait()
+    x = x_ref[...]
+    gate = dot_nt(x, weight(0))
+    up = dot_nt(x, weight(1))
+    hidden = (gate / (1.0 + jnp.exp(-gate)) * up).astype(jnp.bfloat16)
+    down = weight(2)
     for part in range(parts):
-        here = slice(part * (rows // parts), (part + 1) * (rows // parts))
-        out = jnp.dot(hidden[here], down_ref[...], preferred_element_type=jnp.float32)
+        here = slice(part * size, (part + 1) * size)
+        out = jnp.dot(hidden[here], down, preferred_element_type=jnp.float32)
         for b in range(blocks):
             target = (even_ref, odd_ref)[b % 2]
             j = lax.rem(b // 2 - own_ref[1] + around, around)
@@ -171,6 +179,8 @@
         each(part, lambda copy: copy.start())
     for part in range(parts):
         each(part, lambda copy: copy.wait())
+    for copy in fetches:
+        copy.wait()
 
 
 def combine_kernel(high_ref, low_ref, part_ref, rest_ref, out_ref):
@@ -181,26 +191,26 @@
     out_ref[...] = (rest_ref[...].astype(jnp.float32) + summed.T[:width]).astype(out_ref.dtype)
 
 
-def run_expert(x, stacks, place, blocks, padded):
-    rows, features = x.shape
-    hidden = stacks[0].shape[1]
+def run_expert(x, weights, place, blocks, padded):
+    rows, _ = x.shape
+    ready = weights[0].ndim == 2
     parts = 2
     half = (blocks // 2, rows, padded)
     out = jax.ShapeDtypeStruct(half, jnp.bfloat16)
-    weight = pltpu.VMEM((hidden, features), jnp.bfloat16)
-    return pl.pallas_call(
-        functools.partial(expert_kernel, blocks, parts),
-        in_specs=[smem()] + [hbm()] * 4,
-        out_specs=[hbm(), hbm()],
-        out_shape=[out, out],
+    shapes = [] if ready else [pltpu.VMEM(weight.shape[1:], weight.dtype) for weight in weights]
+    results = pl.pallas_call(
+        functools.partial(expert_kernel, blocks, parts, ready),
+        in_specs=[smem(), hbm()] + [vmem() if ready else hbm()] * 3,
+        out_specs=[hbm(), hbm()] + [vmem()] * len(shapes),
+        out_shape=[out, out] + shapes,
         scratch_shapes=[
-            pltpu.VMEM(x.shape, jnp.bfloat16), weight, weight, weight,
-            pltpu.VMEM(half, jnp.bfloat16), pltpu.VMEM(half, jnp.bfloat16),
-            pltpu.SemaphoreType.DMA((4,)), pltpu.SemaphoreType.DMA((parts, 2)),
-        ],
+            pltpu.VMEM(x.shape, jnp.bfloat16), pltpu.VMEM(half, jnp.bfloat16), pltpu.VMEM(half, jnp.bfloat16),
+            pltpu.SemaphoreType.DMA((7,)), pltpu.SemaphoreType.DMA((parts, 2)),
+        ] + shapes,
         compiler_params=params(32),
-        name="expert",
-    )(place, x, *stacks)
+        name="second" if ready else "first",
+    )(place, x, *weights)
+    return results[0], results[1], results[2:]
 
 
 def run_combine(high, low, part, rest, dtype):
@@ -227,19 +237,23 @@
     return x.astype(jnp.float32)
 
 
-def reduced_over_y(keep, got):
-    half = keep.shape[1] // 2
-    pair = lambda j: wide(keep[j]) + wide(got[j])
-    far = pair(2).astype(keep.dtype)
+def reduced_over_y(keep, got, shape):
+    def pair(keep, got, j):
+        parts = [wide(keep[e][j]) + wide(got[1 - e][j]) for e in range(2)]
+        return jnp.concatenate([part.reshape(shape) for part in parts], axis=1)
+
+    half = shape[0] // 2
+    far = pair(keep, got, 2).astype(jnp.bfloat16)
+    keep, got, far = lax.optimization_barrier((keep, got, far))
     from_low = shift_y(far[:half], 1)
     from_high = shift_y(far[half:], -1)
-    up = pair(1)
-    down = pair(3)
-    up = jnp.concatenate([up[:half] + wide(from_low), up[half:]]).astype(keep.dtype)
-    down = jnp.concatenate([down[:half], down[half:] + wide(from_high)]).astype(keep.dtype)
+    up = pair(keep, got, 1)
+    down = pair(keep, got, 3)
+    up = jnp.concatenate([up[:half] + wide(from_low), up[half:]]).astype(jnp.bfloat16)
+    down = jnp.concatenate([down[:half], down[half:] + wide(from_high)]).astype(jnp.bfloat16)
     from_low = shift_y(up, 1)
     from_high = shift_y(down, -1)
-    return (pair(0) + wide(from_low) + wide(from_high)).astype(keep.dtype)
+    return (pair(keep, got, 0) + wide(from_low) + wide(from_high)).astype(jnp.bfloat16)
 
 
 def merge_stats(first, second):
@@ -302,21 +316,19 @@
         route_ids, route_weight, tokens, next_gain, next_gate, next_ids,
     )
 
-    def place(expert):
-        return jnp.stack([core, lax.axis_index("y"), expert]).astype(jnp.int32)
+    def place(k):
+        return jnp.stack([core, lax.axis_index("y"), own[k], others[k]]).astype(jnp.int32)
 
     mixed = lax.dynamic_slice_in_dim(tokens, position * width, width, 0)
     for k in range(chunks):
         mine = arrived[k]
         theirs = swap_cores(mine)
-        keep0, send0 = run_expert(mine.reshape(rows, features), stacks, place(own[k]), blocks, padded)
+        keep0, send0, ahead = run_expert(mine.reshape(rows, features), stacks, place(k), blocks, padded)
         got0 = swap_cores(send0)
-        keep1, send1 = run_expert(theirs.reshape(rows, features), stacks, place(others[k]), blocks, padded)
+        keep1, send1, _ = run_expert(theirs.reshape(rows, features), ahead, place(k), blocks, padded)
         got1 = swap_cores(send1)
-        shape = (y_count, row_count, 1, CAP, padded)
-        keep = jnp.concatenate([keep0.reshape(shape), keep1.reshape(shape)], axis=2)
-        got = jnp.concatenate([got1.reshape(shape), got0.reshape(shape)], axis=2)
-        summed = reduced_over_y(keep, got)
+        keep, got = (keep0, keep1), (got0, got1)
+        summed = reduced_over_y(keep, got, (row_count, 1, CAP, padded))
         back = lax.all_to_all(summed, "row", split_axis=0, concat_axis=0, tiled=True)
         dtype = jnp.bfloat16 if k == chunks - 1 else jnp.float32
         mixed = run_combine(high[k], low[k], back.reshape(2 * rows, padded), mixed, dtype)

time: 197 us -> 204 us (1.036)
  local copies, waits for them, and re-layouts: 13.4 us -> 21.9 us
  Pallas kernels: 41.2 us -> 38.8 us
  other arithmetic: 12 us -> 14.2 us
    unnamed x46 -> x52, local copies, waits for them, and re-layouts: 10.8 us -> 19.6 us
    another operation x6 -> x14, other arithmetic: 0.43 us -> 3.78 us
    pallas_call x4, Pallas kernels: 33.4 us -> 30.9 us  [run_expert(): pl.pallas_call(functools.partial(expert_kernel, blocks, parts, ready), in...]
  transfers between devices with their start and end apart: 21 -> 21, of which waited for: 9 -> 7; matrix products, arithmetic and copies ran while one was open for 7% -> 8% of each run, Pallas kernels for 20% -> 18%
where the time goes in v3:
time: 204 us; the launch traced here: 203 us
  waiting for transfers between devices  87.6 us (43%)
  starting transfers between devices  39.1 us (19%)
  Pallas kernels  38.8 us (19%)
  local copies, waits for them, and re-layouts  21.9 us (11%)
  other arithmetic  14.2 us (7%)
    all_to_all x2, waiting for transfers between devices, local(): lax.all_to_all(sent, 'row', split_axis=0, concat_axis=0, tiled=True)  63.7 us
    pallas_call x4, Pallas kernels, run_expert(): pl.pallas_call(functools.partial(expert_kernel, blocks, parts, ready), in...  30.9 us
    unnamed x52, local copies, waits for them, and re-layouts  19.6 us
    ppermute x8, waiting for transfers between devices, shift_y(): return lax.ppermute(x, 'y', [(i, (i + step) % count) for i in range(count)])  15.1 us
    ppermute x8, starting transfers between devices, shift_y(): return lax.ppermute(x, 'y', [(i, (i + step) % count) for i in range(count)])  13.4 us
    all_to_all x2, starting transfers between devices, local(): lax.all_to_all(sent, 'row', split_axis=0, concat_axis=0, tiled=True)  12.8 us
    all_to_all x2, waiting for transfers between devices, local(): lax.all_to_all(summed, 'row', split_axis=0, concat_axis=0, tiled=True)  8.77 us
    all_to_all x2, starting transfers between devices, local(): lax.all_to_all(summed, 'row', split_axis=0, concat_axis=0, tiled=True)  7.16 us
  transfers between devices with their start and end apart: 21, of which 7 were waited for; matrix products, arithmetic and copies ran while one was open for 8% of the time, Pallas kernels for 18%

profile of v3, /device:TPU:0, one launch (start us, length us, event | category | flops | bytes accessed | tf_op | source)
XLA Modules:
  0.0 202.6 jit_solution(2787802373230515000)
XLA Ops:
  1.3 1.4 copy-done
  3.4 1.1 dispatch.3
  4.5 1.4 copy-done.3
  5.9 8.2 %all-to-all-start.2 = ((bf16[16,24,2880]{2,1,0:T(8,128)(2,1)}), bf16[16,24,2880]{2,1,0:T(8,128)(2,1)}, u32[]{:S(2)}, u32[]{:S(2)}) async-start(bf16[16,24,2880]{2,1,0:T(8,128)(2,1)} %bitcast.89), calls=%async_computation.2 | async-start | bytes 4521984 | tf_op jit(solution)/shard_map/all_to_all | solution.py:304
  14.1 1.1 dispatch.2
  15.3 1.4 copy-done.2
  16.6 31.7 %all-to-all-done.2 = bf16[16,24,2880]{2,1,0:T(8,128)(2,1)} async-done(((bf16[16,24,2880]{2,1,0:T(8,128)(2,1)}), bf16[16,24,2880]{2,1,0:T(8,128)(2,1)}, u32[]{:S(2)}, u32[]{:S(2)}) %all-to-all-start.2) | async-done | bytes 2211872 | tf_op jit(solution)/shard_map/all_to_all | solution.py:304
  48.4 4.6 %all-to-all-start = ((bf16[16,24,2880]{2,1,0:T(8,128)(2,1)}), bf16[16,24,2880]{2,1,0:T(8,128)(2,1)}, u32[]{:S(2)}, u32[]{:S(2)}) async-start(bf16[16,24,2880]{2,1,0:T(8,128)(2,1)} %bitcast.88), calls=%async_computation | async-start | bytes 4521984 | tf_op jit(solution)/shard_map/all_to_all | solution.py:304
  53.1 32.0 %all-to-all-done = bf16[16,24,2880]{2,1,0:T(8,128)(2,1)} async-done(((bf16[16,24,2880]{2,1,0:T(8,128)(2,1)}), bf16[16,24,2880]{2,1,0:T(8,128)(2,1)}, u32[]{:S(2)}, u32[]{:S(2)}) %all-to-all-start) | async-done | bytes 2211872 | tf_op jit(solution)/shard_map/all_to_all | solution.py:304
  85.6 3.6 %route.1 = (bf16[2,256,768]{2,1,0:T(8,128)(2,1)S(1)}, bf16[2,256,768]{2,1,0:T(8,128)(2,1)S(1)}, f32[8,256]{1,0:T(8,128)S(1)}) custom-call(s32[2]{0:T(128)S(1)} %pad_add_fusion.own_ref, s32[4,256]{1,0:T(4,128)S(1)} %bitcast.95, f32[4,256]{1,0:T(4,128)S(1)} %bitcast.96, bf16[2880,256]{1,0:T(8,128)(2,1)S(1)} %bitcast.87, ...), custom_call_target="tpu_custom_call" | custom-call | tf_op jit(solution)/shard_map/route/pallas_call | solution.py:307
  90.1 0.9 copy-done.18
  91.6 8.4 %first.3 = (bf16[4,384,384]{2,1,0:T(8,128)(2,1)S(1)}, bf16[4,384,384]{2,1,0:T(8,128)(2,1)}, bf16[360,2880]{1,0:T(8,128)(2,1)S(1)}, bf16[360,2880]{1,0:T(8,128)(2,1)S(1)}, bf16[360,2880]{1,0:T(8,128)(2,1)S(1)}) custom-call(s32[4]{0:T(128)S(1)} %pad_add_fusion.3.own_ref, bf16[384,2880]{1,0:T(8,128)(2,1)} %bitcast.39.x_hbm, bf16[4,360,2880]{2,1,0:T(8,128)(2,1)} %bitcast.98, ...), custom_call_target="tpu_custom_call" | custom-call | tf_op jit(solution)/shard_map/first/pallas_call | solution.py:201
  100.4 8.4 %first.2 = (bf16[4,384,384]{2,1,0:T(8,128)(2,1)S(1)}, bf16[4,384,384]{2,1,0:T(8,128)(2,1)}, bf16[360,2880]{1,0:T(8,128)(2,1)S(1)}, bf16[360,2880]{1,0:T(8,128)(2,1)S(1)}, bf16[360,2880]{1,0:T(8,128)(2,1)S(1)}) custom-call(s32[4]{0:T(128)S(1)} %pad_add_fusion.1.own_ref, bf16[384,2880]{1,0:T(8,128)(2,1)} %bitcast.13.x_hbm, bf16[4,360,2880]{2,1,0:T(8,128)(2,1)} %bitcast.99, ...), custom_call_target="tpu_custom_call" | custom-call | tf_op jit(solution)/shard_map/first/pallas_call | solution.py:201
  108.8 1.3 copy-done.4
  110.1 1.4 copy-done.6
  111.4 1.3 copy-done.8
  112.8 1.0 copy-done.12
  114.3 7.4 %second.3 = (bf16[4,384,384]{2,1,0:T(8,128)(2,1)S(1)}, bf16[4,384,384]{2,1,0:T(8,128)(2,1)}) custom-call(s32[4]{0:T(128)S(1)} %pad_add_fusion.3.own_ref, bf16[384,2880]{1,0:T(8,128)(2,1)} %bitcast.40.x_hbm, bf16[360,2880]{1,0:T(8,128)(2,1)S(1)} %get-tuple-element.44.gate_in, bf16[360,2880]{1,0:T(8,128)(2,1)S(1)} %get-tuple-element.45.up_in, ...), custom_call_target="tpu_custom_call" | custom-call | tf_op jit(solution)/shard_map/second/pallas_call | solution.py:201
  121.7 1.1 copy-done.14
  122.8 1.6 collective-permute-start.15
  124.5 1.0 slice_bitcast_fusion
  125.5 1.6 copy-done.5
  127.1 1.6 copy-done.7
  128.7 1.6 copy-done.9
  130.3 6.7 %second.2 = (bf16[4,384,384]{2,1,0:T(8,128)(2,1)S(1)}, bf16[4,384,384]{2,1,0:T(8,128)(2,1)S(1)}) custom-call(s32[4]{0:T(128)S(1)} %pad_add_fusion.1.own_ref, bf16[384,2880]{1,0:T(8,128)(2,1)} %bitcast.16.x_hbm, bf16[360,2880]{1,0:T(8,128)(2,1)S(1)} %copy-done.5, bf16[360,2880]{1,0:T(8,128)(2,1)S(1)} %copy-done.7, bf16[360,2880]{1,0:T(8,128)(2,1)S(1)} %copy-done.9), custom_call_target="tpu_custom_call" | custom-call | tf_op jit(solution)/shard_map/second/pallas_call | solution.py:201
  137.3 1.0 add_convert_fusion
  138.4 1.0 add_convert_fusion.2
  139.4 1.0 add_convert_fusion.1
  141.4 2.8 %collective-permute-start.12 = (bf16[8,2,24,384]{3,2,1,0:T(8,128)(2,1)S(1)}, bf16[8,2,24,384]{3,2,1,0:T(8,128)(2,1)S(1)}, u32[]{:S(2)}, u32[]{:S(2)}) collective-permute-start(bf16[8,2,24,384]{3,2,1,0:T(8,128)(2,1)S(1)} %get-tuple-element.77), channel_id=1, source_target_pairs={{0,96},{32,0},{64,32},{96,64},{1,97},{33,1},{65,33},{97,65},{2,98}... | collective-permute-start | bytes 884744 | tf_op jit(solution)/shard_map/ppermute | solution.py:233
  144.5 3.2 %collective-permute-start.5 = (bf16[8,2,24,384]{3,2,1,0:T(8,128)(2,1)S(1)}, bf16[8,2,24,384]{3,2,1,0:T(8,128)(2,1)S(1)}, u32[]{:S(2)}, u32[]{:S(2)}) collective-permute-start(bf16[8,2,24,384]{3,2,1,0:T(8,128)(2,1)S(1)} %get-tuple-element.79), channel_id=1, source_target_pairs={{0,96},{32,0},{64,32},{96,64},{1,97},{33,1},{65,33},{97,65},{2,98}... | collective-permute-start | bytes 884744 | tf_op jit(solution)/shard_map/ppermute | solution.py:233
  147.7 1.8 convert_add_fusion.2
  149.5 2.3 %convert_add_fusion.8 = (f32[1,384,384]{2,1,0:T(8,128)S(1)}, f32[1,384,384]{2,1,0:T(8,128)S(1)}, f32[1,384,384]{2,1,0:T(8,128)S(1)}, f32[1,384,384]{2,1,0:T(8,12...) fusion(bf16[4,384,384]{2,1,0:T(8,128)(2,1)} %collective-permute-done.1, ...), kind=kLoop, calls=%fused_computation.50 | loop fusion | flops 2654208 | bytes 7077888 | tf_op jit(solution)/shard_map/add | solution.py:242
  152.4 3.3 %collective-permute-start.13 = (bf16[16,2,24,384]{3,2,1,0:T(8,128)(2,1)S(1)}, bf16[16,2,24,384]{3,2,1,0:T(8,128)(2,1)S(1)}, u32[]{:S(2)}, u32[]{:S(2)}) collective-permute-start(bf16[16,2,24,384]{3,2,1,0:T(8,128)(2,1)S(1)} %pad_maximum_fusion.9), channel_id=1, source_target_pairs={{0,96},{32,0},{64,32},{96,64},{1,97},{33,1},{65,33},{97,65},{2,98}... | collective-permute-start | bytes 1769480 | tf_op jit(solution)/shard_map/ppermute | solution.py:233
  155.7 2.7 %collective-permute-done.3 = bf16[8,2,24,384]{3,2,1,0:T(8,128)(2,1)S(1)} collective-permute-done((bf16[8,2,24,384]{3,2,1,0:T(8,128)(2,1)S(1)}, bf16[8,2,24,384]{3,2,1,0:T(8,128)(2,1)S(1)}, u32[]{:S(2)}, u32[]{:S(2)}) %collective-permute-start.3) | collective-permute-done | bytes 294944 | tf_op jit(solution)/shard_map/ppermute | solution.py:233
  158.4 0.9 pad_maximum_fusion.5
  160.3 3.2 %collective-permute-start.6 = (bf16[16,2,24,384]{3,2,1,0:T(8,128)(2,1)}, bf16[16,2,24,384]{3,2,1,0:T(8,128)(2,1)}, u32[]{:S(2)}, u32[]{:S(2)}) collective-permute-start(bf16[16,2,24,384]{3,2,1,0:T(8,128)(2,1)} %pad_maximum_fusion.6), channel_id=1, source_target_pairs={{0,96},{32,0},{64,32},{96,64},{1,97},{33,1},{65,33},{97,65},{2,98}... | collective-permute-start | bytes 1769480 | tf_op jit(solution)/shard_map/ppermute | solution.py:233
  163.5 7.5 %collective-permute-done.11 = bf16[16,2,24,384]{3,2,1,0:T(8,128)(2,1)S(1)} collective-permute-done((bf16[16,2,24,384]{3,2,1,0:T(8,128)(2,1)S(1)}, bf16[16,2,24,384]{3,2,1,0:T(8,128)(2,1)S(1)}, u32[]{:S(2)}, u32[]{:S(2)}) %collective-permute-start.11) | collective-permute-done | bytes 589856 | tf_op jit(solution)/shard_map/ppermute | solution.py:233
  171.0 1.1 fusion.3
  172.0 3.6 %all-to-all-start.3 = ((bf16[16,2,24,384]{3,2,1,0:T(8,128)(2,1)}), bf16[16,2,24,384]{3,2,1,0:T(8,128)(2,1)S(1)}, u32[]{:S(2)}, u32[]{:S(2)}) async-start(bf16[16,2,24,384]{3,2,1,0:T(8,128)(2,1)} %fusion.3), calls=%async_computation.3 | async-start | bytes 1179648 | tf_op jit(solution)/shard_map/all_to_all | solution.py:332
  175.7 2.5 %collective-permute-start.16 = (f32[8,256]{1,0:T(8,128)S(1)}, f32[8,256]{1,0:T(8,128)S(1)}, u32[]{:S(2)}, u32[]{:S(2)}) collective-permute-start(f32[8,256]{1,0:T(8,128)S(1)} %pad_maximum_fusion.11), channel_id=1, source_target_pairs={{0,64},{32,96},{64,0},{96,32},{1,65},{33,97},{65,1},{97,33},{2,66}... | collective-permute-start | bytes 24584 | tf_op jit(solution)/shard_map/ppermute | solution.py:338
  178.2 4.9 %collective-permute-done.4 = bf16[16,2,24,384]{3,2,1,0:T(8,128)(2,1)} collective-permute-done((bf16[16,2,24,384]{3,2,1,0:T(8,128)(2,1)}, bf16[16,2,24,384]{3,2,1,0:T(8,128)(2,1)}, u32[]{:S(2)}, u32[]{:S(2)}) %collective-permute-start.4) | collective-permute-done | bytes 589856 | tf_op jit(solution)/shard_map/ppermute | solution.py:233
  183.1 2.4 %fusion.1 = bf16[16,2,24,384]{3,2,1,0:T(8,128)(2,1)} fusion(f32[16,1,24,384]{3,2,1,0:T(8,128)S(1)} %bitcast.118, f32[16,1,24,384]{3,2,1,0:T(8,128)} %bitcast.119, bf16[16,2,24,384]{3,2,1,0:T(8,128)(2,1)} %collective-permute-done.6, bf16[16,2,24,384]{3,2,1,0:T(8,128)(2,1)} %collective-permute-done.4), kind=kLoop, calls=%fused_computation.2 | loop fusion | flops 1769472 | bytes 2949120 | tf_op jit(solution)/shard_map/convert_element_type | solution.py:256
  185.6 1.5 all-to-all-done.3
  187.0 3.6 %all-to-all-start.1 = ((bf16[16,2,24,384]{3,2,1,0:T(8,128)(2,1)}), bf16[16,2,24,384]{3,2,1,0:T(8,128)(2,1)S(1)}, u32[]{:S(2)}, u32[]{:S(2)}) async-start(bf16[16,2,24,384]{3,2,1,0:T(8,128)(2,1)} %fusion.1), calls=%async_computation.1 | async-start | bytes 1179648 | tf_op jit(solution)/shard_map/all_to_all | solution.py:332
  191.3 1.0 copy-done.10
  192.3 1.0 copy-done.11
  194.0 7.3 %all-to-all-done.1 = bf16[16,2,24,384]{3,2,1,0:T(8,128)(2,1)S(1)} async-done(((bf16[16,2,24,384]{3,2,1,0:T(8,128)(2,1)}), bf16[16,2,24,384]{3,2,1,0:T(8,128)(2,1)S(1)}, u32[]{:S(2)}, u32[]{:S(2)}) %all-to-all-start.1) | async-done | bytes 589856 | tf_op jit(solution)/shard_map/all_to_all | solution.py:332
  201.3 1.3 combine.3
  (95 shorter events, 8.8 us)
Async XLA Ops:
  1.3 1.4 copy-start
  2.7 0.7 copy-start.21
  4.5 1.4 copy-start.3
  5.9 8.2 %copy-start.1 = (bf16[256,2880]{0,1:T(8,128)(2,1)S(1)}, bf16[256,2880]{0,1:T(8,128)(2,1)}, u32[]{:S(2)}) copy-start(bf16[256,2880]{0,1:T(8,128)(2,1)} %param.10) | copy-start | bytes 4423684
  5.9 8.2 %copy-start.22 = (s32[256,4]{0,1:T(4,128)S(1)}, s32[256,4]{0,1:T(4,128)}, u32[]{:S(2)}) copy-start(s32[256,4]{0,1:T(4,128)} %param.12) | copy-start | bytes 12292
  5.9 42.4 %all-to-all-start.2 = ((bf16[16,24,2880]{2,1,0:T(8,128)(2,1)}), bf16[16,24,2880]{2,1,0:T(8,128)(2,1)}, u32[]{:S(2)}, u32[]{:S(2)}) async-start(bf16[16,24,2880]{2,1,0:T(8,128)(2,1)} %bitcast.89), calls=%async_computation.2 | async-start | bytes 4521984 | tf_op jit(solution)/shard_map/all_to_all | solution.py:304
  15.2 1.4 copy-start.2
  48.4 36.7 %copy-start.25 = (bf16[2880]{0:T(1024)(128)(2,1)S(1)}, bf16[2880]{0:T(1024)(128)(2,1)}, u32[]{:S(2)}) copy-start(bf16[2880]{0:T(1024)(128)(2,1)} %param.17) | copy-start | bytes 17284
  48.4 37.2 %copy-start.20 = (bf16[2880,16]{0,1:T(8,128)(2,1)S(1)}, bf16[2880,16]{0,1:T(8,128)(2,1)}, u32[]{:S(2)}) copy-start(bf16[2880,16]{0,1:T(8,128)(2,1)} %param.18) | copy-start | bytes 276484
  48.4 37.2 %copy-start.23 = (f32[256,4]{0,1:T(4,128)S(1)}, f32[256,4]{0,1:T(4,128)}, u32[]{:S(2)}) copy-start(f32[256,4]{0,1:T(4,128)} %param.13) | copy-start | bytes 12292
  48.4 37.2 %copy-start.24 = (s32[256,4]{0,1:T(4,128)S(1)}, s32[256,4]{0,1:T(4,128)}, u32[]{:S(2)}) copy-start(s32[256,4]{0,1:T(4,128)} %param.19) | copy-start | bytes 12292
  48.4 36.7 %all-to-all-start = ((bf16[16,24,2880]{2,1,0:T(8,128)(2,1)}), bf16[16,24,2880]{2,1,0:T(8,128)(2,1)}, u32[]{:S(2)}, u32[]{:S(2)}) async-start(bf16[16,24,2880]{2,1,0:T(8,128)(2,1)} %bitcast.88), calls=%async_computation | async-start | bytes 4521984 | tf_op jit(solution)/shard_map/all_to_all | solution.py:304
  53.0 61.3 %collective-permute-start.7 = (bf16[16,24,2880]{2,1,0:T(8,128)(2,1)}, bf16[16,24,2880]{2,1,0:T(8,128)(2,1)}, u32[]{:S(2)}, u32[]{:S(2)}) collective-permute-start(bf16[16,24,2880]{2,1,0:T(8,128)(2,1)} %all-to-all-done.2), channel_id=1, source_target_pairs={{0,16},{16,0},{1,17},{17,1},{2,18},{18,2},{3,19},{19,3},{4,20},{20... | collective-permute-start | bytes 6635528 | tf_op jit(solution)/shard_map/ppermute | solution.py:228
  85.0 40.5 %collective-permute-start = (bf16[16,24,2880]{2,1,0:T(8,128)(2,1)}, bf16[16,24,2880]{2,1,0:T(8,128)(2,1)}, u32[]{:S(2)}, u32[]{:S(2)}) collective-permute-start(bf16[16,24,2880]{2,1,0:T(8,128)(2,1)} %all-to-all-done), channel_id=1, source_target_pairs={{0,16},{16,0},{1,17},{17,1},{2,18},{18,2},{3,19},{19,3},{4,20},{20... | collective-permute-start | bytes 6635528 | tf_op jit(solution)/shard_map/ppermute | solution.py:228
  89.2 0.9 copy-start.16
  90.1 0.9 copy-start.18
  91.0 23.3 %collective-permute-start.14 = (f32[8,256]{1,0:T(8,128)S(1)}, f32[8,256]{1,0:T(8,128)S(1)}, u32[]{:S(2)}, u32[]{:S(2)}) collective-permute-start(f32[8,256]{1,0:T(8,128)S(1)} %get-tuple-element.55), channel_id=1, source_target_pairs={{0,16},{16,0},{1,17},{17,1},{2,18},{18,2},{3,19},{19,3},{4,20},{20... | collective-permute-start | bytes 24584 | tf_op jit(solution)/shard_map/ppermute | solution.py:228
  100.0 37.3 %collective-permute-start.8 = (bf16[4,384,384]{2,1,0:T(8,128)(2,1)}, bf16[4,384,384]{2,1,0:T(8,128)(2,1)}, u32[]{:S(2)}, u32[]{:S(2)}) collective-permute-start(bf16[4,384,384]{2,1,0:T(8,128)(2,1)} %get-tuple-element.48), channel_id=1, source_target_pairs={{0,16},{16,0},{1,17},{17,1},{2,18},{18,2},{3,19},{19,3},{4,20},{20... | collective-permute-start | bytes 3538952 | tf_op jit(solution)/shard_map/ppermute | solution.py:228
  108.8 1.3 copy-start.4
  110.1 1.4 copy-start.6
  111.4 1.3 copy-start.8
  112.8 1.0 copy-start.12
  113.8 24.6 %collective-permute-start.1 = (bf16[4,384,384]{2,1,0:T(8,128)(2,1)}, bf16[4,384,384]{2,1,0:T(8,128)(2,1)}, u32[]{:S(2)}, u32[]{:S(2)}) collective-permute-start(bf16[4,384,384]{2,1,0:T(8,128)(2,1)} %get-tuple-element.36), channel_id=1, source_target_pairs={{0,16},{16,0},{1,17},{17,1},{2,18},{18,2},{3,19},{19,3},{4,20},{20... | collective-permute-start | bytes 3538952 | tf_op jit(solution)/shard_map/ppermute | solution.py:228
  114.3 10.2 %copy-start.17 = (bf16[2,256,768]{2,1,0:T(8,128)(2,1)S(1)}, bf16[2,256,768]{2,1,0:T(8,128)(2,1)}, u32[]{:S(2)}) copy-start(bf16[2,256,768]{2,1,0:T(8,128)(2,1)} %copy-done.16) | copy-start | bytes 2359300
  114.3 10.2 %copy-start.19 = (bf16[2,256,768]{2,1,0:T(8,128)(2,1)S(1)}, bf16[2,256,768]{2,1,0:T(8,128)(2,1)}, u32[]{:S(2)}) copy-start(bf16[2,256,768]{2,1,0:T(8,128)(2,1)} %copy-done.18) | copy-start | bytes 2359300
  121.7 1.1 copy-start.14
  122.8 16.6 %collective-permute-start.9 = (bf16[4,384,384]{2,1,0:T(8,128)(2,1)}, bf16[4,384,384]{2,1,0:T(8,128)(2,1)}, u32[]{:S(2)}, u32[]{:S(2)}) collective-permute-start(bf16[4,384,384]{2,1,0:T(8,128)(2,1)} %get-tuple-element.49), channel_id=1, source_target_pairs={{0,16},{16,0},{1,17},{17,1},{2,18},{18,2},{3,19},{19,3},{4,20},{20... | collective-permute-start | bytes 3538952 | tf_op jit(solution)/shard_map/ppermute | solution.py:228
  122.8 14.5 %collective-permute-start.15 = (f32[8,256]{1,0:T(8,128)S(1)}, f32[8,256]{1,0:T(8,128)S(1)}, u32[]{:S(2)}, u32[]{:S(2)}) collective-permute-start(f32[8,256]{1,0:T(8,128)S(1)} %pad_maximum_fusion.10), channel_id=1, source_target_pairs={{0,32},{32,0},{64,96},{96,64},{1,33},{33,1},{65,97},{97,65},{2,34}... | collective-permute-start | bytes 24584 | tf_op jit(solution)/shard_map/ppermute | solution.py:338
  125.5 1.6 copy-start.5
  127.1 1.6 copy-start.7
  128.7 1.6 copy-start.9
  130.3 7.0 %copy-start.15 = (bf16[4,384,384]{2,1,0:T(8,128)(2,1)S(1)}, bf16[4,384,384]{2,1,0:T(8,128)(2,1)}, u32[]{:S(2)}) copy-start(bf16[4,384,384]{2,1,0:T(8,128)(2,1)} %copy-done.14) | copy-start | bytes 3538948
  137.0 7.1 %collective-permute-start.2 = (bf16[4,384,384]{2,1,0:T(8,128)(2,1)S(1)}, bf16[4,384,384]{2,1,0:T(8,128)(2,1)S(1)}, u32[]{:S(2)}, u32[]{:S(2)}) collective-permute-start(bf16[4,384,384]{2,1,0:T(8,128)(2,1)S(1)} %get-tuple-element.37), channel_id=1, source_target_pairs={{0,16},{16,0},{1,17},{17,1},{2,18},{18,2},{3,19},{19,3},{4,20},{20... | collective-permute-start | bytes 3538952 | tf_op jit(solution)/shard_map/ppermute | solution.py:228
  140.5 3.7 %copy-start.13 = (bf16[4,384,384]{2,1,0:T(8,128)(2,1)S(1)}, bf16[4,384,384]{2,1,0:T(8,128)(2,1)}, u32[]{:S(2)}) copy-start(bf16[4,384,384]{2,1,0:T(8,128)(2,1)} %copy-done.12) | copy-start | bytes 3538948
  140.6 11.4 %collective-permute-start.10 = (bf16[8,2,24,384]{3,2,1,0:T(8,128)(2,1)S(1)}, bf16[8,2,24,384]{3,2,1,0:T(8,128)(2,1)S(1)}, u32[]{:S(2)}, u32[]{:S(2)}) collective-permute-start(bf16[8,2,24,384]{3,2,1,0:T(8,128)(2,1)S(1)} %get-tuple-element.76), channel_id=1, source_target_pairs={{0,32},{32,64},{64,96},{96,0},{1,33},{33,65},{65,97},{97,1},{2,34}... | collective-permute-start | bytes 884744 | tf_op jit(solution)/shard_map/ppermute | solution.py:233
  141.4 10.9 %collective-permute-start.12 = (bf16[8,2,24,384]{3,2,1,0:T(8,128)(2,1)S(1)}, bf16[8,2,24,384]{3,2,1,0:T(8,128)(2,1)S(1)}, u32[]{:S(2)}, u32[]{:S(2)}) collective-permute-start(bf16[8,2,24,384]{3,2,1,0:T(8,128)(2,1)S(1)} %get-tuple-element.77), channel_id=1, source_target_pairs={{0,96},{32,0},{64,32},{96,64},{1,97},{33,1},{65,33},{97,65},{2,98}... | collective-permute-start | bytes 884744 | tf_op jit(solution)/shard_map/ppermute | solution.py:233
  144.4 13.9 %collective-permute-start.3 = (bf16[8,2,24,384]{3,2,1,0:T(8,128)(2,1)S(1)}, bf16[8,2,24,384]{3,2,1,0:T(8,128)(2,1)S(1)}, u32[]{:S(2)}, u32[]{:S(2)}) collective-permute-start(bf16[8,2,24,384]{3,2,1,0:T(8,128)(2,1)S(1)} %get-tuple-element.78), channel_id=1, source_target_pairs={{0,32},{32,64},{64,96},{96,0},{1,33},{33,65},{65,97},{97,1},{2,34}... | collective-permute-start | bytes 884744 | tf_op jit(solution)/shard_map/ppermute | solution.py:233
  144.5 14.8 %collective-permute-start.5 = (bf16[8,2,24,384]{3,2,1,0:T(8,128)(2,1)S(1)}, bf16[8,2,24,384]{3,2,1,0:T(8,128)(2,1)S(1)}, u32[]{:S(2)}, u32[]{:S(2)}) collective-permute-start(bf16[8,2,24,384]{3,2,1,0:T(8,128)(2,1)S(1)} %get-tuple-element.79), channel_id=1, source_target_pairs={{0,96},{32,0},{64,32},{96,64},{1,97},{33,1},{65,33},{97,65},{2,98}... | collective-permute-start | bytes 884744 | tf_op jit(solution)/shard_map/ppermute | solution.py:233
  152.1 18.8 %collective-permute-start.11 = (bf16[16,2,24,384]{3,2,1,0:T(8,128)(2,1)S(1)}, bf16[16,2,24,384]{3,2,1,0:T(8,128)(2,1)S(1)}, u32[]{:S(2)}, u32[]{:S(2)}) collective-permute-start(bf16[16,2,24,384]{3,2,1,0:T(8,128)(2,1)S(1)} %pad_maximum_fusion.8), channel_id=1, source_target_pairs={{0,32},{32,64},{64,96},{96,0},{1,33},{33,65},{65,97},{97,1},{2,34}... | collective-permute-start | bytes 1769480 | tf_op jit(solution)/shard_map/ppermute | solution.py:233
  152.4 18.6 %collective-permute-start.13 = (bf16[16,2,24,384]{3,2,1,0:T(8,128)(2,1)S(1)}, bf16[16,2,24,384]{3,2,1,0:T(8,128)(2,1)S(1)}, u32[]{:S(2)}, u32[]{:S(2)}) collective-permute-start(bf16[16,2,24,384]{3,2,1,0:T(8,128)(2,1)S(1)} %pad_maximum_fusion.9), channel_id=1, source_target_pairs={{0,96},{32,0},{64,32},{96,64},{1,97},{33,1},{65,33},{97,65},{2,98}... | collective-permute-start | bytes 1769480 | tf_op jit(solution)/shard_map/ppermute | solution.py:233
  159.3 23.8 %collective-permute-start.4 = (bf16[16,2,24,384]{3,2,1,0:T(8,128)(2,1)}, bf16[16,2,24,384]{3,2,1,0:T(8,128)(2,1)}, u32[]{:S(2)}, u32[]{:S(2)}) collective-permute-start(bf16[16,2,24,384]{3,2,1,0:T(8,128)(2,1)} %pad_maximum_fusion.5), channel_id=1, source_target_pairs={{0,32},{32,64},{64,96},{96,0},{1,33},{33,65},{65,97},{97,1},{2,34}... | collective-permute-start | bytes 1769480 | tf_op jit(solution)/shard_map/ppermute | solution.py:233
  160.3 22.9 %collective-permute-start.6 = (bf16[16,2,24,384]{3,2,1,0:T(8,128)(2,1)}, bf16[16,2,24,384]{3,2,1,0:T(8,128)(2,1)}, u32[]{:S(2)}, u32[]{:S(2)}) collective-permute-start(bf16[16,2,24,384]{3,2,1,0:T(8,128)(2,1)} %pad_maximum_fusion.6), channel_id=1, source_target_pairs={{0,96},{32,0},{64,32},{96,64},{1,97},{33,1},{65,33},{97,65},{2,98}... | collective-permute-start | bytes 1769480 | tf_op jit(solution)/shard_map/ppermute | solution.py:233
  172.0 15.0 %all-to-all-start.3 = ((bf16[16,2,24,384]{3,2,1,0:T(8,128)(2,1)}), bf16[16,2,24,384]{3,2,1,0:T(8,128)(2,1)S(1)}, u32[]{:S(2)}, u32[]{:S(2)}) async-start(bf16[16,2,24,384]{3,2,1,0:T(8,128)(2,1)} %fusion.3), calls=%async_computation.3 | async-start | bytes 1179648 | tf_op jit(solution)/shard_map/all_to_all | solution.py:332
  175.7 15.0 %collective-permute-start.16 = (f32[8,256]{1,0:T(8,128)S(1)}, f32[8,256]{1,0:T(8,128)S(1)}, u32[]{:S(2)}, u32[]{:S(2)}) collective-permute-start(f32[8,256]{1,0:T(8,128)S(1)} %pad_maximum_fusion.11), channel_id=1, source_target_pairs={{0,64},{32,96},{64,0},{96,32},{1,65},{33,97},{65,1},{97,33},{2,66}... | collective-permute-start | bytes 24584 | tf_op jit(solution)/shard_map/ppermute | solution.py:338
  187.0 14.2 %all-to-all-start.1 = ((bf16[16,2,24,384]{3,2,1,0:T(8,128)(2,1)}), bf16[16,2,24,384]{3,2,1,0:T(8,128)(2,1)S(1)}, u32[]{:S(2)}, u32[]{:S(2)}) async-start(bf16[16,2,24,384]{3,2,1,0:T(8,128)(2,1)} %fusion.1), calls=%async_computation.1 | async-start | bytes 1179648 | tf_op jit(solution)/shard_map/all_to_all | solution.py:332
  191.3 1.0 copy-start.10
  192.3 1.0 copy-start.11

commit v4 on v3

--- a/solution.py
+++ b/solution.py
@@ -12,6 +12,7 @@
 TOP = 4
 CAP = 24
 COL = ("y", "core")
+DISPATCH_PARTS = 2
 LANES = 128
 
 
@@ -25,6 +26,10 @@
 
 def hbm():
     return pl.BlockSpec(memory_space=pltpu.MemorySpace.HBM)
+
+
+def in_hbm(x):
+    return pltpu.with_memory_space_constraint(x, pltpu.MemorySpace.HBM)
 
 
 def smem():
@@ -69,15 +74,39 @@
     )
 
 
-def dispatch_kernel(local_experts, own_ref, tokens_ref, gain_ref, ids_ref, out_ref):
-    tokens = tokens_ref[...]
+def dispatch_kernel(
+    local_experts, parts, own_ref, tokens_hbm, gain_ref, ids_hbm, out_hbm,
+    tokens_ref, ids_ref, out_ref, in_sems, out_sems,
+):
+    loads = [
+        pltpu.make_async_copy(source, target, in_sems.at[i])
+        for i, (source, target) in enumerate(
+            ((ids_hbm, ids_ref), (tokens_hbm, tokens_ref))
+        )
+    ]
+    for copy in loads:
+        copy.start()
     rows = out_ref.shape[0]
     row = lax.broadcasted_iota(jnp.int32, (rows, 1), 0)
+    loads[0].wait()
     hot = named_by(ids_ref[...], (row // CAP) * local_experts + own_ref[0])
     chosen = slot_mask(hot, row % CAP)
+    gain = gain_ref[...].astype(jnp.float32)
+    loads[1].wait()
+    tokens = tokens_ref[...]
     inverse = jnp.sum(chosen * inverse_norm(tokens), axis=1, keepdims=True)
-    picked = dot_nt(chosen.astype(jnp.bfloat16), tokens)
-    out_ref[...] = (picked * inverse * gain_ref[...].astype(jnp.float32)).astype(jnp.bfloat16)
+    chosen = chosen.astype(jnp.bfloat16)
+    size = rows // parts
+    stores = []
+    for part in range(parts):
+        here = slice(part * size, (part + 1) * size)
+        picked = dot_nt(chosen[here], tokens)
+        out_ref[here] = (picked * inverse[here] * gain).astype(jnp.bfloat16)
+        there = pl.ds(part * size, size)
+        stores.append(pltpu.make_async_copy(out_ref.at[there], out_hbm.at[there], out_sems.at[part]))
+        stores[-1].start()
+    for copy in stores:
+        copy.wait()
 
 
 def route_kernel(
@@ -112,29 +141,28 @@
 
 
 def expert_kernel(
-    blocks, parts, ready, own_ref, x_hbm, gate_in, up_in, down_in, keep_hbm, send_hbm, *refs
+    blocks, parts, ready, own_ref, x_ref, gate_in, up_in, down_in, keep_hbm, send_hbm, *refs
 ):
     expert, following = own_ref[2], own_ref[3]
     weights_in = (gate_in, up_in, down_in)
     if ready:
-        x_ref, even_ref, odd_ref, in_sems, out_sems = refs
+        even_ref, odd_ref, out_sems = refs
         weights = weights_in
         loads = []
         fetches = []
     else:
         ahead, refs = refs[:3], refs[3:]
-        x_ref, even_ref, odd_ref, in_sems, out_sems = refs[:5]
-        weights = refs[5:8]
+        even_ref, odd_ref, out_sems, in_sems = refs[:4]
+        weights = refs[4:7]
         loads = [
-            pltpu.make_async_copy(source.at[expert], target, in_sems.at[1 + i])
+            pltpu.make_async_copy(source.at[expert], target, in_sems.at[i])
             for i, (source, target) in enumerate(zip(weights_in, weights))
         ]
         fetches = [
-            pltpu.make_async_copy(source.at[following], target, in_sems.at[4 + i])
+            pltpu.make_async_copy(source.at[following], target, in_sems.at[3 + i])
             for i, (source, target) in enumerate(zip(weights_in, ahead))
         ]
-    first = pltpu.make_async_copy(x_hbm, x_ref, in_sems.at[0])
-    for copy in [first, *loads, *fetches]:
+    for copy in [*loads, *fetches]:
         copy.start()
     rows, features = x_ref.shape
     around = blocks // 2
@@ -162,7 +190,6 @@
             loads[i].wait()
         return weights[i][...]
 
-    first.wait()
     x = x_ref[...]
     gate = dot_nt(x, weight(0))
     up = dot_nt(x, weight(1))
@@ -200,13 +227,13 @@
     shapes = [] if ready else [pltpu.VMEM(weight.shape[1:], weight.dtype) for weight in weights]
     results = pl.pallas_call(
         functools.partial(expert_kernel, blocks, parts, ready),
-        in_specs=[smem(), hbm()] + [vmem() if ready else hbm()] * 3,
+        in_specs=[smem(), vmem()] + [vmem() if ready else hbm()] * 3,
         out_specs=[hbm(), hbm()] + [vmem()] * len(shapes),
         out_shape=[out, out] + shapes,
         scratch_shapes=[
-            pltpu.VMEM(x.shape, jnp.bfloat16), pltpu.VMEM(half, jnp.bfloat16), pltpu.VMEM(half, jnp.bfloat16),
-            pltpu.SemaphoreType.DMA((7,)), pltpu.SemaphoreType.DMA((parts, 2)),
-        ] + shapes,
+            pltpu.VMEM(half, jnp.bfloat16), pltpu.VMEM(half, jnp.bfloat16),
+            pltpu.SemaphoreType.DMA((parts, 2)),
+        ] + ([] if ready else [pltpu.SemaphoreType.DMA((6,))]) + shapes,
         compiler_params=params(32),
         name="second" if ready else "first",
     )(place, x, *weights)
@@ -284,19 +311,22 @@
 
     own = [core * chunks + k for k in range(chunks)]
     others = [(1 - core) * chunks + k for k in range(chunks)]
-    stacks = tuple(
-        pltpu.with_memory_space_constraint(stack, pltpu.MemorySpace.HBM) for stack in (w_gate, w_up, w_down)
-    )
+    stacks = tuple(in_hbm(stack) for stack in (w_gate, w_up, w_down))
 
     def dispatched(k):
         return pl.pallas_call(
-            functools.partial(dispatch_kernel, local_experts),
-            in_specs=[smem(), vmem(), vmem(), vmem()],
-            out_specs=vmem(),
-            out_shape=jax.ShapeDtypeStruct((rows, features), jnp.bfloat16),
+            functools.partial(dispatch_kernel, local_experts, DISPATCH_PARTS),
+            in_specs=[smem(), hbm(), vmem(), hbm()],
+            out_specs=hbm(),
+            out_shape=pltpu.MemorySpace.HBM((rows, features), jnp.bfloat16),
+            scratch_shapes=[
+                pltpu.VMEM(tokens.shape, tokens.dtype),
+                pltpu.VMEM(route_ids.shape, route_ids.dtype), pltpu.VMEM((rows, features), jnp.bfloat16),
+                pltpu.SemaphoreType.DMA((2,)), pltpu.SemaphoreType.DMA((DISPATCH_PARTS,)),
+            ],
             compiler_params=params(),
             name="dispatch",
-        )(own[k].reshape(1).astype(jnp.int32), tokens, moe_gain, route_ids)
+        )(own[k].reshape(1).astype(jnp.int32), in_hbm(tokens), moe_gain, in_hbm(route_ids))
 
     arrived = []
     for k in range(chunks):

time: 204 us -> 203 us (level)
  Pallas kernels: 38.8 us -> 43.6 us
  local copies, waits for them, and re-layouts: 21.9 us -> 17.1 us
    pallas_call x2, Pallas kernels: 2.22 us -> 7.14 us  [dispatched(): pl.pallas_call(functools.partial(dispatch_kernel, local_experts, DISPATCH...]
    unnamed x52 -> x46, local copies, waits for them, and re-layouts: 19.6 us -> 14.8 us
  transfers between devices with their start and end apart: 21 -> 21, of which waited for: 7 -> 7; matrix products, arithmetic and copies ran while one was open for 8% -> 8% of each run, Pallas kernels for 18% -> 19%
where the time goes in v4:
time: 203 us; the launch traced here: 202 us
  waiting for transfers between devices  86.3 us (43%)
  Pallas kernels  43.6 us (21%)
  starting transfers between devices  39.1 us (19%)
  local copies, waits for them, and re-layouts  17.1 us (8%)
  other arithmetic  14.4 us (7%)
    all_to_all x2, waiting for transfers between devices, local(): lax.all_to_all(sent, 'row', split_axis=0, concat_axis=0, tiled=True)  62.6 us
    pallas_call x4, Pallas kernels, run_expert(): pl.pallas_call(functools.partial(expert_kernel, blocks, parts, ready), in...  30.8 us
    unnamed x46, local copies, waits for them, and re-layouts  14.8 us
    ppermute x8, waiting for transfers between devices, shift_y(): return lax.ppermute(x, 'y', [(i, (i + step) % count) for i in range(count)])  14.8 us
    ppermute x8, starting transfers between devices, shift_y(): return lax.ppermute(x, 'y', [(i, (i + step) % count) for i in range(count)])  13.4 us
    all_to_all x2, starting transfers between devices, local(): lax.all_to_all(sent, 'row', split_axis=0, concat_axis=0, tiled=True)  12.6 us
    all_to_all x2, waiting for transfers between devices, local(): lax.all_to_all(summed, 'row', split_axis=0, concat_axis=0, tiled=True)  8.92 us
    all_to_all x2, starting transfers between devices, local(): lax.all_to_all(summed, 'row', split_axis=0, concat_axis=0, tiled=True)  7.3 us
  transfers between devices with their start and end apart: 21, of which 7 were waited for; matrix products, arithmetic and copies ran while one was open for 8% of the time, Pallas kernels for 19%

profile of v4, /device:TPU:0, one launch (start us, length us, event | category | flops | bytes accessed | tf_op | source)
XLA Modules:
  0.0 201.6 jit_solution(5798294136764851026)
XLA Ops:
  1.3 3.6 %dispatch.3 = bf16[384,2880]{1,0:T(8,128)(2,1)} custom-call(s32[1]{0:T(128)} %bitcast.36.own_ref, bf16[2880,256]{1,0:T(8,128)(2,1)} %bitcast.85, bf16[1,2880]{1,0:T(2,128)(2,1)S(1)} %reshape.473.gain_ref, s32[4,256]{1,0:T(4,128)} %bitcast.91), custom_call_target="tpu_custom_call" | custom-call | tf_op jit(solution)/shard_map/dispatch/pallas_call | solution.py:317
  4.9 8.0 %all-to-all-start.2 = ((bf16[16,24,2880]{2,1,0:T(8,128)(2,1)}), bf16[16,24,2880]{2,1,0:T(8,128)(2,1)}, u32[]{:S(2)}, u32[]{:S(2)}) async-start(bf16[16,24,2880]{2,1,0:T(8,128)(2,1)} %bitcast.101), calls=%async_computation.2 | async-start | bytes 4521984 | tf_op jit(solution)/shard_map/all_to_all | solution.py:334
  13.0 3.6 %dispatch.2 = bf16[384,2880]{1,0:T(8,128)(2,1)} custom-call(s32[1]{0:T(128)} %bitcast.10.own_ref, bf16[2880,256]{1,0:T(8,128)(2,1)} %bitcast.86, bf16[1,2880]{1,0:T(2,128)(2,1)S(1)} %reshape.473.gain_ref, s32[4,256]{1,0:T(4,128)} %bitcast.92), custom_call_target="tpu_custom_call" | custom-call | tf_op jit(solution)/shard_map/dispatch/pallas_call | solution.py:317
  16.6 30.7 %all-to-all-done.2 = bf16[16,24,2880]{2,1,0:T(8,128)(2,1)} async-done(((bf16[16,24,2880]{2,1,0:T(8,128)(2,1)}), bf16[16,24,2880]{2,1,0:T(8,128)(2,1)}, u32[]{:S(2)}, u32[]{:S(2)}) %all-to-all-start.2) | async-done | bytes 2211872 | tf_op jit(solution)/shard_map/all_to_all | solution.py:334
  47.2 4.6 %all-to-all-start = ((bf16[16,24,2880]{2,1,0:T(8,128)(2,1)}), bf16[16,24,2880]{2,1,0:T(8,128)(2,1)}, u32[]{:S(2)}, u32[]{:S(2)}) async-start(bf16[16,24,2880]{2,1,0:T(8,128)(2,1)} %bitcast.100), calls=%async_computation | async-start | bytes 4521984 | tf_op jit(solution)/shard_map/all_to_all | solution.py:334
  51.9 32.0 %all-to-all-done = bf16[16,24,2880]{2,1,0:T(8,128)(2,1)} async-done(((bf16[16,24,2880]{2,1,0:T(8,128)(2,1)}), bf16[16,24,2880]{2,1,0:T(8,128)(2,1)}, u32[]{:S(2)}, u32[]{:S(2)}) %all-to-all-start) | async-done | bytes 2211872 | tf_op jit(solution)/shard_map/all_to_all | solution.py:334
  84.5 3.6 %route.1 = (bf16[2,256,768]{2,1,0:T(8,128)(2,1)S(1)}, bf16[2,256,768]{2,1,0:T(8,128)(2,1)S(1)}, f32[8,256]{1,0:T(8,128)S(1)}) custom-call(s32[2]{0:T(128)S(1)} %pad_add_fusion.own_ref, s32[4,256]{1,0:T(4,128)S(1)} %bitcast.93, f32[4,256]{1,0:T(4,128)S(1)} %bitcast.94, bf16[2880,256]{1,0:T(8,128)(2,1)S(1)} %bitcast.87, ...), custom_call_target="tpu_custom_call" | custom-call | tf_op jit(solution)/shard_map/route/pallas_call | solution.py:337
  88.1 0.9 copy-done.13
  89.0 0.9 copy-done.15
  90.5 8.9 %first.3 = (bf16[4,384,384]{2,1,0:T(8,128)(2,1)S(1)}, bf16[4,384,384]{2,1,0:T(8,128)(2,1)}, bf16[360,2880]{1,0:T(8,128)(2,1)S(1)}, bf16[360,2880]{1,0:T(8,128)(2,1)S(1)}, bf16[360,2880]{1,0:T(8,128)(2,1)S(1)}) custom-call(s32[4]{0:T(128)S(1)} %pad_add_fusion.3.own_ref, bf16[384,2880]{1,0:T(8,128)(2,1)} %bitcast.39.x_ref, bf16[4,360,2880]{2,1,0:T(8,128)(2,1)} %bitcast.96, ...), custom_call_target="tpu_custom_call" | custom-call | tf_op jit(solution)/shard_map/first/pallas_call | solution.py:228
  99.7 8.8 %first.2 = (bf16[4,384,384]{2,1,0:T(8,128)(2,1)S(1)}, bf16[4,384,384]{2,1,0:T(8,128)(2,1)}, bf16[360,2880]{1,0:T(8,128)(2,1)S(1)}, bf16[360,2880]{1,0:T(8,128)(2,1)S(1)}, bf16[360,2880]{1,0:T(8,128)(2,1)S(1)}) custom-call(s32[4]{0:T(128)S(1)} %pad_add_fusion.1.own_ref, bf16[384,2880]{1,0:T(8,128)(2,1)} %bitcast.13.x_ref, bf16[4,360,2880]{2,1,0:T(8,128)(2,1)} %bitcast.97, ...), custom_call_target="tpu_custom_call" | custom-call | tf_op jit(solution)/shard_map/first/pallas_call | solution.py:228
  108.6 1.3 copy-done.1
  109.9 1.4 copy-done.3
  111.3 1.3 copy-done.5
  112.6 1.0 copy-done.9
  114.1 6.9 %second.3 = (bf16[4,384,384]{2,1,0:T(8,128)(2,1)S(1)}, bf16[4,384,384]{2,1,0:T(8,128)(2,1)}) custom-call(s32[4]{0:T(128)S(1)} %pad_add_fusion.3.own_ref, bf16[384,2880]{1,0:T(8,128)(2,1)} %bitcast.40.x_ref, bf16[360,2880]{1,0:T(8,128)(2,1)S(1)} %get-tuple-element.44.gate_in, bf16[360,2880]{1,0:T(8,128)(2,1)S(1)} %get-tuple-element.45.up_in, ...), custom_call_target="tpu_custom_call" | custom-call | tf_op jit(solution)/shard_map/second/pallas_call | solution.py:228
  121.0 1.1 copy-done.11
  122.2 1.7 collective-permute-start.15
  123.9 1.0 slice_bitcast_fusion
  124.9 1.6 copy-done.2
  126.5 1.6 copy-done.4
  128.1 1.6 copy-done.6
  129.7 6.2 %second.2 = (bf16[4,384,384]{2,1,0:T(8,128)(2,1)S(1)}, bf16[4,384,384]{2,1,0:T(8,128)(2,1)S(1)}) custom-call(s32[4]{0:T(128)S(1)} %pad_add_fusion.1.own_ref, bf16[384,2880]{1,0:T(8,128)(2,1)} %bitcast.16.x_ref, bf16[360,2880]{1,0:T(8,128)(2,1)S(1)} %copy-done.2, bf16[360,2880]{1,0:T(8,128)(2,1)S(1)} %copy-done.4, bf16[360,2880]{1,0:T(8,128)(2,1)S(1)} %copy-done.6), custom_call_target="tpu_custom_call" | custom-call | tf_op jit(solution)/shard_map/second/pallas_call | solution.py:228
  136.2 1.0 add_convert_fusion
  137.3 1.0 add_convert_fusion.2
  138.3 1.0 add_convert_fusion.1
  139.5 0.7 collective-permute-start.10
  140.3 2.8 %collective-permute-start.12 = (bf16[8,2,24,384]{3,2,1,0:T(8,128)(2,1)S(1)}, bf16[8,2,24,384]{3,2,1,0:T(8,128)(2,1)S(1)}, u32[]{:S(2)}, u32[]{:S(2)}) collective-permute-start(bf16[8,2,24,384]{3,2,1,0:T(8,128)(2,1)S(1)} %get-tuple-element.77), channel_id=1, source_target_pairs={{0,96},{32,0},{64,32},{96,64},{1,97},{33,1},{65,33},{97,65},{2,98}... | collective-permute-start | bytes 884744 | tf_op jit(solution)/shard_map/ppermute | solution.py:260
  143.4 3.2 %collective-permute-start.5 = (bf16[8,2,24,384]{3,2,1,0:T(8,128)(2,1)S(1)}, bf16[8,2,24,384]{3,2,1,0:T(8,128)(2,1)S(1)}, u32[]{:S(2)}, u32[]{:S(2)}) collective-permute-start(bf16[8,2,24,384]{3,2,1,0:T(8,128)(2,1)S(1)} %get-tuple-element.79), channel_id=1, source_target_pairs={{0,96},{32,0},{64,32},{96,64},{1,97},{33,1},{65,33},{97,65},{2,98}... | collective-permute-start | bytes 884744 | tf_op jit(solution)/shard_map/ppermute | solution.py:260
  146.6 1.8 convert_add_fusion.2
  148.4 2.5 %convert_add_fusion.8 = (f32[1,384,384]{2,1,0:T(8,128)S(1)}, f32[1,384,384]{2,1,0:T(8,128)S(1)}, f32[1,384,384]{2,1,0:T(8,128)}, f32[1,384,384]{2,1,0:T(8,128)},...) fusion(bf16[4,384,384]{2,1,0:T(8,128)(2,1)} %collective-permute-done.1, ...), kind=kLoop, calls=%fused_computation.50 | loop fusion | flops 2654208 | bytes 7077888 | tf_op jit(solution)/shard_map/add | solution.py:269
  151.5 3.3 %collective-permute-start.13 = (bf16[16,2,24,384]{3,2,1,0:T(8,128)(2,1)S(1)}, bf16[16,2,24,384]{3,2,1,0:T(8,128)(2,1)S(1)}, u32[]{:S(2)}, u32[]{:S(2)}) collective-permute-start(bf16[16,2,24,384]{3,2,1,0:T(8,128)(2,1)S(1)} %pad_maximum_fusion.9), channel_id=1, source_target_pairs={{0,96},{32,0},{64,32},{96,64},{1,97},{33,1},{65,33},{97,65},{2,98}... | collective-permute-start | bytes 1769480 | tf_op jit(solution)/shard_map/ppermute | solution.py:260
  154.8 2.5 %collective-permute-done.3 = bf16[8,2,24,384]{3,2,1,0:T(8,128)(2,1)S(1)} collective-permute-done((bf16[8,2,24,384]{3,2,1,0:T(8,128)(2,1)S(1)}, bf16[8,2,24,384]{3,2,1,0:T(8,128)(2,1)S(1)}, u32[]{:S(2)}, u32[]{:S(2)}) %collective-permute-start.3) | collective-permute-done | bytes 294944 | tf_op jit(solution)/shard_map/ppermute | solution.py:260
  157.3 0.9 pad_maximum_fusion.5
  158.2 0.9 pad_maximum_fusion.6
  159.1 3.2 %collective-permute-start.6 = (bf16[16,2,24,384]{3,2,1,0:T(8,128)(2,1)}, bf16[16,2,24,384]{3,2,1,0:T(8,128)(2,1)}, u32[]{:S(2)}, u32[]{:S(2)}) collective-permute-start(bf16[16,2,24,384]{3,2,1,0:T(8,128)(2,1)} %pad_maximum_fusion.6), channel_id=1, source_target_pairs={{0,96},{32,0},{64,32},{96,64},{1,97},{33,1},{65,33},{97,65},{2,98}... | collective-permute-start | bytes 1769480 | tf_op jit(solution)/shard_map/ppermute | solution.py:260
  162.4 7.5 %collective-permute-done.11 = bf16[16,2,24,384]{3,2,1,0:T(8,128)(2,1)S(1)} collective-permute-done((bf16[16,2,24,384]{3,2,1,0:T(8,128)(2,1)S(1)}, bf16[16,2,24,384]{3,2,1,0:T(8,128)(2,1)S(1)}, u32[]{:S(2)}, u32[]{:S(2)}) %collective-permute-start.11) | collective-permute-done | bytes 589856 | tf_op jit(solution)/shard_map/ppermute | solution.py:260
  169.9 1.1 fusion.3
  170.9 3.7 %all-to-all-start.3 = ((bf16[16,2,24,384]{3,2,1,0:T(8,128)(2,1)}), bf16[16,2,24,384]{3,2,1,0:T(8,128)(2,1)S(1)}, u32[]{:S(2)}, u32[]{:S(2)}) async-start(bf16[16,2,24,384]{3,2,1,0:T(8,128)(2,1)} %fusion.3), calls=%async_computation.3 | async-start | bytes 1179648 | tf_op jit(solution)/shard_map/all_to_all | solution.py:362
  174.7 2.5 %collective-permute-start.16 = (f32[8,256]{1,0:T(8,128)S(1)}, f32[8,256]{1,0:T(8,128)S(1)}, u32[]{:S(2)}, u32[]{:S(2)}) collective-permute-start(f32[8,256]{1,0:T(8,128)S(1)} %pad_maximum_fusion.11), channel_id=1, source_target_pairs={{0,64},{32,96},{64,0},{96,32},{1,65},{33,97},{65,1},{97,33},{2,66}... | collective-permute-start | bytes 24584 | tf_op jit(solution)/shard_map/ppermute | solution.py:368
  177.2 4.8 %collective-permute-done.4 = bf16[16,2,24,384]{3,2,1,0:T(8,128)(2,1)} collective-permute-done((bf16[16,2,24,384]{3,2,1,0:T(8,128)(2,1)}, bf16[16,2,24,384]{3,2,1,0:T(8,128)(2,1)}, u32[]{:S(2)}, u32[]{:S(2)}) %collective-permute-start.4) | collective-permute-done | bytes 589856 | tf_op jit(solution)/shard_map/ppermute | solution.py:260
  182.0 2.4 %fusion.1 = bf16[16,2,24,384]{3,2,1,0:T(8,128)(2,1)} fusion(f32[16,1,24,384]{3,2,1,0:T(8,128)S(1)} %bitcast.118, f32[16,1,24,384]{3,2,1,0:T(8,128)} %bitcast.119, bf16[16,2,24,384]{3,2,1,0:T(8,128)(2,1)} %collective-permute-done.6, bf16[16,2,24,384]{3,2,1,0:T(8,128)(2,1)} %collective-permute-done.4), kind=kLoop, calls=%fused_computation.2 | loop fusion | flops 1769472 | bytes 2949120 | tf_op jit(solution)/shard_map/convert_element_type | solution.py:283
  184.4 1.6 all-to-all-done.3
  186.1 3.6 %all-to-all-start.1 = ((bf16[16,2,24,384]{3,2,1,0:T(8,128)(2,1)}), bf16[16,2,24,384]{3,2,1,0:T(8,128)(2,1)S(1)}, u32[]{:S(2)}, u32[]{:S(2)}) async-start(bf16[16,2,24,384]{3,2,1,0:T(8,128)(2,1)} %fusion.1), calls=%async_computation.1 | async-start | bytes 1179648 | tf_op jit(solution)/shard_map/all_to_all | solution.py:362
  190.3 1.0 copy-done.7
  191.3 1.0 copy-done.8
  193.0 7.3 %all-to-all-done.1 = bf16[16,2,24,384]{3,2,1,0:T(8,128)(2,1)S(1)} async-done(((bf16[16,2,24,384]{3,2,1,0:T(8,128)(2,1)}), bf16[16,2,24,384]{3,2,1,0:T(8,128)(2,1)S(1)}, u32[]{:S(2)}, u32[]{:S(2)}) %all-to-all-start.1) | async-done | bytes 589856 | tf_op jit(solution)/shard_map/all_to_all | solution.py:362
  200.3 1.3 combine.3
  (89 shorter events, 5.5 us)
Async XLA Ops:
  4.9 42.3 %all-to-all-start.2 = ((bf16[16,24,2880]{2,1,0:T(8,128)(2,1)}), bf16[16,24,2880]{2,1,0:T(8,128)(2,1)}, u32[]{:S(2)}, u32[]{:S(2)}) async-start(bf16[16,24,2880]{2,1,0:T(8,128)(2,1)} %bitcast.101), calls=%async_computation.2 | async-start | bytes 4521984 | tf_op jit(solution)/shard_map/all_to_all | solution.py:334
  47.2 36.7 %copy-start.22 = (bf16[2880]{0:T(1024)(128)(2,1)S(1)}, bf16[2880]{0:T(1024)(128)(2,1)}, u32[]{:S(2)}) copy-start(bf16[2880]{0:T(1024)(128)(2,1)} %param.17) | copy-start | bytes 17284
  47.2 37.2 %copy-start = (bf16[256,2880]{0,1:T(8,128)(2,1)S(1)}, bf16[256,2880]{0,1:T(8,128)(2,1)}, u32[]{:S(2)}) copy-start(bf16[256,2880]{0,1:T(8,128)(2,1)} %param.10) | copy-start | bytes 4423684
  47.2 37.2 %copy-start.17 = (bf16[2880,16]{0,1:T(8,128)(2,1)S(1)}, bf16[2880,16]{0,1:T(8,128)(2,1)}, u32[]{:S(2)}) copy-start(bf16[2880,16]{0,1:T(8,128)(2,1)} %param.18) | copy-start | bytes 276484
  47.2 37.2 %copy-start.18 = (s32[256,4]{0,1:T(4,128)S(1)}, s32[256,4]{0,1:T(4,128)}, u32[]{:S(2)}) copy-start(s32[256,4]{0,1:T(4,128)} %param.12) | copy-start | bytes 12292
  47.2 37.2 %copy-start.19 = (f32[256,4]{0,1:T(4,128)S(1)}, f32[256,4]{0,1:T(4,128)}, u32[]{:S(2)}) copy-start(f32[256,4]{0,1:T(4,128)} %param.13) | copy-start | bytes 12292
  47.2 37.2 %copy-start.20 = (s32[256,4]{0,1:T(4,128)S(1)}, s32[256,4]{0,1:T(4,128)}, u32[]{:S(2)}) copy-start(s32[256,4]{0,1:T(4,128)} %param.19) | copy-start | bytes 12292
  47.2 36.7 %all-to-all-start = ((bf16[16,24,2880]{2,1,0:T(8,128)(2,1)}), bf16[16,24,2880]{2,1,0:T(8,128)(2,1)}, u32[]{:S(2)}, u32[]{:S(2)}) async-start(bf16[16,24,2880]{2,1,0:T(8,128)(2,1)} %bitcast.100), calls=%async_computation | async-start | bytes 4521984 | tf_op jit(solution)/shard_map/all_to_all | solution.py:334
  51.8 62.2 %collective-permute-start.7 = (bf16[16,24,2880]{2,1,0:T(8,128)(2,1)}, bf16[16,24,2880]{2,1,0:T(8,128)(2,1)}, u32[]{:S(2)}, u32[]{:S(2)}) collective-permute-start(bf16[16,24,2880]{2,1,0:T(8,128)(2,1)} %all-to-all-done.2), channel_id=1, source_target_pairs={{0,16},{16,0},{1,17},{17,1},{2,18},{18,2},{3,19},{19,3},{4,20},{20... | collective-permute-start | bytes 6635528 | tf_op jit(solution)/shard_map/ppermute | solution.py:255
  83.9 41.0 %collective-permute-start = (bf16[16,24,2880]{2,1,0:T(8,128)(2,1)}, bf16[16,24,2880]{2,1,0:T(8,128)(2,1)}, u32[]{:S(2)}, u32[]{:S(2)}) collective-permute-start(bf16[16,24,2880]{2,1,0:T(8,128)(2,1)} %all-to-all-done), channel_id=1, source_target_pairs={{0,16},{16,0},{1,17},{17,1},{2,18},{18,2},{3,19},{19,3},{4,20},{20... | collective-permute-start | bytes 6635528 | tf_op jit(solution)/shard_map/ppermute | solution.py:255
  88.1 0.9 copy-start.13
  89.0 0.9 copy-start.15
  89.9 24.1 %collective-permute-start.14 = (f32[8,256]{1,0:T(8,128)S(1)}, f32[8,256]{1,0:T(8,128)S(1)}, u32[]{:S(2)}, u32[]{:S(2)}) collective-permute-start(f32[8,256]{1,0:T(8,128)S(1)} %get-tuple-element.55), channel_id=1, source_target_pairs={{0,16},{16,0},{1,17},{17,1},{2,18},{18,2},{3,19},{19,3},{4,20},{20... | collective-permute-start | bytes 24584 | tf_op jit(solution)/shard_map/ppermute | solution.py:255
  99.4 36.8 %collective-permute-start.8 = (bf16[4,384,384]{2,1,0:T(8,128)(2,1)}, bf16[4,384,384]{2,1,0:T(8,128)(2,1)}, u32[]{:S(2)}, u32[]{:S(2)}) collective-permute-start(bf16[4,384,384]{2,1,0:T(8,128)(2,1)} %get-tuple-element.48), channel_id=1, source_target_pairs={{0,16},{16,0},{1,17},{17,1},{2,18},{18,2},{3,19},{19,3},{4,20},{20... | collective-permute-start | bytes 3538952 | tf_op jit(solution)/shard_map/ppermute | solution.py:255
  108.5 1.3 copy-start.1
  109.9 1.4 copy-start.3
  111.3 1.3 copy-start.5
  112.6 1.0 copy-start.9
  113.6 23.7 %collective-permute-start.1 = (bf16[4,384,384]{2,1,0:T(8,128)(2,1)}, bf16[4,384,384]{2,1,0:T(8,128)(2,1)}, u32[]{:S(2)}, u32[]{:S(2)}) collective-permute-start(bf16[4,384,384]{2,1,0:T(8,128)(2,1)} %get-tuple-element.36), channel_id=1, source_target_pairs={{0,16},{16,0},{1,17},{17,1},{2,18},{18,2},{3,19},{19,3},{4,20},{20... | collective-permute-start | bytes 3538952 | tf_op jit(solution)/shard_map/ppermute | solution.py:255
  114.1 9.8 %copy-start.14 = (bf16[2,256,768]{2,1,0:T(8,128)(2,1)S(1)}, bf16[2,256,768]{2,1,0:T(8,128)(2,1)}, u32[]{:S(2)}) copy-start(bf16[2,256,768]{2,1,0:T(8,128)(2,1)} %copy-done.13) | copy-start | bytes 2359300
  114.1 9.8 %copy-start.16 = (bf16[2,256,768]{2,1,0:T(8,128)(2,1)S(1)}, bf16[2,256,768]{2,1,0:T(8,128)(2,1)}, u32[]{:S(2)}) copy-start(bf16[2,256,768]{2,1,0:T(8,128)(2,1)} %copy-done.15) | copy-start | bytes 2359300
  121.0 1.1 copy-start.11
  122.1 16.2 %collective-permute-start.9 = (bf16[4,384,384]{2,1,0:T(8,128)(2,1)}, bf16[4,384,384]{2,1,0:T(8,128)(2,1)}, u32[]{:S(2)}, u32[]{:S(2)}) collective-permute-start(bf16[4,384,384]{2,1,0:T(8,128)(2,1)} %get-tuple-element.49), channel_id=1, source_target_pairs={{0,16},{16,0},{1,17},{17,1},{2,18},{18,2},{3,19},{19,3},{4,20},{20... | collective-permute-start | bytes 3538952 | tf_op jit(solution)/shard_map/ppermute | solution.py:255
  122.2 14.0 %collective-permute-start.15 = (f32[8,256]{1,0:T(8,128)S(1)}, f32[8,256]{1,0:T(8,128)S(1)}, u32[]{:S(2)}, u32[]{:S(2)}) collective-permute-start(f32[8,256]{1,0:T(8,128)S(1)} %pad_maximum_fusion.10), channel_id=1, source_target_pairs={{0,32},{32,0},{64,96},{96,64},{1,33},{33,1},{65,97},{97,65},{2,34}... | collective-permute-start | bytes 24584 | tf_op jit(solution)/shard_map/ppermute | solution.py:368
  124.9 1.6 copy-start.2
  126.5 1.6 copy-start.4
  128.1 1.6 copy-start.6
  129.7 6.5 %copy-start.12 = (bf16[4,384,384]{2,1,0:T(8,128)(2,1)S(1)}, bf16[4,384,384]{2,1,0:T(8,128)(2,1)}, u32[]{:S(2)}) copy-start(bf16[4,384,384]{2,1,0:T(8,128)(2,1)} %copy-done.11) | copy-start | bytes 3538948
  135.9 7.1 %collective-permute-start.2 = (bf16[4,384,384]{2,1,0:T(8,128)(2,1)S(1)}, bf16[4,384,384]{2,1,0:T(8,128)(2,1)S(1)}, u32[]{:S(2)}, u32[]{:S(2)}) collective-permute-start(bf16[4,384,384]{2,1,0:T(8,128)(2,1)S(1)} %get-tuple-element.37), channel_id=1, source_target_pairs={{0,16},{16,0},{1,17},{17,1},{2,18},{18,2},{3,19},{19,3},{4,20},{20... | collective-permute-start | bytes 3538952 | tf_op jit(solution)/shard_map/ppermute | solution.py:255
  139.4 3.7 %copy-start.10 = (bf16[4,384,384]{2,1,0:T(8,128)(2,1)S(1)}, bf16[4,384,384]{2,1,0:T(8,128)(2,1)}, u32[]{:S(2)}) copy-start(bf16[4,384,384]{2,1,0:T(8,128)(2,1)} %copy-done.9) | copy-start | bytes 3538948
  139.5 11.6 %collective-permute-start.10 = (bf16[8,2,24,384]{3,2,1,0:T(8,128)(2,1)S(1)}, bf16[8,2,24,384]{3,2,1,0:T(8,128)(2,1)S(1)}, u32[]{:S(2)}, u32[]{:S(2)}) collective-permute-start(bf16[8,2,24,384]{3,2,1,0:T(8,128)(2,1)S(1)} %get-tuple-element.76), channel_id=1, source_target_pairs={{0,32},{32,64},{64,96},{96,0},{1,33},{33,65},{65,97},{97,1},{2,34}... | collective-permute-start | bytes 884744 | tf_op jit(solution)/shard_map/ppermute | solution.py:260
  140.3 11.1 %collective-permute-start.12 = (bf16[8,2,24,384]{3,2,1,0:T(8,128)(2,1)S(1)}, bf16[8,2,24,384]{3,2,1,0:T(8,128)(2,1)S(1)}, u32[]{:S(2)}, u32[]{:S(2)}) collective-permute-start(bf16[8,2,24,384]{3,2,1,0:T(8,128)(2,1)S(1)} %get-tuple-element.77), channel_id=1, source_target_pairs={{0,96},{32,0},{64,32},{96,64},{1,97},{33,1},{65,33},{97,65},{2,98}... | collective-permute-start | bytes 884744 | tf_op jit(solution)/shard_map/ppermute | solution.py:260
  143.3 13.9 %collective-permute-start.3 = (bf16[8,2,24,384]{3,2,1,0:T(8,128)(2,1)S(1)}, bf16[8,2,24,384]{3,2,1,0:T(8,128)(2,1)S(1)}, u32[]{:S(2)}, u32[]{:S(2)}) collective-permute-start(bf16[8,2,24,384]{3,2,1,0:T(8,128)(2,1)S(1)} %get-tuple-element.78), channel_id=1, source_target_pairs={{0,32},{32,64},{64,96},{96,0},{1,33},{33,65},{65,97},{97,1},{2,34}... | collective-permute-start | bytes 884744 | tf_op jit(solution)/shard_map/ppermute | solution.py:260
  143.4 14.8 %collective-permute-start.5 = (bf16[8,2,24,384]{3,2,1,0:T(8,128)(2,1)S(1)}, bf16[8,2,24,384]{3,2,1,0:T(8,128)(2,1)S(1)}, u32[]{:S(2)}, u32[]{:S(2)}) collective-permute-start(bf16[8,2,24,384]{3,2,1,0:T(8,128)(2,1)S(1)} %get-tuple-element.79), channel_id=1, source_target_pairs={{0,96},{32,0},{64,32},{96,64},{1,97},{33,1},{65,33},{97,65},{2,98}... | collective-permute-start | bytes 884744 | tf_op jit(solution)/shard_map/ppermute | solution.py:260
  151.2 18.6 %collective-permute-start.11 = (bf16[16,2,24,384]{3,2,1,0:T(8,128)(2,1)S(1)}, bf16[16,2,24,384]{3,2,1,0:T(8,128)(2,1)S(1)}, u32[]{:S(2)}, u32[]{:S(2)}) collective-permute-start(bf16[16,2,24,384]{3,2,1,0:T(8,128)(2,1)S(1)} %pad_maximum_fusion.8), channel_id=1, source_target_pairs={{0,32},{32,64},{64,96},{96,0},{1,33},{33,65},{65,97},{97,1},{2,34}... | collective-permute-start | bytes 1769480 | tf_op jit(solution)/shard_map/ppermute | solution.py:260
  151.5 18.4 %collective-permute-start.13 = (bf16[16,2,24,384]{3,2,1,0:T(8,128)(2,1)S(1)}, bf16[16,2,24,384]{3,2,1,0:T(8,128)(2,1)S(1)}, u32[]{:S(2)}, u32[]{:S(2)}) collective-permute-start(bf16[16,2,24,384]{3,2,1,0:T(8,128)(2,1)S(1)} %pad_maximum_fusion.9), channel_id=1, source_target_pairs={{0,96},{32,0},{64,32},{96,64},{1,97},{33,1},{65,33},{97,65},{2,98}... | collective-permute-start | bytes 1769480 | tf_op jit(solution)/shard_map/ppermute | solution.py:260
  158.2 23.8 %collective-permute-start.4 = (bf16[16,2,24,384]{3,2,1,0:T(8,128)(2,1)}, bf16[16,2,24,384]{3,2,1,0:T(8,128)(2,1)}, u32[]{:S(2)}, u32[]{:S(2)}) collective-permute-start(bf16[16,2,24,384]{3,2,1,0:T(8,128)(2,1)} %pad_maximum_fusion.5), channel_id=1, source_target_pairs={{0,32},{32,64},{64,96},{96,0},{1,33},{33,65},{65,97},{97,1},{2,34}... | collective-permute-start | bytes 1769480 | tf_op jit(solution)/shard_map/ppermute | solution.py:260
  159.1 22.9 %collective-permute-start.6 = (bf16[16,2,24,384]{3,2,1,0:T(8,128)(2,1)}, bf16[16,2,24,384]{3,2,1,0:T(8,128)(2,1)}, u32[]{:S(2)}, u32[]{:S(2)}) collective-permute-start(bf16[16,2,24,384]{3,2,1,0:T(8,128)(2,1)} %pad_maximum_fusion.6), channel_id=1, source_target_pairs={{0,96},{32,0},{64,32},{96,64},{1,97},{33,1},{65,33},{97,65},{2,98}... | collective-permute-start | bytes 1769480 | tf_op jit(solution)/shard_map/ppermute | solution.py:260
  170.9 11.1 %copy-start.21 = (f32[1,384,384]{2,1,0:T(8,128)S(1)}, f32[1,384,384]{2,1,0:T(8,128)}, u32[]{:S(2)}) copy-start(f32[1,384,384]{2,1,0:T(8,128)} %get-tuple-element.71) | copy-start | bytes 1769476
  170.9 15.1 %all-to-all-start.3 = ((bf16[16,2,24,384]{3,2,1,0:T(8,128)(2,1)}), bf16[16,2,24,384]{3,2,1,0:T(8,128)(2,1)S(1)}, u32[]{:S(2)}, u32[]{:S(2)}) async-start(bf16[16,2,24,384]{3,2,1,0:T(8,128)(2,1)} %fusion.3), calls=%async_computation.3 | async-start | bytes 1179648 | tf_op jit(solution)/shard_map/all_to_all | solution.py:362
  174.7 15.0 %collective-permute-start.16 = (f32[8,256]{1,0:T(8,128)S(1)}, f32[8,256]{1,0:T(8,128)S(1)}, u32[]{:S(2)}, u32[]{:S(2)}) collective-permute-start(f32[8,256]{1,0:T(8,128)S(1)} %pad_maximum_fusion.11), channel_id=1, source_target_pairs={{0,64},{32,96},{64,0},{96,32},{1,65},{33,97},{65,1},{97,33},{2,66}... | collective-permute-start | bytes 24584 | tf_op jit(solution)/shard_map/ppermute | solution.py:368
  186.1 14.2 %all-to-all-start.1 = ((bf16[16,2,24,384]{3,2,1,0:T(8,128)(2,1)}), bf16[16,2,24,384]{3,2,1,0:T(8,128)(2,1)S(1)}, u32[]{:S(2)}, u32[]{:S(2)}) async-start(bf16[16,2,24,384]{3,2,1,0:T(8,128)(2,1)} %fusion.1), calls=%async_computation.1 | async-start | bytes 1179648 | tf_op jit(solution)/shard_map/all_to_all | solution.py:362
  190.3 1.0 copy-start.7
  191.3 1.0 copy-start.8

commit v5 on v4

--- a/solution.py
+++ b/solution.py
@@ -75,7 +75,7 @@
 
 
 def dispatch_kernel(
-    local_experts, parts, own_ref, tokens_hbm, gain_ref, ids_hbm, out_hbm,
+    local_experts, parts, split, own_ref, tokens_hbm, gain_ref, ids_hbm, out_hbm,
     tokens_ref, ids_ref, out_ref, in_sems, out_sems,
 ):
     loads = [
@@ -96,12 +96,32 @@
     tokens = tokens_ref[...]
     inverse = jnp.sum(chosen * inverse_norm(tokens), axis=1, keepdims=True)
     chosen = chosen.astype(jnp.bfloat16)
+    if split:
+        held = out_ref.shape[1]
+
+        def emit(start, count):
+            picked = dot_nt(chosen, tokens_ref[start : start + count])
+            scaled = picked * inverse * gain[:, start : start + count]
+            out_ref[:, :count] = scaled.astype(jnp.bfloat16)
+            if count < held:
+                out_ref[:, count:] = jnp.zeros((rows, held - count), jnp.bfloat16)
+
+        @pl.when(own_ref[1] == 0)
+        def _():
+            emit(0, held)
+
+        @pl.when(own_ref[1] != 0)
+        def _():
+            emit(held, tokens_ref.shape[0] - held)
+
+        parts = 1
     size = rows // parts
     stores = []
     for part in range(parts):
         here = slice(part * size, (part + 1) * size)
-        picked = dot_nt(chosen[here], tokens)
-        out_ref[here] = (picked * inverse[here] * gain).astype(jnp.bfloat16)
+        if not split:
+            picked = dot_nt(chosen[here], tokens)
+            out_ref[here] = (picked * inverse[here] * gain).astype(jnp.bfloat16)
         there = pl.ds(part * size, size)
         stores.append(pltpu.make_async_copy(out_ref.at[there], out_hbm.at[there], out_sems.at[part]))
         stores[-1].start()
@@ -141,15 +161,18 @@
 
 
 def expert_kernel(
-    blocks, parts, ready, own_ref, x_ref, gate_in, up_in, down_in, keep_hbm, send_hbm, *refs
+    blocks, parts, ready, pieces, own_ref, *refs
 ):
     expert, following = own_ref[2], own_ref[3]
-    weights_in = (gate_in, up_in, down_in)
+    given, refs = refs[:pieces], refs[pieces:]
+    x_ref = given[0]
+    if pieces > 1:
+        x_ref, refs = refs[-1], refs[:-1]
+    weights_in, keep_hbm, send_hbm, refs = refs[:3], refs[3], refs[4], refs[5:]
+    loads, fetches = [], []
     if ready:
         even_ref, odd_ref, out_sems = refs
         weights = weights_in
-        loads = []
-        fetches = []
     else:
         ahead, refs = refs[:3], refs[3:]
         even_ref, odd_ref, out_sems, in_sems = refs[:4]
@@ -164,6 +187,25 @@
         ]
     for copy in [*loads, *fetches]:
         copy.start()
+    if pieces > 1:
+        mine, low, high = given
+        held = mine.shape[1]
+        left = x_ref.shape[1] - held
+        middle = low.shape[0]
+        odd = lax.rem(own_ref[1], 2)
+
+        @pl.when(odd == 0)
+        def _():
+            x_ref[:, :held] = mine[...]
+            x_ref[:middle, held:] = low[:, :left]
+            x_ref[middle:, held:] = high[:, :left]
+
+        @pl.when(odd != 0)
+        def _():
+            x_ref[:, held:] = mine[:, :left]
+            x_ref[:middle, :held] = low[...]
+            x_ref[middle:, :held] = high[...]
+
     rows, features = x_ref.shape
     around = blocks // 2
     width = features // blocks
@@ -219,24 +261,26 @@
 
 
 def run_expert(x, weights, place, blocks, padded):
-    rows, _ = x.shape
+    rows = x[0].shape[0]
+    features = weights[0].shape[-1]
     ready = weights[0].ndim == 2
     parts = 2
     half = (blocks // 2, rows, padded)
     out = jax.ShapeDtypeStruct(half, jnp.bfloat16)
     shapes = [] if ready else [pltpu.VMEM(weight.shape[1:], weight.dtype) for weight in weights]
     results = pl.pallas_call(
-        functools.partial(expert_kernel, blocks, parts, ready),
-        in_specs=[smem(), vmem()] + [vmem() if ready else hbm()] * 3,
+        functools.partial(expert_kernel, blocks, parts, ready, len(x)),
+        in_specs=[smem()] + [vmem()] * len(x) + [vmem() if ready else hbm()] * 3,
         out_specs=[hbm(), hbm()] + [vmem()] * len(shapes),
         out_shape=[out, out] + shapes,
         scratch_shapes=[
             pltpu.VMEM(half, jnp.bfloat16), pltpu.VMEM(half, jnp.bfloat16),
             pltpu.SemaphoreType.DMA((parts, 2)),
-        ] + ([] if ready else [pltpu.SemaphoreType.DMA((6,))]) + shapes,
+        ] + ([] if ready else [pltpu.SemaphoreType.DMA((6,))]) + shapes
+        + ([pltpu.VMEM((rows, features), jnp.bfloat16)] if len(x) > 1 else []),
         compiler_params=params(32),
         name="second" if ready else "first",
-    )(place, x, *weights)
+    )(place, *x, *weights)
     return results[0], results[1], results[2:]
 
 
@@ -313,24 +357,28 @@
     others = [(1 - core) * chunks + k for k in range(chunks)]
     stacks = tuple(in_hbm(stack) for stack in (w_gate, w_up, w_down))
 
+    held = round_up(features // 2, 2 * LANES)
+    odd = lax.axis_index("y") % 2
+
     def dispatched(k):
+        share = held if k == 0 else features
         return pl.pallas_call(
-            functools.partial(dispatch_kernel, local_experts, DISPATCH_PARTS),
+            functools.partial(dispatch_kernel, local_experts, DISPATCH_PARTS, k == 0),
             in_specs=[smem(), hbm(), vmem(), hbm()],
             out_specs=hbm(),
-            out_shape=pltpu.MemorySpace.HBM((rows, features), jnp.bfloat16),
+            out_shape=pltpu.MemorySpace.HBM((rows, share), jnp.bfloat16),
             scratch_shapes=[
                 pltpu.VMEM(tokens.shape, tokens.dtype),
-                pltpu.VMEM(route_ids.shape, route_ids.dtype), pltpu.VMEM((rows, features), jnp.bfloat16),
+                pltpu.VMEM(route_ids.shape, route_ids.dtype), pltpu.VMEM((rows, share), jnp.bfloat16),
                 pltpu.SemaphoreType.DMA((2,)), pltpu.SemaphoreType.DMA((DISPATCH_PARTS,)),
             ],
             compiler_params=params(),
             name="dispatch",
-        )(own[k].reshape(1).astype(jnp.int32), in_hbm(tokens), moe_gain, in_hbm(route_ids))
+        )(jnp.stack([own[k], odd]).astype(jnp.int32), in_hbm(tokens), moe_gain, in_hbm(route_ids))
 
     arrived = []
     for k in range(chunks):
-        sent = dispatched(k).reshape(row_count, CAP, features)
+        sent = dispatched(k).reshape(row_count, CAP, -1)
         arrived.append(lax.all_to_all(sent, "row", split_axis=0, concat_axis=0, tiled=True))
 
     table = jax.ShapeDtypeStruct((chunks, tok_rows, 2 * rows), jnp.bfloat16)
@@ -351,11 +399,15 @@
 
     mixed = lax.dynamic_slice_in_dim(tokens, position * width, width, 0)
     for k in range(chunks):
-        mine = arrived[k]
-        theirs = swap_cores(mine)
-        keep0, send0, ahead = run_expert(mine.reshape(rows, features), stacks, place(k), blocks, padded)
+        mine = [arrived[k]]
+        if k == 0:
+            half = row_count // 2
+            mine += [shift_y(mine[0][:half], 1), shift_y(mine[0][half:], -1)]
+        theirs = [swap_cores(piece) for piece in mine]
+        flat = lambda pieces: [piece.reshape(-1, piece.shape[-1]) for piece in pieces]
+        keep0, send0, ahead = run_expert(flat(mine), stacks, place(k), blocks, padded)
         got0 = swap_cores(send0)
-        keep1, send1, _ = run_expert(theirs.reshape(rows, features), ahead, place(k), blocks, padded)
+        keep1, send1, _ = run_expert(flat(theirs), ahead, place(k), blocks, padded)
         got1 = swap_cores(send1)
         keep, got = (keep0, keep1), (got0, got1)
         summed = reduced_over_y(keep, got, (row_count, 1, CAP, padded))

time: 203 us -> 171 us (0.84)
  waiting for transfers between devices: 86.3 us -> 62.5 us
  local copies, waits for them, and re-layouts: 17.1 us -> 7.25 us
  starting transfers between devices: 39.1 us -> 42.7 us
    all_to_all x2, waiting for transfers between devices: 62.6 us -> 15.1 us  [local(): lax.all_to_all(sent, 'row', split_axis=0, concat_axis=0, tiled=True)]
    ppermute x8 -> x10, waiting for transfers between devices: 14.8 us -> 33.3 us  [shift_y(): return lax.ppermute(x, 'y', [(i, (i + step) % count) for i in range(count)])]
    unnamed x46 -> x32, local copies, waits for them, and re-layouts: 14.8 us -> 4.86 us
    all_to_all x2, starting transfers between devices: 7.3 us -> 10.7 us  [local(): lax.all_to_all(summed, 'row', split_axis=0, concat_axis=0, tiled=True)]
    ppermute x8 -> x10, starting transfers between devices: 13.4 us -> 16.5 us  [shift_y(): return lax.ppermute(x, 'y', [(i, (i + step) % count) for i in range(count)])]
    all_to_all x2, waiting for transfers between devices: 8.92 us -> 12 us  [local(): lax.all_to_all(summed, 'row', split_axis=0, concat_axis=0, tiled=True)]
    ppermute x2, starting transfers between devices: 4.17 us -> 1.75 us  [local(): moved = lax.ppermute(merged, 'y', [(i, i ^ step) for i in range(y_count)])]
    add x2 -> x4, other arithmetic: 4.29 us -> 3.81 us  [pair(): parts = [wide(keep[e][j]) + wide(got[1 - e][j]) for e in range(2)]]
  transfers between devices with their start and end apart: 21 -> 25, of which waited for: 7 -> 9; matrix products, arithmetic and copies ran while one was open for 8% -> 9% of each run, Pallas kernels for 19% -> 23%
where the time goes in v5:
time: 171 us; the launch traced here: 170 us
  waiting for transfers between devices  62.5 us (37%)
  Pallas kernels  43.8 us (26%)
  starting transfers between devices  42.7 us (25%)
  other arithmetic  13 us (8%)
  local copies, waits for them, and re-layouts  7.25 us (4%)
    ppermute x10, waiting for transfers between devices, shift_y(): return lax.ppermute(x, 'y', [(i, (i + step) % count) for i in range(count)])  33.3 us
    pallas_call x4, Pallas kernels, run_expert(): pl.pallas_call(functools.partial(expert_kernel, blocks, parts, ready, len...  30.2 us
    ppermute x10, starting transfers between devices, shift_y(): return lax.ppermute(x, 'y', [(i, (i + step) % count) for i in range(count)])  16.5 us
    all_to_all x2, waiting for transfers between devices, local(): lax.all_to_all(sent, 'row', split_axis=0, concat_axis=0, tiled=True)  15.1 us
    all_to_all x2, starting transfers between devices, local(): lax.all_to_all(sent, 'row', split_axis=0, concat_axis=0, tiled=True)  12.4 us
    all_to_all x2, waiting for transfers between devices, local(): lax.all_to_all(summed, 'row', split_axis=0, concat_axis=0, tiled=True)  12 us
    all_to_all x2, starting transfers between devices, local(): lax.all_to_all(summed, 'row', split_axis=0, concat_axis=0, tiled=True)  10.7 us
    pallas_call x2, Pallas kernels, dispatched(): pl.pallas_call(functools.partial(dispatch_kernel, local_experts, DISPATCH...  7.99 us
  transfers between devices with their start and end apart: 25, of which 9 were waited for; matrix products, arithmetic and copies ran while one was open for 9% of the time, Pallas kernels for 23%

profile of v5, /device:TPU:0, one launch (start us, length us, event | category | flops | bytes accessed | tf_op | source)
XLA Modules:
  0.0 170.4 jit_solution(3066937443981346312)
XLA Ops:
  0.6 0.7 reshape.483.gain_ref
  1.4 3.9 %dispatch.3 = bf16[384,1536]{1,0:T(8,128)(2,1)} custom-call(s32[2]{0:T(128)S(1)} %get-tuple-element.87.own_ref, bf16[2880,256]{1,0:T(8,128)(2,1)} %bitcast.90, bf16[1,2880]{1,0:T(2,128)(2,1)S(1)} %reshape.483.gain_ref, s32[4,256]{1,0:T(4,128)} %bitcast.98), custom_call_target="tpu_custom_call" | custom-call | tf_op jit(solution)/shard_map/dispatch/pallas_call | solution.py:365
  5.3 8.0 %all-to-all-start.2 = ((bf16[16,24,1536]{2,1,0:T(8,128)(2,1)}), bf16[16,24,1536]{2,1,0:T(8,128)(2,1)S(1)}, u32[]{:S(2)}, u32[]{:S(2)}) async-start(bf16[16,24,1536]{2,1,0:T(8,128)(2,1)} %bitcast.124), calls=%async_computation.2 | async-start | bytes 2359296 | tf_op jit(solution)/shard_map/all_to_all | solution.py:382
  13.3 4.1 %dispatch.2 = bf16[384,2880]{1,0:T(8,128)(2,1)} custom-call(s32[2]{0:T(128)S(1)} %get-tuple-element.86.own_ref, bf16[2880,256]{1,0:T(8,128)(2,1)} %bitcast.91, bf16[1,2880]{1,0:T(2,128)(2,1)S(1)} %reshape.483.gain_ref, s32[4,256]{1,0:T(4,128)} %bitcast.99), custom_call_target="tpu_custom_call" | custom-call | tf_op jit(solution)/shard_map/dispatch/pallas_call | solution.py:365
  17.4 15.1 %all-to-all-done.2 = bf16[16,24,1536]{2,1,0:T(8,128)(2,1)S(1)} async-done(((bf16[16,24,1536]{2,1,0:T(8,128)(2,1)}), bf16[16,24,1536]{2,1,0:T(8,128)(2,1)S(1)}, u32[]{:S(2)}, u32[]{:S(2)}) %all-to-all-start.2) | async-done | bytes 1179680 | tf_op jit(solution)/shard_map/all_to_all | solution.py:382
  32.6 4.4 %all-to-all-start = ((bf16[16,24,2880]{2,1,0:T(8,128)(2,1)}), bf16[16,24,2880]{2,1,0:T(8,128)(2,1)}, u32[]{:S(2)}, u32[]{:S(2)}) async-start(bf16[16,24,2880]{2,1,0:T(8,128)(2,1)} %bitcast.107), calls=%async_computation | async-start | bytes 4521984 | tf_op jit(solution)/shard_map/all_to_all | solution.py:382
  37.2 1.6 collective-permute-start.7
  38.8 1.7 collective-permute-start.8
  40.5 11.6 %collective-permute-done.7 = bf16[8,24,1536]{2,1,0:T(8,128)(2,1)S(1)} collective-permute-done((bf16[8,24,1536]{2,1,0:T(8,128)(2,1)S(1)}, bf16[8,24,1536]{2,1,0:T(8,128)(2,1)S(1)}, u32[]{:S(2)}, u32[]{:S(2)}) %collective-permute-start.7) | collective-permute-done | bytes 589856 | tf_op jit(solution)/shard_map/ppermute | solution.py:304
  52.1 2.5 %collective-permute-done.8 = bf16[8,24,1536]{2,1,0:T(8,128)(2,1)} collective-permute-done((bf16[8,24,1536]{2,1,0:T(8,128)(2,1)S(1)}, bf16[8,24,1536]{2,1,0:T(8,128)(2,1)}, u32[]{:S(2)}, u32[]{:S(2)}) %collective-permute-start.8) | collective-permute-done | bytes 589856 | tf_op jit(solution)/shard_map/ppermute | solution.py:304
  55.2 3.6 %route.1 = (bf16[2,256,768]{2,1,0:T(8,128)(2,1)S(1)}, bf16[2,256,768]{2,1,0:T(8,128)(2,1)S(1)}, f32[8,256]{1,0:T(8,128)S(1)}) custom-call(s32[2]{0:T(128)S(1)} %pad_add_fusion.own_ref, s32[4,256]{1,0:T(4,128)S(1)} %bitcast.100, f32[4,256]{1,0:T(4,128)S(1)} %bitcast.101, bf16[2880,256]{1,0:T(8,128)(2,1)S(1)} %bitcast.92, ...), custom_call_target="tpu_custom_call" | custom-call | tf_op jit(solution)/shard_map/route/pallas_call | solution.py:385
  58.9 0.9 copy-done.7
  59.7 0.9 copy-done.9
  60.7 0.5 collective-permute-start.18
  61.2 8.3 %first.3 = (bf16[4,384,384]{2,1,0:T(8,128)(2,1)S(1)}, bf16[4,384,384]{2,1,0:T(8,128)(2,1)}, bf16[360,2880]{1,0:T(8,128)(2,1)S(1)}, bf16[360,2880]{1,0:T(8,128)(2,1)S(1)}, bf16[360,2880]{1,0:T(8,128)(2,1)S(1)}) custom-call(s32[4]{0:T(128)S(1)} %pad_add_fusion.4.own_ref, bf16[384,1536]{1,0:T(8,128)(2,1)S(1)} %bitcast.93, bf16[192,1536]{1,0:T(8,128)(2,1)S(1)} %bitcast.96, ...), custom_call_target="tpu_custom_call" | custom-call | tf_op jit(solution)/shard_map/first/pallas_call | solution.py:271
  69.7 7.2 %second.3 = (bf16[4,384,384]{2,1,0:T(8,128)(2,1)S(1)}, bf16[4,384,384]{2,1,0:T(8,128)(2,1)}) custom-call(s32[4]{0:T(128)S(1)} %pad_add_fusion.4.own_ref, bf16[384,1536]{1,0:T(8,128)(2,1)} %bitcast.43.refs_0_, bf16[192,1536]{1,0:T(8,128)(2,1)} %bitcast.44.refs_1_, bf16[192,1536]{1,0:T(8,128)(2,1)} %bitcast.45.refs_2_, ...), custom_call_target="tpu_custom_call" | custom-call | tf_op jit(solution)/shard_map/second/pallas_call | solution.py:271
  77.0 1.0 copy-done.5
  78.2 1.0 slice_bitcast_fusion
  79.6 1.7 collective-permute-start.19
  81.3 2.0 %collective-permute-done.19 = f32[8,256]{1,0:T(8,128)S(1)} collective-permute-done((f32[8,256]{1,0:T(8,128)S(1)}, f32[8,256]{1,0:T(8,128)S(1)}, u32[]{:S(2)}, u32[]{:S(2)}) %collective-permute-start.19) | collective-permute-done | bytes 8224 | tf_op jit(solution)/shard_map/ppermute | solution.py:420
  83.3 8.5 %first.2 = (bf16[4,384,384]{2,1,0:T(8,128)(2,1)S(1)}, bf16[4,384,384]{2,1,0:T(8,128)(2,1)S(1)}, bf16[360,2880]{1,0:T(8,128)(2,1)S(1)}, bf16[360,2880]{1,0:T(8,128)(2,1)S(1)}, bf16[360,2880]{1,0:T(8,128)(2,1)S(1)}) custom-call(s32[4]{0:T(128)S(1)} %pad_add_fusion.1.own_ref, bf16[384,2880]{1,0:T(8,128)(2,1)} %bitcast.14.refs_0_, ...), custom_call_target="tpu_custom_call" | custom-call | tf_op jit(solution)/shard_map/first/pallas_call | solution.py:271
  91.9 1.0 add_convert_fusion
  93.0 1.0 add_convert_fusion.1
  94.2 1.7 collective-permute-start.14
  95.8 1.7 collective-permute-start.16
  97.5 1.3 convert_add_fusion.3
  98.8 1.3 convert_add_fusion.2
  100.1 6.1 %second.2 = (bf16[4,384,384]{2,1,0:T(8,128)(2,1)S(1)}, bf16[4,384,384]{2,1,0:T(8,128)(2,1)S(1)}) custom-call(s32[4]{0:T(128)S(1)} %pad_add_fusion.1.own_ref, bf16[384,2880]{1,0:T(8,128)(2,1)} %bitcast.17.refs_0_, bf16[360,2880]{1,0:T(8,128)(2,1)S(1)} %get-tuple-element.32.refs_1_, bf16[360,2880]{1,0:T(8,128)(2,1)S(1)} %get-tuple-element.33.refs_2_, ...), custom_call_target="tpu_custom_call" | custom-call | tf_op jit(solution)/shard_map/second/pallas_call | solution.py:271
  106.6 0.4 collective-permute-start.15
  107.2 2.9 %collective-permute-start.17 = (bf16[16,2,24,384]{3,2,1,0:T(8,128)(2,1)S(1)}, bf16[16,2,24,384]{3,2,1,0:T(8,128)(2,1)S(1)}, u32[]{:S(2)}, u32[]{:S(2)}) collective-permute-start(bf16[16,2,24,384]{3,2,1,0:T(8,128)(2,1)S(1)} %pad_maximum_fusion.9), channel_id=1, source_target_pairs={{0,96},{32,0},{64,32},{96,64},{1,97},{33,1},{65,33},{97,65},{2,98}... | collective-permute-start | bytes 1769480 | tf_op jit(solution)/shard_map/ppermute | solution.py:304
  110.6 3.2 %collective-permute-start.5 = (bf16[8,2,24,384]{3,2,1,0:T(8,128)(2,1)S(1)}, bf16[8,2,24,384]{3,2,1,0:T(8,128)(2,1)S(1)}, u32[]{:S(2)}, u32[]{:S(2)}) collective-permute-start(bf16[8,2,24,384]{3,2,1,0:T(8,128)(2,1)S(1)} %get-tuple-element.81), channel_id=1, source_target_pairs={{0,96},{32,0},{64,32},{96,64},{1,97},{33,1},{65,33},{97,65},{2,98}... | collective-permute-start | bytes 884744 | tf_op jit(solution)/shard_map/ppermute | solution.py:304
  114.0 1.0 convert_add_fusion.8
  115.1 14.9 %collective-permute-done.3 = bf16[8,2,24,384]{3,2,1,0:T(8,128)(2,1)S(1)} collective-permute-done((bf16[8,2,24,384]{3,2,1,0:T(8,128)(2,1)S(1)}, bf16[8,2,24,384]{3,2,1,0:T(8,128)(2,1)S(1)}, u32[]{:S(2)}, u32[]{:S(2)}) %collective-permute-start.3) | collective-permute-done | bytes 294944 | tf_op jit(solution)/shard_map/ppermute | solution.py:304
  130.0 0.9 pad_maximum_fusion.5
  131.0 0.9 pad_maximum_fusion.6
  131.9 3.2 %collective-permute-start.6 = (bf16[16,2,24,384]{3,2,1,0:T(8,128)(2,1)}, bf16[16,2,24,384]{3,2,1,0:T(8,128)(2,1)}, u32[]{:S(2)}, u32[]{:S(2)}) collective-permute-start(bf16[16,2,24,384]{3,2,1,0:T(8,128)(2,1)} %pad_maximum_fusion.6), channel_id=1, source_target_pairs={{0,96},{32,0},{64,32},{96,64},{1,97},{33,1},{65,33},{97,65},{2,98}... | collective-permute-start | bytes 1769480 | tf_op jit(solution)/shard_map/ppermute | solution.py:304
  135.1 1.1 fusion.3
  136.2 7.1 %all-to-all-start.3 = ((bf16[16,2,24,384]{3,2,1,0:T(8,128)(2,1)}), bf16[16,2,24,384]{3,2,1,0:T(8,128)(2,1)S(1)}, u32[]{:S(2)}, u32[]{:S(2)}) async-start(bf16[16,2,24,384]{3,2,1,0:T(8,128)(2,1)} %fusion.3), calls=%async_computation.3 | async-start | bytes 1179648 | tf_op jit(solution)/shard_map/all_to_all | solution.py:414
  143.4 4.0 %collective-permute-done.4 = bf16[16,2,24,384]{3,2,1,0:T(8,128)(2,1)} collective-permute-done((bf16[16,2,24,384]{3,2,1,0:T(8,128)(2,1)}, bf16[16,2,24,384]{3,2,1,0:T(8,128)(2,1)}, u32[]{:S(2)}, u32[]{:S(2)}) %collective-permute-start.4) | collective-permute-done | bytes 589856 | tf_op jit(solution)/shard_map/ppermute | solution.py:304
  147.7 2.4 %fusion.1 = bf16[16,2,24,384]{3,2,1,0:T(8,128)(2,1)} fusion(f32[16,1,24,384]{3,2,1,0:T(8,128)} %bitcast.128, f32[16,1,24,384]{3,2,1,0:T(8,128)S(1)} %bitcast.127, bf16[16,2,24,384]{3,2,1,0:T(8,128)(2,1)} %collective-permute-done.6, bf16[16,2,24,384]{3,2,1,0:T(8,128)(2,1)} %collective-permute-done.4), kind=kLoop, calls=%fused_computation.2 | loop fusion | flops 1769472 | bytes 2949120 | tf_op jit(solution)/shard_map/convert_element_type | solution.py:327
  150.1 4.7 %all-to-all-done.3 = bf16[16,2,24,384]{3,2,1,0:T(8,128)(2,1)S(1)} async-done(((bf16[16,2,24,384]{3,2,1,0:T(8,128)(2,1)}), bf16[16,2,24,384]{3,2,1,0:T(8,128)(2,1)S(1)}, u32[]{:S(2)}, u32[]{:S(2)}) %all-to-all-start.3) | async-done | bytes 589856 | tf_op jit(solution)/shard_map/all_to_all | solution.py:414
  154.8 3.6 %all-to-all-start.1 = ((bf16[16,2,24,384]{3,2,1,0:T(8,128)(2,1)}), bf16[16,2,24,384]{3,2,1,0:T(8,128)(2,1)S(1)}, u32[]{:S(2)}, u32[]{:S(2)}) async-start(bf16[16,2,24,384]{3,2,1,0:T(8,128)(2,1)} %fusion.1), calls=%async_computation.1 | async-start | bytes 1179648 | tf_op jit(solution)/shard_map/all_to_all | solution.py:414
  158.5 0.6 fusion.22
  159.1 1.0 copy-done.1
  160.1 1.0 copy-done.2
  161.1 0.7 combine.2.rest_ref
  161.7 7.3 %all-to-all-done.1 = bf16[16,2,24,384]{3,2,1,0:T(8,128)(2,1)S(1)} async-done(((bf16[16,2,24,384]{3,2,1,0:T(8,128)(2,1)}), bf16[16,2,24,384]{3,2,1,0:T(8,128)(2,1)S(1)}, u32[]{:S(2)}, u32[]{:S(2)}) %all-to-all-start.1) | async-done | bytes 589856 | tf_op jit(solution)/shard_map/all_to_all | solution.py:414
  169.1 1.3 combine.3
  (87 shorter events, 3.5 us)
Async XLA Ops:
  5.3 27.3 %all-to-all-start.2 = ((bf16[16,24,1536]{2,1,0:T(8,128)(2,1)}), bf16[16,24,1536]{2,1,0:T(8,128)(2,1)S(1)}, u32[]{:S(2)}, u32[]{:S(2)}) async-start(bf16[16,24,1536]{2,1,0:T(8,128)(2,1)} %bitcast.124), calls=%async_computation.2 | async-start | bytes 2359296 | tf_op jit(solution)/shard_map/all_to_all | solution.py:382
  32.6 46.7 %all-to-all-start = ((bf16[16,24,2880]{2,1,0:T(8,128)(2,1)}), bf16[16,24,2880]{2,1,0:T(8,128)(2,1)}, u32[]{:S(2)}, u32[]{:S(2)}) async-start(bf16[16,24,2880]{2,1,0:T(8,128)(2,1)} %bitcast.107), calls=%async_computation | async-start | bytes 4521984 | tf_op jit(solution)/shard_map/all_to_all | solution.py:382
  37.0 17.7 %copy-start.15 = (bf16[2880]{0:T(1024)(128)(2,1)S(1)}, bf16[2880]{0:T(1024)(128)(2,1)}, u32[]{:S(2)}) copy-start(bf16[2880]{0:T(1024)(128)(2,1)} %param.17) | copy-start | bytes 17284
  37.0 18.2 %copy-start = (bf16[256,2880]{0,1:T(8,128)(2,1)S(1)}, bf16[256,2880]{0,1:T(8,128)(2,1)}, u32[]{:S(2)}) copy-start(bf16[256,2880]{0,1:T(8,128)(2,1)} %param.10) | copy-start | bytes 4423684
  37.0 18.2 %copy-start.11 = (bf16[2880,16]{0,1:T(8,128)(2,1)S(1)}, bf16[2880,16]{0,1:T(8,128)(2,1)}, u32[]{:S(2)}) copy-start(bf16[2880,16]{0,1:T(8,128)(2,1)} %param.18) | copy-start | bytes 276484
  37.1 18.2 %copy-start.12 = (s32[256,4]{0,1:T(4,128)S(1)}, s32[256,4]{0,1:T(4,128)}, u32[]{:S(2)}) copy-start(s32[256,4]{0,1:T(4,128)} %param.12) | copy-start | bytes 12292
  37.1 18.1 %copy-start.13 = (f32[256,4]{0,1:T(4,128)S(1)}, f32[256,4]{0,1:T(4,128)}, u32[]{:S(2)}) copy-start(f32[256,4]{0,1:T(4,128)} %param.13) | copy-start | bytes 12292
  37.1 18.1 %copy-start.14 = (s32[256,4]{0,1:T(4,128)S(1)}, s32[256,4]{0,1:T(4,128)}, u32[]{:S(2)}) copy-start(s32[256,4]{0,1:T(4,128)} %param.19) | copy-start | bytes 12292
  37.2 14.9 %collective-permute-start.7 = (bf16[8,24,1536]{2,1,0:T(8,128)(2,1)S(1)}, bf16[8,24,1536]{2,1,0:T(8,128)(2,1)S(1)}, u32[]{:S(2)}, u32[]{:S(2)}) collective-permute-start(bf16[8,24,1536]{2,1,0:T(8,128)(2,1)S(1)} %get-tuple-element.73), channel_id=1, source_target_pairs={{0,32},{32,64},{64,96},{96,0},{1,33},{33,65},{65,97},{97,1},{2,34}... | collective-permute-start | bytes 1769480 | tf_op jit(solution)/shard_map/ppermute | solution.py:304
  38.8 30.8 %collective-permute-start.9 = (bf16[16,24,1536]{2,1,0:T(8,128)(2,1)S(1)}, bf16[16,24,1536]{2,1,0:T(8,128)(2,1)}, u32[]{:S(2)}, u32[]{:S(2)}) collective-permute-start(bf16[16,24,1536]{2,1,0:T(8,128)(2,1)S(1)} %all-to-all-done.2), channel_id=1, source_target_pairs={{0,16},{16,0},{1,17},{17,1},{2,18},{18,2},{3,19},{19,3},{4,20},{20... | collective-permute-start | bytes 3538952 | tf_op jit(solution)/shard_map/ppermute | solution.py:299
  38.8 15.8 %collective-permute-start.8 = (bf16[8,24,1536]{2,1,0:T(8,128)(2,1)S(1)}, bf16[8,24,1536]{2,1,0:T(8,128)(2,1)}, u32[]{:S(2)}, u32[]{:S(2)}) collective-permute-start(bf16[8,24,1536]{2,1,0:T(8,128)(2,1)S(1)} %get-tuple-element.72), channel_id=1, source_target_pairs={{0,96},{32,0},{64,32},{96,64},{1,97},{33,1},{65,33},{97,65},{2,98}... | collective-permute-start | bytes 1769480 | tf_op jit(solution)/shard_map/ppermute | solution.py:304
  52.1 17.5 %collective-permute-start.10 = (bf16[8,24,1536]{2,1,0:T(8,128)(2,1)S(1)}, bf16[8,24,1536]{2,1,0:T(8,128)(2,1)}, u32[]{:S(2)}, u32[]{:S(2)}) collective-permute-start(bf16[8,24,1536]{2,1,0:T(8,128)(2,1)S(1)} %collective-permute-done.7), channel_id=1, source_target_pairs={{0,16},{16,0},{1,17},{17,1},{2,18},{18,2},{3,19},{19,3},{4,20},{20... | collective-permute-start | bytes 1769480 | tf_op jit(solution)/shard_map/ppermute | solution.py:299
  54.7 15.0 %collective-permute-start.11 = (bf16[8,24,1536]{2,1,0:T(8,128)(2,1)}, bf16[8,24,1536]{2,1,0:T(8,128)(2,1)}, u32[]{:S(2)}, u32[]{:S(2)}) collective-permute-start(bf16[8,24,1536]{2,1,0:T(8,128)(2,1)} %collective-permute-done.8), channel_id=1, source_target_pairs={{0,16},{16,0},{1,17},{17,1},{2,18},{18,2},{3,19},{19,3},{4,20},{20... | collective-permute-start | bytes 1769480 | tf_op jit(solution)/shard_map/ppermute | solution.py:299
  58.9 0.9 copy-start.7
  59.7 0.9 copy-start.9
  60.7 18.9 %collective-permute-start.18 = (f32[8,256]{1,0:T(8,128)S(1)}, f32[8,256]{1,0:T(8,128)S(1)}, u32[]{:S(2)}, u32[]{:S(2)}) collective-permute-start(f32[8,256]{1,0:T(8,128)S(1)} %get-tuple-element.55), channel_id=1, source_target_pairs={{0,16},{16,0},{1,17},{17,1},{2,18},{18,2},{3,19},{19,3},{4,20},{20... | collective-permute-start | bytes 24584 | tf_op jit(solution)/shard_map/ppermute | solution.py:299
  69.6 7.4 %copy-start.3 = (bf16[4,384,384]{2,1,0:T(8,128)(2,1)}, bf16[4,384,384]{2,1,0:T(8,128)(2,1)S(1)}, u32[]{:S(2)}) copy-start(bf16[4,384,384]{2,1,0:T(8,128)(2,1)S(1)} %get-tuple-element.50) | copy-start | bytes 3538948
  69.6 22.4 %collective-permute-start.12 = (bf16[4,384,384]{2,1,0:T(8,128)(2,1)}, bf16[4,384,384]{2,1,0:T(8,128)(2,1)}, u32[]{:S(2)}, u32[]{:S(2)}) collective-permute-start(bf16[4,384,384]{2,1,0:T(8,128)(2,1)} %get-tuple-element.48), channel_id=1, source_target_pairs={{0,16},{16,0},{1,17},{17,1},{2,18},{18,2},{3,19},{19,3},{4,20},{20... | collective-permute-start | bytes 3538952 | tf_op jit(solution)/shard_map/ppermute | solution.py:299
  69.7 8.5 %copy-start.8 = (bf16[2,256,768]{2,1,0:T(8,128)(2,1)S(1)}, bf16[2,256,768]{2,1,0:T(8,128)(2,1)}, u32[]{:S(2)}) copy-start(bf16[2,256,768]{2,1,0:T(8,128)(2,1)} %copy-done.7) | copy-start | bytes 2359300
  69.7 8.5 %copy-start.10 = (bf16[2,256,768]{2,1,0:T(8,128)(2,1)S(1)}, bf16[2,256,768]{2,1,0:T(8,128)(2,1)}, u32[]{:S(2)}) copy-start(bf16[2,256,768]{2,1,0:T(8,128)(2,1)} %copy-done.9) | copy-start | bytes 2359300
  77.0 1.0 copy-start.5
  78.0 15.0 %collective-permute-start.13 = (bf16[4,384,384]{2,1,0:T(8,128)(2,1)}, bf16[4,384,384]{2,1,0:T(8,128)(2,1)}, u32[]{:S(2)}, u32[]{:S(2)}) collective-permute-start(bf16[4,384,384]{2,1,0:T(8,128)(2,1)} %get-tuple-element.49), channel_id=1, source_target_pairs={{0,16},{16,0},{1,17},{17,1},{2,18},{18,2},{3,19},{19,3},{4,20},{20... | collective-permute-start | bytes 3538952 | tf_op jit(solution)/shard_map/ppermute | solution.py:299
  79.2 20.9 %collective-permute-start = (bf16[16,24,2880]{2,1,0:T(8,128)(2,1)}, bf16[16,24,2880]{2,1,0:T(8,128)(2,1)}, u32[]{:S(2)}, u32[]{:S(2)}) collective-permute-start(bf16[16,24,2880]{2,1,0:T(8,128)(2,1)} %all-to-all-done), channel_id=1, source_target_pairs={{0,16},{16,0},{1,17},{17,1},{2,18},{18,2},{3,19},{19,3},{4,20},{20... | collective-permute-start | bytes 6635528 | tf_op jit(solution)/shard_map/ppermute | solution.py:299
  79.6 3.7 %collective-permute-start.19 = (f32[8,256]{1,0:T(8,128)S(1)}, f32[8,256]{1,0:T(8,128)S(1)}, u32[]{:S(2)}, u32[]{:S(2)}) collective-permute-start(f32[8,256]{1,0:T(8,128)S(1)} %pad_maximum_fusion.10), channel_id=1, source_target_pairs={{0,32},{32,0},{64,96},{96,64},{1,33},{33,1},{65,97},{97,65},{2,34}... | collective-permute-start | bytes 24584 | tf_op jit(solution)/shard_map/ppermute | solution.py:420
  83.3 8.6 %copy-start.6 = (bf16[4,384,384]{2,1,0:T(8,128)(2,1)S(1)}, bf16[4,384,384]{2,1,0:T(8,128)(2,1)}, u32[]{:S(2)}) copy-start(bf16[4,384,384]{2,1,0:T(8,128)(2,1)} %copy-done.5) | copy-start | bytes 3538948
  83.3 9.7 %copy-start.4 = (bf16[4,384,384]{2,1,0:T(8,128)(2,1)S(1)}, bf16[4,384,384]{2,1,0:T(8,128)(2,1)}, u32[]{:S(2)}) copy-start(bf16[4,384,384]{2,1,0:T(8,128)(2,1)} %copy-done.3) | copy-start | bytes 3538948
  91.8 18.3 %collective-permute-start.1 = (bf16[4,384,384]{2,1,0:T(8,128)(2,1)S(1)}, bf16[4,384,384]{2,1,0:T(8,128)(2,1)S(1)}, u32[]{:S(2)}, u32[]{:S(2)}) collective-permute-start(bf16[4,384,384]{2,1,0:T(8,128)(2,1)S(1)} %get-tuple-element.36), channel_id=1, source_target_pairs={{0,16},{16,0},{1,17},{17,1},{2,18},{18,2},{3,19},{19,3},{4,20},{20... | collective-permute-start | bytes 3538952 | tf_op jit(solution)/shard_map/ppermute | solution.py:299
  94.2 12.3 %collective-permute-start.14 = (bf16[8,2,24,384]{3,2,1,0:T(8,128)(2,1)S(1)}, bf16[8,2,24,384]{3,2,1,0:T(8,128)(2,1)S(1)}, u32[]{:S(2)}, u32[]{:S(2)}) collective-permute-start(bf16[8,2,24,384]{3,2,1,0:T(8,128)(2,1)S(1)} %get-tuple-element.78), channel_id=1, source_target_pairs={{0,32},{32,64},{64,96},{96,0},{1,33},{33,65},{65,97},{97,1},{2,34}... | collective-permute-start | bytes 884744 | tf_op jit(solution)/shard_map/ppermute | solution.py:304
  95.8 11.2 %collective-permute-start.16 = (bf16[8,2,24,384]{3,2,1,0:T(8,128)(2,1)S(1)}, bf16[8,2,24,384]{3,2,1,0:T(8,128)(2,1)S(1)}, u32[]{:S(2)}, u32[]{:S(2)}) collective-permute-start(bf16[8,2,24,384]{3,2,1,0:T(8,128)(2,1)S(1)} %get-tuple-element.79), channel_id=1, source_target_pairs={{0,96},{32,0},{64,32},{96,64},{1,97},{33,1},{65,33},{97,65},{2,98}... | collective-permute-start | bytes 884744 | tf_op jit(solution)/shard_map/ppermute | solution.py:304
  106.3 4.0 %collective-permute-start.2 = (bf16[4,384,384]{2,1,0:T(8,128)(2,1)S(1)}, bf16[4,384,384]{2,1,0:T(8,128)(2,1)S(1)}, u32[]{:S(2)}, u32[]{:S(2)}) collective-permute-start(bf16[4,384,384]{2,1,0:T(8,128)(2,1)S(1)} %get-tuple-element.37), channel_id=1, source_target_pairs={{0,16},{16,0},{1,17},{17,1},{2,18},{18,2},{3,19},{19,3},{4,20},{20... | collective-permute-start | bytes 3538952 | tf_op jit(solution)/shard_map/ppermute | solution.py:299
  106.6 28.5 %collective-permute-start.15 = (bf16[16,2,24,384]{3,2,1,0:T(8,128)(2,1)S(1)}, bf16[16,2,24,384]{3,2,1,0:T(8,128)(2,1)S(1)}, u32[]{:S(2)}, u32[]{:S(2)}) collective-permute-start(bf16[16,2,24,384]{3,2,1,0:T(8,128)(2,1)S(1)} %pad_maximum_fusion.8), channel_id=1, source_target_pairs={{0,32},{32,64},{64,96},{96,0},{1,33},{33,65},{65,97},{97,1},{2,34}... | collective-permute-start | bytes 1769480 | tf_op jit(solution)/shard_map/ppermute | solution.py:304
  107.2 27.9 %collective-permute-start.17 = (bf16[16,2,24,384]{3,2,1,0:T(8,128)(2,1)S(1)}, bf16[16,2,24,384]{3,2,1,0:T(8,128)(2,1)S(1)}, u32[]{:S(2)}, u32[]{:S(2)}) collective-permute-start(bf16[16,2,24,384]{3,2,1,0:T(8,128)(2,1)S(1)} %pad_maximum_fusion.9), channel_id=1, source_target_pairs={{0,96},{32,0},{64,32},{96,64},{1,97},{33,1},{65,33},{97,65},{2,98}... | collective-permute-start | bytes 1769480 | tf_op jit(solution)/shard_map/ppermute | solution.py:304
  110.5 19.5 %collective-permute-start.3 = (bf16[8,2,24,384]{3,2,1,0:T(8,128)(2,1)S(1)}, bf16[8,2,24,384]{3,2,1,0:T(8,128)(2,1)S(1)}, u32[]{:S(2)}, u32[]{:S(2)}) collective-permute-start(bf16[8,2,24,384]{3,2,1,0:T(8,128)(2,1)S(1)} %get-tuple-element.80), channel_id=1, source_target_pairs={{0,32},{32,64},{64,96},{96,0},{1,33},{33,65},{65,97},{97,1},{2,34}... | collective-permute-start | bytes 884744 | tf_op jit(solution)/shard_map/ppermute | solution.py:304
  110.6 20.4 %collective-permute-start.5 = (bf16[8,2,24,384]{3,2,1,0:T(8,128)(2,1)S(1)}, bf16[8,2,24,384]{3,2,1,0:T(8,128)(2,1)S(1)}, u32[]{:S(2)}, u32[]{:S(2)}) collective-permute-start(bf16[8,2,24,384]{3,2,1,0:T(8,128)(2,1)S(1)} %get-tuple-element.81), channel_id=1, source_target_pairs={{0,96},{32,0},{64,32},{96,64},{1,97},{33,1},{65,33},{97,65},{2,98}... | collective-permute-start | bytes 884744 | tf_op jit(solution)/shard_map/ppermute | solution.py:304
  130.9 16.5 %collective-permute-start.4 = (bf16[16,2,24,384]{3,2,1,0:T(8,128)(2,1)}, bf16[16,2,24,384]{3,2,1,0:T(8,128)(2,1)}, u32[]{:S(2)}, u32[]{:S(2)}) collective-permute-start(bf16[16,2,24,384]{3,2,1,0:T(8,128)(2,1)} %pad_maximum_fusion.5), channel_id=1, source_target_pairs={{0,32},{32,64},{64,96},{96,0},{1,33},{33,65},{65,97},{97,1},{2,34}... | collective-permute-start | bytes 1769480 | tf_op jit(solution)/shard_map/ppermute | solution.py:304
  131.9 15.8 %collective-permute-start.6 = (bf16[16,2,24,384]{3,2,1,0:T(8,128)(2,1)}, bf16[16,2,24,384]{3,2,1,0:T(8,128)(2,1)}, u32[]{:S(2)}, u32[]{:S(2)}) collective-permute-start(bf16[16,2,24,384]{3,2,1,0:T(8,128)(2,1)} %pad_maximum_fusion.6), channel_id=1, source_target_pairs={{0,96},{32,0},{64,32},{96,64},{1,97},{33,1},{65,33},{97,65},{2,98}... | collective-permute-start | bytes 1769480 | tf_op jit(solution)/shard_map/ppermute | solution.py:304
  136.2 18.6 %all-to-all-start.3 = ((bf16[16,2,24,384]{3,2,1,0:T(8,128)(2,1)}), bf16[16,2,24,384]{3,2,1,0:T(8,128)(2,1)S(1)}, u32[]{:S(2)}, u32[]{:S(2)}) async-start(bf16[16,2,24,384]{3,2,1,0:T(8,128)(2,1)} %fusion.3), calls=%async_computation.3 | async-start | bytes 1179648 | tf_op jit(solution)/shard_map/all_to_all | solution.py:414
  143.4 15.1 %collective-permute-start.20 = (f32[8,256]{1,0:T(8,128)S(1)}, f32[8,256]{1,0:T(8,128)S(1)}, u32[]{:S(2)}, u32[]{:S(2)}) collective-permute-start(f32[8,256]{1,0:T(8,128)S(1)} %pad_maximum_fusion.11), channel_id=1, source_target_pairs={{0,64},{32,96},{64,0},{96,32},{1,65},{33,97},{65,1},{97,33},{2,66}... | collective-permute-start | bytes 24584 | tf_op jit(solution)/shard_map/ppermute | solution.py:420
  154.8 14.3 %all-to-all-start.1 = ((bf16[16,2,24,384]{3,2,1,0:T(8,128)(2,1)}), bf16[16,2,24,384]{3,2,1,0:T(8,128)(2,1)S(1)}, u32[]{:S(2)}, u32[]{:S(2)}) async-start(bf16[16,2,24,384]{3,2,1,0:T(8,128)(2,1)} %fusion.1), calls=%async_computation.1 | async-start | bytes 1179648 | tf_op jit(solution)/shard_map/all_to_all | solution.py:414
  159.1 1.0 copy-start.1
  160.1 1.0 copy-start.2

commit v6 on v5

--- a/solution.py
+++ b/solution.py
@@ -314,17 +314,21 @@
         return jnp.concatenate([part.reshape(shape) for part in parts], axis=1)
 
     half = shape[0] // 2
-    far = pair(keep, got, 2).astype(jnp.bfloat16)
-    keep, got, far = lax.optimization_barrier((keep, got, far))
-    from_low = shift_y(far[:half], 1)
-    from_high = shift_y(far[half:], -1)
-    up = pair(keep, got, 1)
-    down = pair(keep, got, 3)
-    up = jnp.concatenate([up[:half] + wide(from_low), up[half:]]).astype(jnp.bfloat16)
-    down = jnp.concatenate([down[:half], down[half:] + wide(from_high)]).astype(jnp.bfloat16)
-    from_low = shift_y(up, 1)
-    from_high = shift_y(down, -1)
-    return (pair(keep, got, 0) + wide(from_low) + wide(from_high)).astype(jnp.bfloat16)
+    narrow = lambda x: x.astype(jnp.bfloat16)
+    far, up, down = (pair(keep, got, j) for j in (2, 1, 3))
+    rising = narrow(jnp.stack([far[:half], up[half:]]))
+    falling = narrow(jnp.stack([far[half:], down[:half]]))
+    keep, got, rising, falling = lax.optimization_barrier((keep, got, rising, falling))
+    low = shift_y(rising, 1)
+    high = shift_y(falling, -1)
+    up = narrow(pair(keep, got, 1)[:half] + wide(low[0]))
+    down = narrow(pair(keep, got, 3)[half:] + wide(high[0]))
+    last_low = shift_y(up, 1)
+    last_high = shift_y(down, -1)
+    own = pair(keep, got, 0)
+    first = own[:half] + wide(high[1]) + wide(last_low)
+    second = own[half:] + wide(low[1]) + wide(last_high)
+    return narrow(jnp.concatenate([first, second]))
 
 
 def merge_stats(first, second):

time: 171 us -> 177 us (1.035)
  blocking collectives: 0 us -> 26.6 us
  waiting for transfers between devices: 62.5 us -> 41.4 us
  starting transfers between devices: 42.7 us -> 32.2 us
  local copies, waits for them, and re-layouts: 7.25 us -> 15.6 us
  other arithmetic: 13 us -> 17.1 us
    all_to_all x0 -> x1, blocking collectives: none -> 26.6 us  [local(): lax.all_to_all(sent, 'row', split_axis=0, concat_axis=0, tiled=True)]
    all_to_all x2 -> x1, waiting for transfers between devices: 15.1 us -> 0.01 us  [local(): lax.all_to_all(sent, 'row', split_axis=0, concat_axis=0, tiled=True)]
    unnamed x32 -> x48, local copies, waits for them, and re-layouts: 4.86 us -> 13 us
    all_to_all x2 -> x1, starting transfers between devices: 12.4 us -> 4.46 us  [local(): lax.all_to_all(sent, 'row', split_axis=0, concat_axis=0, tiled=True)]
    all_to_all x2, waiting for transfers between devices: 12 us -> 7.12 us  [local(): lax.all_to_all(summed, 'row', split_axis=0, concat_axis=0, tiled=True)]
    another operation x12 -> x16, other arithmetic: 2.69 us -> 6.42 us
    ppermute x10, starting transfers between devices: 16.5 us -> 13 us  [shift_y(): return lax.ppermute(x, 'y', [(i, (i + step) % count) for i in range(count)])]
    add x4 -> x8, other arithmetic: 3.81 us -> 6.65 us  [pair(): parts = [wide(keep[e][j]) + wide(got[1 - e][j]) for e in range(2)]]
  transfers between devices with their start and end apart: 25 -> 24, of which waited for: 9 -> 10; matrix products, arithmetic and copies ran while one was open for 9% -> 9% of each run, Pallas kernels for 23% -> 21%
where the time goes in v6:
time: 177 us; the launch traced here: 176 us
  Pallas kernels  42.2 us (24%)
  waiting for transfers between devices  41.4 us (23%)
  starting transfers between devices  32.2 us (18%)
  blocking collectives  26.6 us (15%)
  other arithmetic  17.1 us (10%)
  local copies, waits for them, and re-layouts  15.6 us (9%)
    ppermute x10, waiting for transfers between devices, shift_y(): return lax.ppermute(x, 'y', [(i, (i + step) % count) for i in range(count)])  34.3 us
    pallas_call x4, Pallas kernels, run_expert(): pl.pallas_call(functools.partial(expert_kernel, blocks, parts, ready, len...  28.5 us
    all_to_all x1, blocking collectives, local(): lax.all_to_all(sent, 'row', split_axis=0, concat_axis=0, tiled=True)  26.6 us
    ppermute x10, starting transfers between devices, shift_y(): return lax.ppermute(x, 'y', [(i, (i + step) % count) for i in range(count)])  13 us
    unnamed x48, local copies, waits for them, and re-layouts  13 us
    all_to_all x2, starting transfers between devices, local(): lax.all_to_all(summed, 'row', split_axis=0, concat_axis=0, tiled=True)  10.5 us
    pallas_call x2, Pallas kernels, dispatched(): pl.pallas_call(functools.partial(dispatch_kernel, local_experts, DISPATCH...  8.01 us
    all_to_all x2, waiting for transfers between devices, local(): lax.all_to_all(summed, 'row', split_axis=0, concat_axis=0, tiled=True)  7.12 us
  transfers between devices with their start and end apart: 24, of which 10 were waited for; matrix products, arithmetic and copies ran while one was open for 9% of the time, Pallas kernels for 21%

profile of v6, /device:TPU:0, one launch (start us, length us, event | category | flops | bytes accessed | tf_op | source)
XLA Modules:
  0.0 176.2 jit_solution(15869490041214864893)
XLA Ops:
  1.4 3.9 %dispatch.3 = bf16[384,1536]{1,0:T(8,128)(2,1)} custom-call(s32[2]{0:T(128)S(1)} %get-tuple-element.103.own_ref, bf16[2880,256]{1,0:T(8,128)(2,1)} %bitcast.170, bf16[1,2880]{1,0:T(2,128)(2,1)S(1)} %reshape.719.gain_ref, s32[4,256]{1,0:T(4,128)} %bitcast.179), custom_call_target="tpu_custom_call" | custom-call | tf_op jit(solution)/shard_map/dispatch/pallas_call | solution.py:369
  5.3 26.6 %all_to_all.20 = bf16[16,24,1536]{2,1,0:T(8,128)(2,1)S(1)} all-to-all(bf16[16,24,1536]{2,1,0:T(8,128)(2,1)} %bitcast.189), channel_id=1, replica_groups=mesh['y'=4,'core'=2,'row'=16] {'row'}, dimensions={0} | all-to-all | bytes 2359296 | tf_op jit(solution)/shard_map/all_to_all | solution.py:386
  31.9 1.6 collective-permute-start.7
  33.6 1.7 collective-permute-start.8
  35.3 4.1 %dispatch.2 = bf16[384,2880]{1,0:T(8,128)(2,1)} custom-call(s32[2]{0:T(128)S(1)} %get-tuple-element.102.own_ref, bf16[2880,256]{1,0:T(8,128)(2,1)} %bitcast.171, bf16[1,2880]{1,0:T(2,128)(2,1)S(1)} %reshape.719.gain_ref, s32[4,256]{1,0:T(4,128)} %bitcast.180), custom_call_target="tpu_custom_call" | custom-call | tf_op jit(solution)/shard_map/dispatch/pallas_call | solution.py:369
  39.4 4.5 %all-to-all-start = ((bf16[16,24,2880]{2,1,0:T(8,128)(2,1)}), bf16[16,24,2880]{2,1,0:T(8,128)(2,1)}, u32[]{:S(2)}, u32[]{:S(2)}) async-start(bf16[16,24,2880]{2,1,0:T(8,128)(2,1)} %bitcast.188), calls=%async_computation | async-start | bytes 4521984 | tf_op jit(solution)/shard_map/all_to_all | solution.py:386
  43.9 3.2 %collective-permute-done.7 = bf16[8,24,1536]{2,1,0:T(8,128)(2,1)S(1)} collective-permute-done((bf16[8,24,1536]{2,1,0:T(8,128)(2,1)S(1)}, bf16[8,24,1536]{2,1,0:T(8,128)(2,1)S(1)}, u32[]{:S(2)}, u32[]{:S(2)}) %collective-permute-start.7) | collective-permute-done | bytes 589856 | tf_op jit(solution)/shard_map/ppermute | solution.py:304
  47.0 2.4 %collective-permute-done.8 = bf16[8,24,1536]{2,1,0:T(8,128)(2,1)} collective-permute-done((bf16[8,24,1536]{2,1,0:T(8,128)(2,1)S(1)}, bf16[8,24,1536]{2,1,0:T(8,128)(2,1)}, u32[]{:S(2)}, u32[]{:S(2)}) %collective-permute-start.8) | collective-permute-done | bytes 589856 | tf_op jit(solution)/shard_map/ppermute | solution.py:304
  49.6 8.3 %first.3 = (bf16[4,384,384]{2,1,0:T(8,128)(2,1)S(1)}, bf16[4,384,384]{2,1,0:T(8,128)(2,1)}, bf16[360,2880]{1,0:T(8,128)(2,1)S(1)}, bf16[360,2880]{1,0:T(8,128)(2,1)S(1)}, bf16[360,2880]{1,0:T(8,128)(2,1)S(1)}) custom-call(s32[4]{0:T(128)S(1)} %pad_add_fusion.4.own_ref, bf16[384,1536]{1,0:T(8,128)(2,1)S(1)} %bitcast.173, bf16[192,1536]{1,0:T(8,128)(2,1)S(1)} %bitcast.177, ...), custom_call_target="tpu_custom_call" | custom-call | tf_op jit(solution)/shard_map/first/pallas_call | solution.py:271
  57.9 1.0 copy-done.1
  59.0 1.3 copy-done.6
  60.3 1.4 copy-done.8
  61.7 1.3 copy-done.10
  64.1 3.6 %route.1 = (bf16[2,256,768]{2,1,0:T(8,128)(2,1)S(1)}, bf16[2,256,768]{2,1,0:T(8,128)(2,1)S(1)}, f32[8,256]{1,0:T(8,128)S(1)}) custom-call(s32[2]{0:T(128)S(1)} %pad_add_fusion.own_ref, s32[4,256]{1,0:T(4,128)S(1)} %bitcast.181, f32[4,256]{1,0:T(4,128)S(1)} %bitcast.182, bf16[2880,256]{1,0:T(8,128)(2,1)S(1)} %bitcast.172, ...), custom_call_target="tpu_custom_call" | custom-call | tf_op jit(solution)/shard_map/route/pallas_call | solution.py:389
  67.9 1.6 copy-done.9
  69.5 1.6 copy-done.11
  71.1 6.9 %second.3 = (bf16[4,384,384]{2,1,0:T(8,128)(2,1)S(1)}, bf16[4,384,384]{2,1,0:T(8,128)(2,1)}) custom-call(s32[4]{0:T(128)S(1)} %pad_add_fusion.4.own_ref, bf16[384,1536]{1,0:T(8,128)(2,1)} %bitcast.59.refs_0_, bf16[192,1536]{1,0:T(8,128)(2,1)} %bitcast.60.refs_1_, bf16[192,1536]{1,0:T(8,128)(2,1)} %bitcast.61.refs_2_, bf16[360,2880]{1,0:T(8,128)(2,1)S(1)} %copy-done.7, ...), custom_call_target="tpu_custom_call" | custom-call | tf_op jit(solution)/shard_map/second/pallas_call | solution.py:271
  78.0 1.1 copy-done.3
  79.5 1.2 slice_bitcast_fusion
  80.8 1.7 collective-permute-start.19
  82.5 8.2 %first.2 = (bf16[4,384,384]{2,1,0:T(8,128)(2,1)S(1)}, bf16[4,384,384]{2,1,0:T(8,128)(2,1)S(1)}, bf16[360,2880]{1,0:T(8,128)(2,1)S(1)}, bf16[360,2880]{1,0:T(8,128)(2,1)S(1)}, bf16[360,2880]{1,0:T(8,128)(2,1)S(1)}) custom-call(s32[4]{0:T(128)S(1)} %pad_add_fusion.1.own_ref, bf16[384,2880]{1,0:T(8,128)(2,1)} %bitcast.14.refs_0_, ...), custom_call_target="tpu_custom_call" | custom-call | tf_op jit(solution)/shard_map/first/pallas_call | solution.py:271
  91.5 1.3 add_convert_fusion
  92.8 1.0 convert_add_fusion.6
  93.9 1.2 add_convert_fusion.1
  95.2 1.0 convert_add_fusion.7
  96.5 2.0 %collective-permute-start.14 = (bf16[2,8,2,24,384]{4,3,2,1,0:T(8,128)(2,1)S(1)}, bf16[2,8,2,24,384]{4,3,2,1,0:T(8,128)(2,1)S(1)}, u32[]{:S(2)}, u32[]{:S(2)}) collective-permute-start(bf16[2,8,2,24,384]{4,3,2,1,0:T(8,128)(2,1)S(1)} %pad_maximum_fusion.10), channel_id=1, source_target_pairs={{0,96},{32,0},{64,32},{96,64},{1,97},{33,1},{65,33},{97,65},{2,98}... | collective-permute-start | bytes 1769480 | tf_op jit(solution)/shard_map/ppermute | solution.py:304
  98.6 1.3 convert_add_fusion.2
  99.9 1.3 convert_add_fusion.3
  101.3 5.0 %second.2 = (bf16[4,384,384]{2,1,0:T(8,128)(2,1)S(1)}, bf16[4,384,384]{2,1,0:T(8,128)(2,1)S(1)}) custom-call(s32[4]{0:T(128)S(1)} %pad_add_fusion.1.own_ref, bf16[384,2880]{1,0:T(8,128)(2,1)S(1)} %bitcast.176, bf16[360,2880]{1,0:T(8,128)(2,1)S(1)} %get-tuple-element.34.refs_1_, bf16[360,2880]{1,0:T(8,128)(2,1)S(1)} %get-tuple-element.35.refs_2_, ...), custom_call_target="tpu_custom_call" | custom-call | tf_op jit(solution)/shard_map/second/pallas_call | solution.py:271
  106.4 5.5 %collective-permute-done.14 = bf16[2,8,2,24,384]{4,3,2,1,0:T(8,128)(2,1)S(1)} collective-permute-done((bf16[2,8,2,24,384]{4,3,2,1,0:T(8,128)(2,1)S(1)}, bf16[2,8,2,24,384]{4,3,2,1,0:T(8,128)(2,1)S(1)}, u32[]{:S(2)}, u32[]{:S(2)}) %collective-permute-start.14) | collective-permute-done | bytes 589856 | tf_op jit(solution)/shard_map/ppermute | solution.py:304
  112.0 3.2 %collective-permute-start.17 = (bf16[8,2,24,384]{3,2,1,0:T(8,128)(2,1)S(1)}, bf16[8,2,24,384]{3,2,1,0:T(8,128)(2,1)S(1)}, u32[]{:S(2)}, u32[]{:S(2)}) collective-permute-start(bf16[8,2,24,384]{3,2,1,0:T(8,128)(2,1)S(1)} %fusion.9), channel_id=1, source_target_pairs={{0,96},{32,0},{64,32},{96,64},{1,97},{33,1},{65,33},{97,65},{2,98}... | collective-permute-start | bytes 884744 | tf_op jit(solution)/shard_map/ppermute | solution.py:304
  116.3 4.5 %collective-permute-done.17 = bf16[8,2,24,384]{3,2,1,0:T(8,128)(2,1)S(1)} collective-permute-done((bf16[8,2,24,384]{3,2,1,0:T(8,128)(2,1)S(1)}, bf16[8,2,24,384]{3,2,1,0:T(8,128)(2,1)S(1)}, u32[]{:S(2)}, u32[]{:S(2)}) %collective-permute-start.17) | collective-permute-done | bytes 294944 | tf_op jit(solution)/shard_map/ppermute | solution.py:304
  120.8 3.6 %collective-permute-done.16 = bf16[8,2,24,384]{3,2,1,0:T(8,128)(2,1)S(1)} collective-permute-done((bf16[8,2,24,384]{3,2,1,0:T(8,128)(2,1)S(1)}, bf16[8,2,24,384]{3,2,1,0:T(8,128)(2,1)S(1)}, u32[]{:S(2)}, u32[]{:S(2)}) %collective-permute-start.16) | collective-permute-done | bytes 294944 | tf_op jit(solution)/shard_map/ppermute | solution.py:304
  128.7 3.6 %all-to-all-start.3 = ((bf16[16,2,24,384]{3,2,1,0:T(8,128)(2,1)}), bf16[16,2,24,384]{3,2,1,0:T(8,128)(2,1)S(1)}, u32[]{:S(2)}, u32[]{:S(2)}) async-start(bf16[16,2,24,384]{3,2,1,0:T(8,128)(2,1)} %pad_maximum_fusion.11), calls=%async_computation.3 | async-start | bytes 1179648 | tf_op jit(solution)/shard_map/all_to_all | solution.py:418
  132.3 2.0 %collective-permute-start.4 = (bf16[2,8,2,24,384]{4,3,2,1,0:T(8,128)(2,1)}, bf16[2,8,2,24,384]{4,3,2,1,0:T(8,128)(2,1)S(1)}, u32[]{:S(2)}, u32[]{:S(2)}) collective-permute-start(bf16[2,8,2,24,384]{4,3,2,1,0:T(8,128)(2,1)} %pad_maximum_fusion.6), channel_id=1, source_target_pairs={{0,32},{32,64},{64,96},{96,0},{1,33},{33,65},{65,97},{97,1},{2,34}... | collective-permute-start | bytes 1769480 | tf_op jit(solution)/shard_map/ppermute | solution.py:304
  134.3 1.6 convert_add_fusion.10
  136.1 5.3 %collective-permute-done.3 = bf16[2,8,2,24,384]{4,3,2,1,0:T(8,128)(2,1)} collective-permute-done((bf16[2,8,2,24,384]{4,3,2,1,0:T(8,128)(2,1)}, bf16[2,8,2,24,384]{4,3,2,1,0:T(8,128)(2,1)}, u32[]{:S(2)}, u32[]{:S(2)}) %collective-permute-start.3) | collective-permute-done | bytes 589856 | tf_op jit(solution)/shard_map/ppermute | solution.py:304
  141.3 1.0 fusion.16
  142.4 1.7 collective-permute-start.6
  144.1 3.1 %collective-permute-done.4 = bf16[2,8,2,24,384]{4,3,2,1,0:T(8,128)(2,1)S(1)} collective-permute-done((bf16[2,8,2,24,384]{4,3,2,1,0:T(8,128)(2,1)}, bf16[2,8,2,24,384]{4,3,2,1,0:T(8,128)(2,1)S(1)}, u32[]{:S(2)}, u32[]{:S(2)}) %collective-permute-start.4) | collective-permute-done | bytes 589856 | tf_op jit(solution)/shard_map/ppermute | solution.py:304
  149.3 6.1 %collective-permute-done.5 = bf16[8,2,24,384]{3,2,1,0:T(8,128)(2,1)S(1)} collective-permute-done((bf16[8,2,24,384]{3,2,1,0:T(8,128)(2,1)S(1)}, bf16[8,2,24,384]{3,2,1,0:T(8,128)(2,1)S(1)}, u32[]{:S(2)}, u32[]{:S(2)}) %collective-permute-start.5) | collective-permute-done | bytes 294944 | tf_op jit(solution)/shard_map/ppermute | solution.py:304
  155.3 1.2 fusion.7
  156.5 0.9 pad_maximum_fusion.8
  157.4 6.9 %all-to-all-start.1 = ((bf16[16,2,24,384]{3,2,1,0:T(8,128)(2,1)}), bf16[16,2,24,384]{3,2,1,0:T(8,128)(2,1)S(1)}, u32[]{:S(2)}, u32[]{:S(2)}) async-start(bf16[16,2,24,384]{3,2,1,0:T(8,128)(2,1)} %pad_maximum_fusion.8), calls=%async_computation.1 | async-start | bytes 1179648 | tf_op jit(solution)/shard_map/all_to_all | solution.py:418
  165.0 1.0 copy-done.14
  166.0 1.0 copy-done.15
  167.7 7.1 %all-to-all-done.1 = bf16[16,2,24,384]{3,2,1,0:T(8,128)(2,1)S(1)} async-done(((bf16[16,2,24,384]{3,2,1,0:T(8,128)(2,1)}), bf16[16,2,24,384]{3,2,1,0:T(8,128)(2,1)S(1)}, u32[]{:S(2)}, u32[]{:S(2)}) %all-to-all-start.1) | async-done | bytes 589856 | tf_op jit(solution)/shard_map/all_to_all | solution.py:418
  174.8 1.3 combine.3
  (108 shorter events, 13.1 us)
Async XLA Ops:
  31.9 15.1 %collective-permute-start.7 = (bf16[8,24,1536]{2,1,0:T(8,128)(2,1)S(1)}, bf16[8,24,1536]{2,1,0:T(8,128)(2,1)S(1)}, u32[]{:S(2)}, u32[]{:S(2)}) collective-permute-start(bf16[8,24,1536]{2,1,0:T(8,128)(2,1)S(1)} %get-tuple-element.87), channel_id=1, source_target_pairs={{0,32},{32,64},{64,96},{96,0},{1,33},{33,65},{65,97},{97,1},{2,34}... | collective-permute-start | bytes 1769480 | tf_op jit(solution)/shard_map/ppermute | solution.py:304
  33.6 34.2 %collective-permute-start.9 = (bf16[16,24,1536]{2,1,0:T(8,128)(2,1)S(1)}, bf16[16,24,1536]{2,1,0:T(8,128)(2,1)}, u32[]{:S(2)}, u32[]{:S(2)}) collective-permute-start(bf16[16,24,1536]{2,1,0:T(8,128)(2,1)S(1)} %all_to_all.20), channel_id=1, source_target_pairs={{0,16},{16,0},{1,17},{17,1},{2,18},{18,2},{3,19},{19,3},{4,20},{20... | collective-permute-start | bytes 3538952 | tf_op jit(solution)/shard_map/ppermute | solution.py:299
  33.6 15.8 %collective-permute-start.8 = (bf16[8,24,1536]{2,1,0:T(8,128)(2,1)S(1)}, bf16[8,24,1536]{2,1,0:T(8,128)(2,1)}, u32[]{:S(2)}, u32[]{:S(2)}) collective-permute-start(bf16[8,24,1536]{2,1,0:T(8,128)(2,1)S(1)} %get-tuple-element.86), channel_id=1, source_target_pairs={{0,96},{32,0},{64,32},{96,64},{1,97},{33,1},{65,33},{97,65},{2,98}... | collective-permute-start | bytes 1769480 | tf_op jit(solution)/shard_map/ppermute | solution.py:304
  39.4 43.1 %all-to-all-start = ((bf16[16,24,2880]{2,1,0:T(8,128)(2,1)}), bf16[16,24,2880]{2,1,0:T(8,128)(2,1)}, u32[]{:S(2)}, u32[]{:S(2)}) async-start(bf16[16,24,2880]{2,1,0:T(8,128)(2,1)} %bitcast.188), calls=%async_computation | async-start | bytes 4521984 | tf_op jit(solution)/shard_map/all_to_all | solution.py:386
  47.0 20.8 %collective-permute-start.10 = (bf16[8,24,1536]{2,1,0:T(8,128)(2,1)S(1)}, bf16[8,24,1536]{2,1,0:T(8,128)(2,1)}, u32[]{:S(2)}, u32[]{:S(2)}) collective-permute-start(bf16[8,24,1536]{2,1,0:T(8,128)(2,1)S(1)} %collective-permute-done.7), channel_id=1, source_target_pairs={{0,16},{16,0},{1,17},{17,1},{2,18},{18,2},{3,19},{19,3},{4,20},{20... | collective-permute-start | bytes 1769480 | tf_op jit(solution)/shard_map/ppermute | solution.py:299
  49.4 18.4 %collective-permute-start.11 = (bf16[8,24,1536]{2,1,0:T(8,128)(2,1)}, bf16[8,24,1536]{2,1,0:T(8,128)(2,1)}, u32[]{:S(2)}, u32[]{:S(2)}) collective-permute-start(bf16[8,24,1536]{2,1,0:T(8,128)(2,1)} %collective-permute-done.8), channel_id=1, source_target_pairs={{0,16},{16,0},{1,17},{17,1},{2,18},{18,2},{3,19},{19,3},{4,20},{20... | collective-permute-start | bytes 1769480 | tf_op jit(solution)/shard_map/ppermute | solution.py:299
  49.5 14.0 %copy-start.23 = (bf16[2880]{0:T(1024)(128)(2,1)S(1)}, bf16[2880]{0:T(1024)(128)(2,1)}, u32[]{:S(2)}) copy-start(bf16[2880]{0:T(1024)(128)(2,1)} %param.17) | copy-start | bytes 17284
  49.5 14.5 %copy-start = (bf16[256,2880]{0,1:T(8,128)(2,1)S(1)}, bf16[256,2880]{0,1:T(8,128)(2,1)}, u32[]{:S(2)}) copy-start(bf16[256,2880]{0,1:T(8,128)(2,1)} %param.10) | copy-start | bytes 4423684
  49.5 14.5 %copy-start.16 = (bf16[2880,16]{0,1:T(8,128)(2,1)S(1)}, bf16[2880,16]{0,1:T(8,128)(2,1)}, u32[]{:S(2)}) copy-start(bf16[2880,16]{0,1:T(8,128)(2,1)} %param.18) | copy-start | bytes 276484
  49.5 14.5 %copy-start.17 = (s32[256,4]{0,1:T(4,128)S(1)}, s32[256,4]{0,1:T(4,128)}, u32[]{:S(2)}) copy-start(s32[256,4]{0,1:T(4,128)} %param.12) | copy-start | bytes 12292
  49.5 14.5 %copy-start.18 = (f32[256,4]{0,1:T(4,128)S(1)}, f32[256,4]{0,1:T(4,128)}, u32[]{:S(2)}) copy-start(f32[256,4]{0,1:T(4,128)} %param.13) | copy-start | bytes 12292
  49.5 14.5 %copy-start.19 = (s32[256,4]{0,1:T(4,128)S(1)}, s32[256,4]{0,1:T(4,128)}, u32[]{:S(2)}) copy-start(s32[256,4]{0,1:T(4,128)} %param.19) | copy-start | bytes 12292
  57.9 1.1 copy-start.1
  59.0 1.3 copy-start.6
  60.3 1.4 copy-start.8
  61.7 1.3 copy-start.10
  63.0 28.5 %collective-permute-start.12 = (bf16[4,384,384]{2,1,0:T(8,128)(2,1)}, bf16[4,384,384]{2,1,0:T(8,128)(2,1)}, u32[]{:S(2)}, u32[]{:S(2)}) collective-permute-start(bf16[4,384,384]{2,1,0:T(8,128)(2,1)} %get-tuple-element.51), channel_id=1, source_target_pairs={{0,16},{16,0},{1,17},{17,1},{2,18},{18,2},{3,19},{19,3},{4,20},{20... | collective-permute-start | bytes 3538952 | tf_op jit(solution)/shard_map/ppermute | solution.py:299
  63.9 3.9 %copy-start.7 = (bf16[360,2880]{1,0:T(8,128)(2,1)S(1)}, bf16[360,2880]{1,0:T(8,128)(2,1)}, u32[]{:S(2)}) copy-start(bf16[360,2880]{1,0:T(8,128)(2,1)} %copy-done.6) | copy-start | bytes 6220804
  67.7 13.1 %collective-permute-start.18 = (f32[8,256]{1,0:T(8,128)S(1)}, f32[8,256]{1,0:T(8,128)S(1)}, u32[]{:S(2)}, u32[]{:S(2)}) collective-permute-start(f32[8,256]{1,0:T(8,128)S(1)} %get-tuple-element.59), channel_id=1, source_target_pairs={{0,16},{16,0},{1,17},{17,1},{2,18},{18,2},{3,19},{19,3},{4,20},{20... | collective-permute-start | bytes 24584 | tf_op jit(solution)/shard_map/ppermute | solution.py:299
  67.9 1.6 copy-start.9
  69.5 1.6 copy-start.11
  78.0 1.1 copy-start.3
  79.1 14.8 %collective-permute-start.13 = (bf16[4,384,384]{2,1,0:T(8,128)(2,1)}, bf16[4,384,384]{2,1,0:T(8,128)(2,1)}, u32[]{:S(2)}, u32[]{:S(2)}) collective-permute-start(bf16[4,384,384]{2,1,0:T(8,128)(2,1)} %get-tuple-element.52), channel_id=1, source_target_pairs={{0,16},{16,0},{1,17},{17,1},{2,18},{18,2},{3,19},{19,3},{4,20},{20... | collective-permute-start | bytes 3538952 | tf_op jit(solution)/shard_map/ppermute | solution.py:299
  80.8 17.7 %collective-permute-start.19 = (f32[8,256]{1,0:T(8,128)S(1)}, f32[8,256]{1,0:T(8,128)S(1)}, u32[]{:S(2)}, u32[]{:S(2)}) collective-permute-start(f32[8,256]{1,0:T(8,128)S(1)} %pad_maximum_fusion.16), channel_id=1, source_target_pairs={{0,32},{32,0},{64,96},{96,64},{1,33},{33,1},{65,97},{97,65},{2,34}... | collective-permute-start | bytes 24584 | tf_op jit(solution)/shard_map/ppermute | solution.py:424
  82.5 9.0 %copy-start.4 = (bf16[4,384,384]{2,1,0:T(8,128)(2,1)S(1)}, bf16[4,384,384]{2,1,0:T(8,128)(2,1)}, u32[]{:S(2)}) copy-start(bf16[4,384,384]{2,1,0:T(8,128)(2,1)} %copy-done.3) | copy-start | bytes 3538948
  90.7 24.6 %collective-permute-start.1 = (bf16[4,384,384]{2,1,0:T(8,128)(2,1)S(1)}, bf16[4,384,384]{2,1,0:T(8,128)(2,1)S(1)}, u32[]{:S(2)}, u32[]{:S(2)}) collective-permute-start(bf16[4,384,384]{2,1,0:T(8,128)(2,1)S(1)} %get-tuple-element.38), channel_id=1, source_target_pairs={{0,16},{16,0},{1,17},{17,1},{2,18},{18,2},{3,19},{19,3},{4,20},{20... | collective-permute-start | bytes 3538952 | tf_op jit(solution)/shard_map/ppermute | solution.py:299
  91.0 10.3 %collective-permute-start = (bf16[16,24,2880]{2,1,0:T(8,128)(2,1)}, bf16[16,24,2880]{2,1,0:T(8,128)(2,1)S(1)}, u32[]{:S(2)}, u32[]{:S(2)}) collective-permute-start(bf16[16,24,2880]{2,1,0:T(8,128)(2,1)} %all-to-all-done), channel_id=1, source_target_pairs={{0,16},{16,0},{1,17},{17,1},{2,18},{18,2},{3,19},{19,3},{4,20},{20... | collective-permute-start | bytes 6635528 | tf_op jit(solution)/shard_map/ppermute | solution.py:299
  91.5 2.4 %copy-start.2 = (bf16[4,384,384]{2,1,0:T(8,128)(2,1)S(1)}, bf16[4,384,384]{2,1,0:T(8,128)(2,1)}, u32[]{:S(2)}) copy-start(bf16[4,384,384]{2,1,0:T(8,128)(2,1)} %copy-done.1) | copy-start | bytes 3538948
  96.5 15.4 %collective-permute-start.14 = (bf16[2,8,2,24,384]{4,3,2,1,0:T(8,128)(2,1)S(1)}, bf16[2,8,2,24,384]{4,3,2,1,0:T(8,128)(2,1)S(1)}, u32[]{:S(2)}, u32[]{:S(2)}) collective-permute-start(bf16[2,8,2,24,384]{4,3,2,1,0:T(8,128)(2,1)S(1)} %pad_maximum_fusion.10), channel_id=1, source_target_pairs={{0,96},{32,0},{64,32},{96,64},{1,97},{33,1},{65,33},{97,65},{2,98}... | collective-permute-start | bytes 1769480 | tf_op jit(solution)/shard_map/ppermute | solution.py:304
  98.5 16.7 %collective-permute-start.15 = (bf16[2,8,2,24,384]{4,3,2,1,0:T(8,128)(2,1)S(1)}, bf16[2,8,2,24,384]{4,3,2,1,0:T(8,128)(2,1)S(1)}, u32[]{:S(2)}, u32[]{:S(2)}) collective-permute-start(bf16[2,8,2,24,384]{4,3,2,1,0:T(8,128)(2,1)S(1)} %pad_maximum_fusion.9), channel_id=1, source_target_pairs={{0,32},{32,64},{64,96},{96,0},{1,33},{33,65},{65,97},{97,1},{2,34}... | collective-permute-start | bytes 1769480 | tf_op jit(solution)/shard_map/ppermute | solution.py:304
  106.3 9.1 %copy-start.5 = (bf16[4,384,384]{2,1,0:T(8,128)(2,1)}, bf16[4,384,384]{2,1,0:T(8,128)(2,1)S(1)}, u32[]{:S(2)}) copy-start(bf16[4,384,384]{2,1,0:T(8,128)(2,1)S(1)} %get-tuple-element.42) | copy-start | bytes 3538948
  106.3 18.3 %collective-permute-start.2 = (bf16[4,384,384]{2,1,0:T(8,128)(2,1)S(1)}, bf16[4,384,384]{2,1,0:T(8,128)(2,1)S(1)}, u32[]{:S(2)}, u32[]{:S(2)}) collective-permute-start(bf16[4,384,384]{2,1,0:T(8,128)(2,1)S(1)} %get-tuple-element.39), channel_id=1, source_target_pairs={{0,16},{16,0},{1,17},{17,1},{2,18},{18,2},{3,19},{19,3},{4,20},{20... | collective-permute-start | bytes 3538952 | tf_op jit(solution)/shard_map/ppermute | solution.py:299
  112.0 8.8 %collective-permute-start.17 = (bf16[8,2,24,384]{3,2,1,0:T(8,128)(2,1)S(1)}, bf16[8,2,24,384]{3,2,1,0:T(8,128)(2,1)S(1)}, u32[]{:S(2)}, u32[]{:S(2)}) collective-permute-start(bf16[8,2,24,384]{3,2,1,0:T(8,128)(2,1)S(1)} %fusion.9), channel_id=1, source_target_pairs={{0,96},{32,0},{64,32},{96,64},{1,97},{33,1},{65,33},{97,65},{2,98}... | collective-permute-start | bytes 884744 | tf_op jit(solution)/shard_map/ppermute | solution.py:304
  115.2 9.2 %collective-permute-start.16 = (bf16[8,2,24,384]{3,2,1,0:T(8,128)(2,1)S(1)}, bf16[8,2,24,384]{3,2,1,0:T(8,128)(2,1)S(1)}, u32[]{:S(2)}, u32[]{:S(2)}) collective-permute-start(bf16[8,2,24,384]{3,2,1,0:T(8,128)(2,1)S(1)} %fusion.14), channel_id=1, source_target_pairs={{0,32},{32,64},{64,96},{96,0},{1,33},{33,65},{65,97},{97,1},{2,34}... | collective-permute-start | bytes 884744 | tf_op jit(solution)/shard_map/ppermute | solution.py:304
  115.3 1.0 copy-start.20
  124.6 1.1 copy-start.21
  127.7 13.7 %collective-permute-start.3 = (bf16[2,8,2,24,384]{4,3,2,1,0:T(8,128)(2,1)}, bf16[2,8,2,24,384]{4,3,2,1,0:T(8,128)(2,1)}, u32[]{:S(2)}, u32[]{:S(2)}) collective-permute-start(bf16[2,8,2,24,384]{4,3,2,1,0:T(8,128)(2,1)} %pad_maximum_fusion.7), channel_id=1, source_target_pairs={{0,96},{32,0},{64,32},{96,64},{1,97},{33,1},{65,33},{97,65},{2,98}... | collective-permute-start | bytes 1769480 | tf_op jit(solution)/shard_map/ppermute | solution.py:304
  128.7 28.7 %all-to-all-start.3 = ((bf16[16,2,24,384]{3,2,1,0:T(8,128)(2,1)}), bf16[16,2,24,384]{3,2,1,0:T(8,128)(2,1)S(1)}, u32[]{:S(2)}, u32[]{:S(2)}) async-start(bf16[16,2,24,384]{3,2,1,0:T(8,128)(2,1)} %pad_maximum_fusion.11), calls=%async_computation.3 | async-start | bytes 1179648 | tf_op jit(solution)/shard_map/all_to_all | solution.py:418
  132.3 3.5 %copy-start.22 = (bf16[4,384,384]{2,1,0:T(8,128)(2,1)S(1)}, bf16[4,384,384]{2,1,0:T(8,128)(2,1)}, u32[]{:S(2)}) copy-start(bf16[4,384,384]{2,1,0:T(8,128)(2,1)} %copy-done.21) | copy-start | bytes 3538948
  132.3 14.8 %collective-permute-start.4 = (bf16[2,8,2,24,384]{4,3,2,1,0:T(8,128)(2,1)}, bf16[2,8,2,24,384]{4,3,2,1,0:T(8,128)(2,1)S(1)}, u32[]{:S(2)}, u32[]{:S(2)}) collective-permute-start(bf16[2,8,2,24,384]{4,3,2,1,0:T(8,128)(2,1)} %pad_maximum_fusion.6), channel_id=1, source_target_pairs={{0,32},{32,64},{64,96},{96,0},{1,33},{33,65},{65,97},{97,1},{2,34}... | collective-permute-start | bytes 1769480 | tf_op jit(solution)/shard_map/ppermute | solution.py:304
  142.4 6.9 %collective-permute-start.6 = (bf16[8,2,24,384]{3,2,1,0:T(8,128)(2,1)S(1)}, bf16[8,2,24,384]{3,2,1,0:T(8,128)(2,1)S(1)}, u32[]{:S(2)}, u32[]{:S(2)}) collective-permute-start(bf16[8,2,24,384]{3,2,1,0:T(8,128)(2,1)S(1)} %fusion.16), channel_id=1, source_target_pairs={{0,96},{32,0},{64,32},{96,64},{1,97},{33,1},{65,33},{97,65},{2,98}... | collective-permute-start | bytes 884744 | tf_op jit(solution)/shard_map/ppermute | solution.py:304
  147.2 8.1 %collective-permute-start.5 = (bf16[8,2,24,384]{3,2,1,0:T(8,128)(2,1)S(1)}, bf16[8,2,24,384]{3,2,1,0:T(8,128)(2,1)S(1)}, u32[]{:S(2)}, u32[]{:S(2)}) collective-permute-start(bf16[8,2,24,384]{3,2,1,0:T(8,128)(2,1)S(1)} %fusion.21), channel_id=1, source_target_pairs={{0,32},{32,64},{64,96},{96,0},{1,33},{33,65},{65,97},{97,1},{2,34}... | collective-permute-start | bytes 884744 | tf_op jit(solution)/shard_map/ppermute | solution.py:304
  147.8 16.5 %collective-permute-start.20 = (f32[8,256]{1,0:T(8,128)S(1)}, f32[8,256]{1,0:T(8,128)S(1)}, u32[]{:S(2)}, u32[]{:S(2)}) collective-permute-start(f32[8,256]{1,0:T(8,128)S(1)} %pad_maximum_fusion.17), channel_id=1, source_target_pairs={{0,64},{32,96},{64,0},{96,32},{1,65},{33,97},{65,1},{97,33},{2,66}... | collective-permute-start | bytes 24584 | tf_op jit(solution)/shard_map/ppermute | solution.py:424
  157.4 17.4 %all-to-all-start.1 = ((bf16[16,2,24,384]{3,2,1,0:T(8,128)(2,1)}), bf16[16,2,24,384]{3,2,1,0:T(8,128)(2,1)S(1)}, u32[]{:S(2)}, u32[]{:S(2)}) async-start(bf16[16,2,24,384]{3,2,1,0:T(8,128)(2,1)} %pad_maximum_fusion.8), calls=%async_computation.1 | async-start | bytes 1179648 | tf_op jit(solution)/shard_map/all_to_all | solution.py:418
  164.3 10.5 %copy-start.12 = (bf16[256,768]{1,0:T(8,128)(2,1)S(1)}, bf16[256,768]{1,0:T(8,128)(2,1)}, u32[]{:S(2)}) copy-start(bf16[256,768]{1,0:T(8,128)(2,1)} %get-tuple-element.91.low_ref) | copy-start | bytes 1179652
  164.4 10.5 %copy-start.13 = (bf16[256,768]{1,0:T(8,128)(2,1)S(1)}, bf16[256,768]{1,0:T(8,128)(2,1)}, u32[]{:S(2)}) copy-start(bf16[256,768]{1,0:T(8,128)(2,1)} %get-tuple-element.100.high_ref) | copy-start | bytes 1179652
  165.0 1.0 copy-start.14
  166.0 1.0 copy-start.15
